TPU v7x, 512 devices: a 4x2x32 block of a 4x8x32 slice. The times are simulated.
512 devices in a mesh: groups: 2 (over y), inner: 32 (over z), outer: 4 (over x), head: 2 (over core).
Axes of the slice: x: 4, y: 2, z: 32, core: 2. Of those that a mesh axis runs over, the one named last changes fastest.
The devices are a block of a 4x8x32 slice.
Arguments:
- queries: bfloat16 [8, 4096, 8, 128], P(('groups', 'outer'), 'inner', 'head'), parts along dimension 0, may hold values from -112 to 112
- keys: bfloat16 [8, 4096, 128], P(('groups', 'outer'), 'inner'), parts along dimension 0, may hold values from -4 to 4
- values: bfloat16 [8, 4096, 128], P(('groups', 'outer'), 'inner'), parts along dimension 0, may hold values from -6 to 6
- out: bfloat16 [8, 4096, 8, 128], P(('groups', 'outer'), 'inner', 'head'), parts along dimension 0, may hold values from -6 to 6, as said below
- log_total: float32 [8, 8, 4096], P(('groups', 'outer'), 'head', 'inner'), parts along dimension 0, as said below
- d_out: bfloat16 [8, 4096, 8, 128], P(('groups', 'outer'), 'inner', 'head'), parts along dimension 0, may hold values from -6 to 6
- span_order: int32 [8, 64], P(('groups', 'outer')), parts along dimension 0, may hold values from 0 to 63, as said below
Outputs:
- grad_queries: bfloat16 [8, 4096, 8, 128], P(('groups', 'outer'), 'inner', 'head'), parts along dimension 0
- grad_keys: bfloat16 [8, 4096, 128], P(('groups', 'outer'), 'inner'), parts along dimension 0
- grad_values: bfloat16 [8, 4096, 128], P(('groups', 'outer'), 'inner'), parts along dimension 0
There are 2 independent parts, one for each index of `groups`. A program takes and returns all parts, laid end to end along the dimension named above; each array names one. Nothing has to cross between parts.
Inputs may be any that keep to these rules, and one draw needn't show every extreme that they name: `span_order`: each row is a permutation of 0 to 63. `out`: the causal softmax attention output of queries, keys and values in the order given by span_order, rounded to bfloat16. `log_total`: the log of the causal softmax total of each query row and head for the same inputs.
All inputs are finite; a program needn't handle non-finite values.
Results may differ from a plain program's by a relative error of at most 0.0054.
Values may be sent and summed in bfloat16 or wider, within the bound.
No kernel may reach another device: no remote copies, remote signals or barrier semaphores. Data moves between devices by JAX's collectives and lax.ppermute only.
A program may use at most 64 MiB of HBM per device.

v0:
```python
import math

import jax
import jax.numpy as jnp
from jax import lax
from jax.sharding import PartitionSpec as P


def shifted(block, axis, distance):
    devices = range(lax.axis_size(axis))
    route = [((i - distance) % len(devices), i) for i in devices]
    return lax.ppermute(block, axis, route)


def sent_to_all(shard, axis):
    size = lax.axis_size(axis)
    return lax.all_to_all(
        jnp.broadcast_to(shard[None], (size, *shard.shape)), axis, 0, 0, tiled=True
    )


def over_copies(shard, axis):
    everything = sent_to_all(shard, axis)
    return jnp.sum(everything, axis=0)


def packed_total(arrays, axis):
    ends = [0]
    for a in arrays:
        ends.append(ends[-1] + a.size)
    subtotal = over_copies(jnp.concatenate([a.ravel() for a in arrays]), axis)
    return tuple((subtotal[b:e].reshape(a.shape) for a, b, e in zip(arrays, ends, ends[1:])))


def row_positions(block_order, start, count, tok_rows):
    rows = start + jnp.arange(count, dtype=jnp.int32)
    owner = rows // tok_rows
    offset = rows % tok_rows
    half_rows = tok_rows // 2
    slot_index = 2 * owner + offset // half_rows
    table = jnp.arange(block_order.shape[0], dtype=jnp.int32)
    span = jnp.sum(
        jnp.where(slot_index[:, None] == table[None, :], block_order[None, :], 0), axis=1
    )
    return span * half_rows + offset % half_rows


def block_grads(operands):
    query_rows, grad_rows, total_rows, delta_rows, query_pos, key_rows, value_rows, key_pos = (
        operands
    )
    softmax_scale = 1.0 / math.sqrt(key_rows.shape[1])
    visible = key_pos[None, :] <= query_pos[:, None]
    scores = (
        jnp.einsum("thd,ud->htu", query_rows, key_rows, preferred_element_type=jnp.float32)
        * softmax_scale
    )
    probs = jnp.exp(jnp.where(visible[None], scores - total_rows[:, :, None], -jnp.inf))
    grad_probs = jnp.einsum(
        "thd,ud->htu", grad_rows, value_rows, preferred_element_type=jnp.float32
    )
    grad_scores = (probs * (grad_probs - delta_rows[:, :, None]) * softmax_scale).astype(
        jnp.bfloat16
    )
    probs_half = probs.astype(jnp.bfloat16)
    query_grad = jnp.einsum(
        "htu,ud->thd", grad_scores, key_rows, preferred_element_type=jnp.float32
    )
    key_grad = jnp.einsum(
        "htu,thd->ud", grad_scores, query_rows, preferred_element_type=jnp.float32
    )
    value_grad = jnp.einsum(
        "htu,thd->ud", probs_half, grad_rows, preferred_element_type=jnp.float32
    )
    return (query_grad, key_grad, value_grad)


def guarded_grads(operands):
    return block_grads(operands)


def send_key_grads(key_acc, value_acc):
    return shifted((key_acc, value_acc), "inner", 1)


def body(queries, keys, values, out, log_total, d_out, span_order):
    query_rows = queries[0]
    grad_rows = d_out[0]
    key_rows = keys[0]
    value_rows = values[0]
    block_order = span_order[0]
    total_rows = log_total[0]
    tok_rows = key_rows.shape[0]
    cycle_size = lax.axis_size("inner")
    cycle_index = lax.axis_index("inner")
    own_pos = row_positions(block_order, cycle_index * tok_rows, tok_rows, tok_rows)
    delta_rows = jnp.transpose(
        jnp.sum(out[0].astype(jnp.float32) * grad_rows.astype(jnp.float32), axis=-1)
    )
    zero_rows = jnp.zeros(key_rows.shape, jnp.float32)
    zero_queries = jnp.zeros(query_rows.shape, jnp.float32)

    def key_turn(turn_index, state):
        key_block, value_block, query_acc, key_acc, value_acc = state
        owner = (cycle_index - turn_index) % cycle_size
        key_pos = row_positions(block_order, owner * tok_rows, tok_rows, tok_rows)
        query_grad, key_grad, value_grad = guarded_grads(
            (
                query_rows,
                grad_rows,
                total_rows,
                delta_rows,
                own_pos,
                key_block,
                value_block,
                key_pos,
            )
        )
        key_block, value_block = shifted((key_block, value_block), "inner", 1)
        key_acc, value_acc = send_key_grads(key_acc + key_grad, value_acc + value_grad)
        return (key_block, value_block, query_acc + query_grad, key_acc, value_acc)

    state = lax.fori_loop(
        0, cycle_size - 1, key_turn, (key_rows, value_rows, zero_queries, zero_rows, zero_rows)
    )
    key_block, value_block, query_acc, key_acc, value_acc = state
    owner = (cycle_index - (cycle_size - 1)) % cycle_size
    key_pos = row_positions(block_order, owner * tok_rows, tok_rows, tok_rows)
    query_grad, key_grad, value_grad = guarded_grads(
        (query_rows, grad_rows, total_rows, delta_rows, own_pos, key_block, value_block, key_pos)
    )
    query_acc = query_acc + query_grad
    key_acc, value_acc = send_key_grads(key_acc + key_grad, value_acc + value_grad)
    key_total, value_total = packed_total((key_acc, value_acc), "head")
    grad_queries = query_acc.astype(jnp.bfloat16)[None]
    return (
        grad_queries,
        key_total.astype(jnp.bfloat16)[None],
        value_total.astype(jnp.bfloat16)[None],
    )


def solution(mesh):
    in_specs = (
        P(("groups", "outer"), "inner", "head", None),
        P(("groups", "outer"), "inner", None),
        P(("groups", "outer"), "inner", None),
        P(("groups", "outer"), "inner", "head", None),
        P(("groups", "outer"), "head", "inner"),
        P(("groups", "outer"), "inner", "head", None),
        P(("groups", "outer"), None),
    )
    out_specs = (
        P(("groups", "outer"), "inner", "head", None),
        P(("groups", "outer"), "inner", None),
        P(("groups", "outer"), "inner", None),
    )
    return jax.shard_map(body, mesh=mesh, in_specs=in_specs, out_specs=out_specs, check_vma=False)
```

profile of v0, /device:TPU:33, one launch (start us, length us, event | category | flops | bytes accessed | tf_op | source)
XLA Modules:
  0.0 588.6 jit_solution(11550708041333898785)
XLA Ops:
  4.3 508.1 %while.25 = (s32[]{:T(128)}, bf16[128,128]{1,0:T(8,128)(2,1)S(1)}, bf16[128,128]{1,0:T(8,128)(2,1)S(1)}, f32[128,4,128]{2,0,1:T(8,128)S(1)}, f32[128,128]{1,0:T(...) while((s32[]{:T(128)}, bf16[128,128]{1,0:T(8,128)(2,1)S(1)}, ...), condition=%wide.region_4.5_spmd.clone, body=%wide.region_2.4_spmd.clone.sunk | while | flops 84622992 | bytes 3547356 | solution.py:123
  4.4 5.2 collective-permute-start.1
  9.6 4.4 collective-permute-start
  14.9 4.4 collective-permute-start.2
  19.5 5.6 collective-permute-start.3
  25.4 26.1 %collective-permute-done.1 = bf16[128,128]{1,0:T(8,128)(2,1)S(1)} collective-permute-done((bf16[128,128]{1,0:T(8,128)(2,1)S(1)}, bf16[128,128]{1,0:T(8,128)(2,1)S(1)}, u32[]{:S(2)}, u32[]{:S(2)}) %collective-permute-start.1) | collective-permute-done | bytes 32800 | tf_op jit(solution)/shard_map/while/body/eval_jaxpr/ppermute | solution.py:12
  118.5 3.8 collective-permute-start.2
  130.7 3.7 collective-permute-start
  135.3 3.6 collective-permute-start.2
  139.1 4.8 collective-permute-start.3
  145.5 3.8 collective-permute-start.1
  152.3 3.7 collective-permute-start.2
  156.2 4.4 collective-permute-start.3
  162.5 3.3 collective-permute-start.1
  165.8 3.7 collective-permute-start
  172.8 4.9 collective-permute-start.3
  179.0 3.7 collective-permute-start.1
  182.7 3.4 collective-permute-start
  186.9 3.7 collective-permute-start.2
  190.9 3.3 collective-permute-start.3
  205.8 3.2 collective-permute-start.3
  273.6 3.2 collective-permute-start.3
  285.4 3.2 collective-permute-start.2
  288.7 5.1 collective-permute-start.3
  295.1 3.7 collective-permute-start.1
  305.6 4.4 collective-permute-start.3
  311.9 3.2 collective-permute-start.1
  315.1 3.4 collective-permute-start
  322.1 4.9 collective-permute-start.3
  328.4 3.7 collective-permute-start.1
  332.1 3.3 collective-permute-start
  336.3 3.4 collective-permute-start.2
  339.8 3.8 collective-permute-start.3
  349.1 3.6 collective-permute-start
  355.7 4.4 collective-permute-start.3
  365.1 4.0 collective-permute-start
  400.9 3.2 collective-permute-start.3
  455.2 3.5 collective-permute-start.3
  467.1 3.4 collective-permute-start.2
  470.7 4.8 collective-permute-start.3
  477.0 3.8 collective-permute-start.1
  480.8 4.1 collective-permute-start
  485.8 3.7 collective-permute-start.2
  498.7 3.3 collective-permute-start
  502.8 3.2 collective-permute-start.2
  506.2 4.9 collective-permute-start.3
  513.0 4.2 collective-permute-start.4
  523.8 63.8 %all_to_all.6 = f32[2,1,32768]{2,1,0:T(1,128)S(1)} all-to-all(f32[2,1,32768]{2,1,0:T(1,128)S(1)} %broadcast_in_dim.152), channel_id=1, replica_groups=mesh['groups'=2,'inner'=32,'outer'=4,'head'=2] {'head'}, dimensions={0} | all-to-all | bytes 524288 | tf_op jit(solution)/shard_map/all_to_all | solution.py:17
  (580 shorter events, 317.6 us)
Async XLA Ops:
  4.4 47.2 %collective-permute-start.1 = (bf16[128,128]{1,0:T(8,128)(2,1)S(1)}, bf16[128,128]{1,0:T(8,128)(2,1)S(1)}, u32[]{:S(2)}, u32[]{:S(2)}) collective-permute-start(bf16[128,128]{1,0:T(8,128)(2,1)S(1)} %copy.57), channel_id=1, source_target_pairs={{248,0},{0,8},{8,16},{16,24},{24,32},{32,40},{40,48},{48,56},{56,6... | collective-permute-start | bytes 98312 | tf_op jit(solution)/shard_map/while/body/eval_jaxpr/ppermute | solution.py:12
  9.6 43.9 %collective-permute-start = (bf16[128,128]{1,0:T(8,128)(2,1)S(1)}, bf16[128,128]{1,0:T(8,128)(2,1)S(1)}, u32[]{:S(2)}, u32[]{:S(2)}) collective-permute-start(bf16[128,128]{1,0:T(8,128)(2,1)S(1)} %copy.56), channel_id=1, source_target_pairs={{248,0},{0,8},{8,16},{16,24},{24,32},{32,40},{40,48},{48,56},{56,6... | collective-permute-start | bytes 98312 | tf_op jit(solution)/shard_map/while/body/eval_jaxpr/ppermute | solution.py:12
  14.9 41.7 %collective-permute-start.2 = (f32[128,128]{1,0:T(8,128)S(1)}, f32[128,128]{1,0:T(8,128)S(1)}, u32[]{:S(2)}, u32[]{:S(2)}) collective-permute-start(f32[128,128]{1,0:T(8,128)S(1)} %fusion.74), channel_id=1, source_target_pairs={{248,0},{0,8},{8,16},{16,24},{24,32},{32,40},{40,48},{48,56},{56,6... | collective-permute-start | bytes 196616 | tf_op jit(solution)/shard_map/while/body/eval_jaxpr/ppermute | solution.py:12
  19.5 39.3 %collective-permute-start.3 = (f32[128,128]{1,0:T(8,128)S(1)}, f32[128,128]{1,0:T(8,128)S(1)}, u32[]{:S(2)}, u32[]{:S(2)}) collective-permute-start(f32[128,128]{1,0:T(8,128)S(1)} %fusion.75), channel_id=1, source_target_pairs={{248,0},{0,8},{8,16},{16,24},{24,32},{32,40},{40,48},{48,56},{56,6... | collective-permute-start | bytes 196616 | tf_op jit(solution)/shard_map/while/body/eval_jaxpr/ppermute | solution.py:12
  99.5 9.4 %collective-permute-start.1 = (bf16[128,128]{1,0:T(8,128)(2,1)S(1)}, bf16[128,128]{1,0:T(8,128)(2,1)S(1)}, u32[]{:S(2)}, u32[]{:S(2)}) collective-permute-start(bf16[128,128]{1,0:T(8,128)(2,1)S(1)} %copy.57), channel_id=1, source_target_pairs={{248,0},{0,8},{8,16},{16,24},{24,32},{32,40},{40,48},{48,56},{56,6... | collective-permute-start | bytes 98312 | tf_op jit(solution)/shard_map/while/body/eval_jaxpr/ppermute | solution.py:12
  112.7 13.2 %collective-permute-start.1 = (bf16[128,128]{1,0:T(8,128)(2,1)S(1)}, bf16[128,128]{1,0:T(8,128)(2,1)S(1)}, u32[]{:S(2)}, u32[]{:S(2)}) collective-permute-start(bf16[128,128]{1,0:T(8,128)(2,1)S(1)} %copy.57), channel_id=1, source_target_pairs={{248,0},{0,8},{8,16},{16,24},{24,32},{32,40},{40,48},{48,56},{56,6... | collective-permute-start | bytes 98312 | tf_op jit(solution)/shard_map/while/body/eval_jaxpr/ppermute | solution.py:12
  114.6 11.2 %collective-permute-start = (bf16[128,128]{1,0:T(8,128)(2,1)S(1)}, bf16[128,128]{1,0:T(8,128)(2,1)S(1)}, u32[]{:S(2)}, u32[]{:S(2)}) collective-permute-start(bf16[128,128]{1,0:T(8,128)(2,1)S(1)} %copy.56), channel_id=1, source_target_pairs={{248,0},{0,8},{8,16},{16,24},{24,32},{32,40},{40,48},{48,56},{56,6... | collective-permute-start | bytes 98312 | tf_op jit(solution)/shard_map/while/body/eval_jaxpr/ppermute | solution.py:12
  128.7 15.4 %collective-permute-start.1 = (bf16[128,128]{1,0:T(8,128)(2,1)S(1)}, bf16[128,128]{1,0:T(8,128)(2,1)S(1)}, u32[]{:S(2)}, u32[]{:S(2)}) collective-permute-start(bf16[128,128]{1,0:T(8,128)(2,1)S(1)} %copy.57), channel_id=1, source_target_pairs={{248,0},{0,8},{8,16},{16,24},{24,32},{32,40},{40,48},{48,56},{56,6... | collective-permute-start | bytes 98312 | tf_op jit(solution)/shard_map/while/body/eval_jaxpr/ppermute | solution.py:12
  130.7 13.5 %collective-permute-start = (bf16[128,128]{1,0:T(8,128)(2,1)S(1)}, bf16[128,128]{1,0:T(8,128)(2,1)S(1)}, u32[]{:S(2)}, u32[]{:S(2)}) collective-permute-start(bf16[128,128]{1,0:T(8,128)(2,1)S(1)} %copy.56), channel_id=1, source_target_pairs={{248,0},{0,8},{8,16},{16,24},{24,32},{32,40},{40,48},{48,56},{56,6... | collective-permute-start | bytes 98312 | tf_op jit(solution)/shard_map/while/body/eval_jaxpr/ppermute | solution.py:12
  145.5 15.5 %collective-permute-start.1 = (bf16[128,128]{1,0:T(8,128)(2,1)S(1)}, bf16[128,128]{1,0:T(8,128)(2,1)S(1)}, u32[]{:S(2)}, u32[]{:S(2)}) collective-permute-start(bf16[128,128]{1,0:T(8,128)(2,1)S(1)} %copy.57), channel_id=1, source_target_pairs={{248,0},{0,8},{8,16},{16,24},{24,32},{32,40},{40,48},{48,56},{56,6... | collective-permute-start | bytes 98312 | tf_op jit(solution)/shard_map/while/body/eval_jaxpr/ppermute | solution.py:12
  149.3 11.6 %collective-permute-start = (bf16[128,128]{1,0:T(8,128)(2,1)S(1)}, bf16[128,128]{1,0:T(8,128)(2,1)S(1)}, u32[]{:S(2)}, u32[]{:S(2)}) collective-permute-start(bf16[128,128]{1,0:T(8,128)(2,1)S(1)} %copy.56), channel_id=1, source_target_pairs={{248,0},{0,8},{8,16},{16,24},{24,32},{32,40},{40,48},{48,56},{56,6... | collective-permute-start | bytes 98312 | tf_op jit(solution)/shard_map/while/body/eval_jaxpr/ppermute | solution.py:12
  162.5 15.5 %collective-permute-start.1 = (bf16[128,128]{1,0:T(8,128)(2,1)S(1)}, bf16[128,128]{1,0:T(8,128)(2,1)S(1)}, u32[]{:S(2)}, u32[]{:S(2)}) collective-permute-start(bf16[128,128]{1,0:T(8,128)(2,1)S(1)} %copy.57), channel_id=1, source_target_pairs={{248,0},{0,8},{8,16},{16,24},{24,32},{32,40},{40,48},{48,56},{56,6... | collective-permute-start | bytes 98312 | tf_op jit(solution)/shard_map/while/body/eval_jaxpr/ppermute | solution.py:12
  165.8 12.1 %collective-permute-start = (bf16[128,128]{1,0:T(8,128)(2,1)S(1)}, bf16[128,128]{1,0:T(8,128)(2,1)S(1)}, u32[]{:S(2)}, u32[]{:S(2)}) collective-permute-start(bf16[128,128]{1,0:T(8,128)(2,1)S(1)} %copy.56), channel_id=1, source_target_pairs={{248,0},{0,8},{8,16},{16,24},{24,32},{32,40},{40,48},{48,56},{56,6... | collective-permute-start | bytes 98312 | tf_op jit(solution)/shard_map/while/body/eval_jaxpr/ppermute | solution.py:12
  179.0 15.4 %collective-permute-start.1 = (bf16[128,128]{1,0:T(8,128)(2,1)S(1)}, bf16[128,128]{1,0:T(8,128)(2,1)S(1)}, u32[]{:S(2)}, u32[]{:S(2)}) collective-permute-start(bf16[128,128]{1,0:T(8,128)(2,1)S(1)} %copy.57), channel_id=1, source_target_pairs={{248,0},{0,8},{8,16},{16,24},{24,32},{32,40},{40,48},{48,56},{56,6... | collective-permute-start | bytes 98312 | tf_op jit(solution)/shard_map/while/body/eval_jaxpr/ppermute | solution.py:12
  182.7 11.7 %collective-permute-start = (bf16[128,128]{1,0:T(8,128)(2,1)S(1)}, bf16[128,128]{1,0:T(8,128)(2,1)S(1)}, u32[]{:S(2)}, u32[]{:S(2)}) collective-permute-start(bf16[128,128]{1,0:T(8,128)(2,1)S(1)} %copy.56), channel_id=1, source_target_pairs={{248,0},{0,8},{8,16},{16,24},{24,32},{32,40},{40,48},{48,56},{56,6... | collective-permute-start | bytes 98312 | tf_op jit(solution)/shard_map/while/body/eval_jaxpr/ppermute | solution.py:12
  197.6 11.6 %collective-permute-start.1 = (bf16[128,128]{1,0:T(8,128)(2,1)S(1)}, bf16[128,128]{1,0:T(8,128)(2,1)S(1)}, u32[]{:S(2)}, u32[]{:S(2)}) collective-permute-start(bf16[128,128]{1,0:T(8,128)(2,1)S(1)} %copy.57), channel_id=1, source_target_pairs={{248,0},{0,8},{8,16},{16,24},{24,32},{32,40},{40,48},{48,56},{56,6... | collective-permute-start | bytes 98312 | tf_op jit(solution)/shard_map/while/body/eval_jaxpr/ppermute | solution.py:12
  199.8 9.5 %collective-permute-start = (bf16[128,128]{1,0:T(8,128)(2,1)S(1)}, bf16[128,128]{1,0:T(8,128)(2,1)S(1)}, u32[]{:S(2)}, u32[]{:S(2)}) collective-permute-start(bf16[128,128]{1,0:T(8,128)(2,1)S(1)} %copy.56), channel_id=1, source_target_pairs={{248,0},{0,8},{8,16},{16,24},{24,32},{32,40},{40,48},{48,56},{56,6... | collective-permute-start | bytes 98312 | tf_op jit(solution)/shard_map/while/body/eval_jaxpr/ppermute | solution.py:12
  212.4 10.5 %collective-permute-start.1 = (bf16[128,128]{1,0:T(8,128)(2,1)S(1)}, bf16[128,128]{1,0:T(8,128)(2,1)S(1)}, u32[]{:S(2)}, u32[]{:S(2)}) collective-permute-start(bf16[128,128]{1,0:T(8,128)(2,1)S(1)} %copy.57), channel_id=1, source_target_pairs={{248,0},{0,8},{8,16},{16,24},{24,32},{32,40},{40,48},{48,56},{56,6... | collective-permute-start | bytes 98312 | tf_op jit(solution)/shard_map/while/body/eval_jaxpr/ppermute | solution.py:12
  226.6 10.2 %collective-permute-start.1 = (bf16[128,128]{1,0:T(8,128)(2,1)S(1)}, bf16[128,128]{1,0:T(8,128)(2,1)S(1)}, u32[]{:S(2)}, u32[]{:S(2)}) collective-permute-start(bf16[128,128]{1,0:T(8,128)(2,1)S(1)} %copy.57), channel_id=1, source_target_pairs={{248,0},{0,8},{8,16},{16,24},{24,32},{32,40},{40,48},{48,56},{56,6... | collective-permute-start | bytes 98312 | tf_op jit(solution)/shard_map/while/body/eval_jaxpr/ppermute | solution.py:12
  239.8 10.2 %collective-permute-start.1 = (bf16[128,128]{1,0:T(8,128)(2,1)S(1)}, bf16[128,128]{1,0:T(8,128)(2,1)S(1)}, u32[]{:S(2)}, u32[]{:S(2)}) collective-permute-start(bf16[128,128]{1,0:T(8,128)(2,1)S(1)} %copy.57), channel_id=1, source_target_pairs={{248,0},{0,8},{8,16},{16,24},{24,32},{32,40},{40,48},{48,56},{56,6... | collective-permute-start | bytes 98312 | tf_op jit(solution)/shard_map/while/body/eval_jaxpr/ppermute | solution.py:12
  253.4 10.3 %collective-permute-start.1 = (bf16[128,128]{1,0:T(8,128)(2,1)S(1)}, bf16[128,128]{1,0:T(8,128)(2,1)S(1)}, u32[]{:S(2)}, u32[]{:S(2)}) collective-permute-start(bf16[128,128]{1,0:T(8,128)(2,1)S(1)} %copy.57), channel_id=1, source_target_pairs={{248,0},{0,8},{8,16},{16,24},{24,32},{32,40},{40,48},{48,56},{56,6... | collective-permute-start | bytes 98312 | tf_op jit(solution)/shard_map/while/body/eval_jaxpr/ppermute | solution.py:12
  266.7 10.4 %collective-permute-start.1 = (bf16[128,128]{1,0:T(8,128)(2,1)S(1)}, bf16[128,128]{1,0:T(8,128)(2,1)S(1)}, u32[]{:S(2)}, u32[]{:S(2)}) collective-permute-start(bf16[128,128]{1,0:T(8,128)(2,1)S(1)} %copy.57), channel_id=1, source_target_pairs={{248,0},{0,8},{8,16},{16,24},{24,32},{32,40},{40,48},{48,56},{56,6... | collective-permute-start | bytes 98312 | tf_op jit(solution)/shard_map/while/body/eval_jaxpr/ppermute | solution.py:12
  279.8 14.2 %collective-permute-start.1 = (bf16[128,128]{1,0:T(8,128)(2,1)S(1)}, bf16[128,128]{1,0:T(8,128)(2,1)S(1)}, u32[]{:S(2)}, u32[]{:S(2)}) collective-permute-start(bf16[128,128]{1,0:T(8,128)(2,1)S(1)} %copy.57), channel_id=1, source_target_pairs={{248,0},{0,8},{8,16},{16,24},{24,32},{32,40},{40,48},{48,56},{56,6... | collective-permute-start | bytes 98312 | tf_op jit(solution)/shard_map/while/body/eval_jaxpr/ppermute | solution.py:12
  281.8 12.2 %collective-permute-start = (bf16[128,128]{1,0:T(8,128)(2,1)S(1)}, bf16[128,128]{1,0:T(8,128)(2,1)S(1)}, u32[]{:S(2)}, u32[]{:S(2)}) collective-permute-start(bf16[128,128]{1,0:T(8,128)(2,1)S(1)} %copy.56), channel_id=1, source_target_pairs={{248,0},{0,8},{8,16},{16,24},{24,32},{32,40},{40,48},{48,56},{56,6... | collective-permute-start | bytes 98312 | tf_op jit(solution)/shard_map/while/body/eval_jaxpr/ppermute | solution.py:12
  295.1 15.2 %collective-permute-start.1 = (bf16[128,128]{1,0:T(8,128)(2,1)S(1)}, bf16[128,128]{1,0:T(8,128)(2,1)S(1)}, u32[]{:S(2)}, u32[]{:S(2)}) collective-permute-start(bf16[128,128]{1,0:T(8,128)(2,1)S(1)} %copy.57), channel_id=1, source_target_pairs={{248,0},{0,8},{8,16},{16,24},{24,32},{32,40},{40,48},{48,56},{56,6... | collective-permute-start | bytes 98312 | tf_op jit(solution)/shard_map/while/body/eval_jaxpr/ppermute | solution.py:12
  298.9 11.5 %collective-permute-start = (bf16[128,128]{1,0:T(8,128)(2,1)S(1)}, bf16[128,128]{1,0:T(8,128)(2,1)S(1)}, u32[]{:S(2)}, u32[]{:S(2)}) collective-permute-start(bf16[128,128]{1,0:T(8,128)(2,1)S(1)} %copy.56), channel_id=1, source_target_pairs={{248,0},{0,8},{8,16},{16,24},{24,32},{32,40},{40,48},{48,56},{56,6... | collective-permute-start | bytes 98312 | tf_op jit(solution)/shard_map/while/body/eval_jaxpr/ppermute | solution.py:12
  311.9 15.4 %collective-permute-start.1 = (bf16[128,128]{1,0:T(8,128)(2,1)S(1)}, bf16[128,128]{1,0:T(8,128)(2,1)S(1)}, u32[]{:S(2)}, u32[]{:S(2)}) collective-permute-start(bf16[128,128]{1,0:T(8,128)(2,1)S(1)} %copy.57), channel_id=1, source_target_pairs={{248,0},{0,8},{8,16},{16,24},{24,32},{32,40},{40,48},{48,56},{56,6... | collective-permute-start | bytes 98312 | tf_op jit(solution)/shard_map/while/body/eval_jaxpr/ppermute | solution.py:12
  315.1 12.2 %collective-permute-start = (bf16[128,128]{1,0:T(8,128)(2,1)S(1)}, bf16[128,128]{1,0:T(8,128)(2,1)S(1)}, u32[]{:S(2)}, u32[]{:S(2)}) collective-permute-start(bf16[128,128]{1,0:T(8,128)(2,1)S(1)} %copy.56), channel_id=1, source_target_pairs={{248,0},{0,8},{8,16},{16,24},{24,32},{32,40},{40,48},{48,56},{56,6... | collective-permute-start | bytes 98312 | tf_op jit(solution)/shard_map/while/body/eval_jaxpr/ppermute | solution.py:12
  328.4 15.5 %collective-permute-start.1 = (bf16[128,128]{1,0:T(8,128)(2,1)S(1)}, bf16[128,128]{1,0:T(8,128)(2,1)S(1)}, u32[]{:S(2)}, u32[]{:S(2)}) collective-permute-start(bf16[128,128]{1,0:T(8,128)(2,1)S(1)} %copy.57), channel_id=1, source_target_pairs={{248,0},{0,8},{8,16},{16,24},{24,32},{32,40},{40,48},{48,56},{56,6... | collective-permute-start | bytes 98312 | tf_op jit(solution)/shard_map/while/body/eval_jaxpr/ppermute | solution.py:12
  332.1 11.8 %collective-permute-start = (bf16[128,128]{1,0:T(8,128)(2,1)S(1)}, bf16[128,128]{1,0:T(8,128)(2,1)S(1)}, u32[]{:S(2)}, u32[]{:S(2)}) collective-permute-start(bf16[128,128]{1,0:T(8,128)(2,1)S(1)} %copy.56), channel_id=1, source_target_pairs={{248,0},{0,8},{8,16},{16,24},{24,32},{32,40},{40,48},{48,56},{56,6... | collective-permute-start | bytes 98312 | tf_op jit(solution)/shard_map/while/body/eval_jaxpr/ppermute | solution.py:12
  346.2 14.1 %collective-permute-start.1 = (bf16[128,128]{1,0:T(8,128)(2,1)S(1)}, bf16[128,128]{1,0:T(8,128)(2,1)S(1)}, u32[]{:S(2)}, u32[]{:S(2)}) collective-permute-start(bf16[128,128]{1,0:T(8,128)(2,1)S(1)} %copy.57), channel_id=1, source_target_pairs={{248,0},{0,8},{8,16},{16,24},{24,32},{32,40},{40,48},{48,56},{56,6... | collective-permute-start | bytes 98312 | tf_op jit(solution)/shard_map/while/body/eval_jaxpr/ppermute | solution.py:12
  349.1 11.2 %collective-permute-start = (bf16[128,128]{1,0:T(8,128)(2,1)S(1)}, bf16[128,128]{1,0:T(8,128)(2,1)S(1)}, u32[]{:S(2)}, u32[]{:S(2)}) collective-permute-start(bf16[128,128]{1,0:T(8,128)(2,1)S(1)} %copy.56), channel_id=1, source_target_pairs={{248,0},{0,8},{8,16},{16,24},{24,32},{32,40},{40,48},{48,56},{56,6... | collective-permute-start | bytes 98312 | tf_op jit(solution)/shard_map/while/body/eval_jaxpr/ppermute | solution.py:12
  361.9 13.7 %collective-permute-start.1 = (bf16[128,128]{1,0:T(8,128)(2,1)S(1)}, bf16[128,128]{1,0:T(8,128)(2,1)S(1)}, u32[]{:S(2)}, u32[]{:S(2)}) collective-permute-start(bf16[128,128]{1,0:T(8,128)(2,1)S(1)} %copy.57), channel_id=1, source_target_pairs={{248,0},{0,8},{8,16},{16,24},{24,32},{32,40},{40,48},{48,56},{56,6... | collective-permute-start | bytes 98312 | tf_op jit(solution)/shard_map/while/body/eval_jaxpr/ppermute | solution.py:12
  365.1 10.6 %collective-permute-start = (bf16[128,128]{1,0:T(8,128)(2,1)S(1)}, bf16[128,128]{1,0:T(8,128)(2,1)S(1)}, u32[]{:S(2)}, u32[]{:S(2)}) collective-permute-start(bf16[128,128]{1,0:T(8,128)(2,1)S(1)} %copy.56), channel_id=1, source_target_pairs={{248,0},{0,8},{8,16},{16,24},{24,32},{32,40},{40,48},{48,56},{56,6... | collective-permute-start | bytes 98312 | tf_op jit(solution)/shard_map/while/body/eval_jaxpr/ppermute | solution.py:12
  378.7 11.1 %collective-permute-start.1 = (bf16[128,128]{1,0:T(8,128)(2,1)S(1)}, bf16[128,128]{1,0:T(8,128)(2,1)S(1)}, u32[]{:S(2)}, u32[]{:S(2)}) collective-permute-start(bf16[128,128]{1,0:T(8,128)(2,1)S(1)} %copy.57), channel_id=1, source_target_pairs={{248,0},{0,8},{8,16},{16,24},{24,32},{32,40},{40,48},{48,56},{56,6... | collective-permute-start | bytes 98312 | tf_op jit(solution)/shard_map/while/body/eval_jaxpr/ppermute | solution.py:12
  392.6 11.7 %collective-permute-start.1 = (bf16[128,128]{1,0:T(8,128)(2,1)S(1)}, bf16[128,128]{1,0:T(8,128)(2,1)S(1)}, u32[]{:S(2)}, u32[]{:S(2)}) collective-permute-start(bf16[128,128]{1,0:T(8,128)(2,1)S(1)} %copy.57), channel_id=1, source_target_pairs={{248,0},{0,8},{8,16},{16,24},{24,32},{32,40},{40,48},{48,56},{56,6... | collective-permute-start | bytes 98312 | tf_op jit(solution)/shard_map/while/body/eval_jaxpr/ppermute | solution.py:12
  394.6 9.8 %collective-permute-start = (bf16[128,128]{1,0:T(8,128)(2,1)S(1)}, bf16[128,128]{1,0:T(8,128)(2,1)S(1)}, u32[]{:S(2)}, u32[]{:S(2)}) collective-permute-start(bf16[128,128]{1,0:T(8,128)(2,1)S(1)} %copy.56), channel_id=1, source_target_pairs={{248,0},{0,8},{8,16},{16,24},{24,32},{32,40},{40,48},{48,56},{56,6... | collective-permute-start | bytes 98312 | tf_op jit(solution)/shard_map/while/body/eval_jaxpr/ppermute | solution.py:12
  407.1 10.4 %collective-permute-start.1 = (bf16[128,128]{1,0:T(8,128)(2,1)S(1)}, bf16[128,128]{1,0:T(8,128)(2,1)S(1)}, u32[]{:S(2)}, u32[]{:S(2)}) collective-permute-start(bf16[128,128]{1,0:T(8,128)(2,1)S(1)} %copy.57), channel_id=1, source_target_pairs={{248,0},{0,8},{8,16},{16,24},{24,32},{32,40},{40,48},{48,56},{56,6... | collective-permute-start | bytes 98312 | tf_op jit(solution)/shard_map/while/body/eval_jaxpr/ppermute | solution.py:12
  420.3 10.3 %collective-permute-start.1 = (bf16[128,128]{1,0:T(8,128)(2,1)S(1)}, bf16[128,128]{1,0:T(8,128)(2,1)S(1)}, u32[]{:S(2)}, u32[]{:S(2)}) collective-permute-start(bf16[128,128]{1,0:T(8,128)(2,1)S(1)} %copy.57), channel_id=1, source_target_pairs={{248,0},{0,8},{8,16},{16,24},{24,32},{32,40},{40,48},{48,56},{56,6... | collective-permute-start | bytes 98312 | tf_op jit(solution)/shard_map/while/body/eval_jaxpr/ppermute | solution.py:12
  433.5 10.3 %collective-permute-start.1 = (bf16[128,128]{1,0:T(8,128)(2,1)S(1)}, bf16[128,128]{1,0:T(8,128)(2,1)S(1)}, u32[]{:S(2)}, u32[]{:S(2)}) collective-permute-start(bf16[128,128]{1,0:T(8,128)(2,1)S(1)} %copy.57), channel_id=1, source_target_pairs={{248,0},{0,8},{8,16},{16,24},{24,32},{32,40},{40,48},{48,56},{56,6... | collective-permute-start | bytes 98312 | tf_op jit(solution)/shard_map/while/body/eval_jaxpr/ppermute | solution.py:12
  446.7 12.2 %collective-permute-start.1 = (bf16[128,128]{1,0:T(8,128)(2,1)S(1)}, bf16[128,128]{1,0:T(8,128)(2,1)S(1)}, u32[]{:S(2)}, u32[]{:S(2)}) collective-permute-start(bf16[128,128]{1,0:T(8,128)(2,1)S(1)} %copy.57), channel_id=1, source_target_pairs={{248,0},{0,8},{8,16},{16,24},{24,32},{32,40},{40,48},{48,56},{56,6... | collective-permute-start | bytes 98312 | tf_op jit(solution)/shard_map/while/body/eval_jaxpr/ppermute | solution.py:12
  448.7 10.3 %collective-permute-start = (bf16[128,128]{1,0:T(8,128)(2,1)S(1)}, bf16[128,128]{1,0:T(8,128)(2,1)S(1)}, u32[]{:S(2)}, u32[]{:S(2)}) collective-permute-start(bf16[128,128]{1,0:T(8,128)(2,1)S(1)} %copy.56), channel_id=1, source_target_pairs={{248,0},{0,8},{8,16},{16,24},{24,32},{32,40},{40,48},{48,56},{56,6... | collective-permute-start | bytes 98312 | tf_op jit(solution)/shard_map/while/body/eval_jaxpr/ppermute | solution.py:12
  461.4 14.4 %collective-permute-start.1 = (bf16[128,128]{1,0:T(8,128)(2,1)S(1)}, bf16[128,128]{1,0:T(8,128)(2,1)S(1)}, u32[]{:S(2)}, u32[]{:S(2)}) collective-permute-start(bf16[128,128]{1,0:T(8,128)(2,1)S(1)} %copy.57), channel_id=1, source_target_pairs={{248,0},{0,8},{8,16},{16,24},{24,32},{32,40},{40,48},{48,56},{56,6... | collective-permute-start | bytes 98312 | tf_op jit(solution)/shard_map/while/body/eval_jaxpr/ppermute | solution.py:12
  463.7 12.1 %collective-permute-start = (bf16[128,128]{1,0:T(8,128)(2,1)S(1)}, bf16[128,128]{1,0:T(8,128)(2,1)S(1)}, u32[]{:S(2)}, u32[]{:S(2)}) collective-permute-start(bf16[128,128]{1,0:T(8,128)(2,1)S(1)} %copy.56), channel_id=1, source_target_pairs={{248,0},{0,8},{8,16},{16,24},{24,32},{32,40},{40,48},{48,56},{56,6... | collective-permute-start | bytes 98312 | tf_op jit(solution)/shard_map/while/body/eval_jaxpr/ppermute | solution.py:12
  477.0 16.1 %collective-permute-start.1 = (bf16[128,128]{1,0:T(8,128)(2,1)S(1)}, bf16[128,128]{1,0:T(8,128)(2,1)S(1)}, u32[]{:S(2)}, u32[]{:S(2)}) collective-permute-start(bf16[128,128]{1,0:T(8,128)(2,1)S(1)} %copy.57), channel_id=1, source_target_pairs={{248,0},{0,8},{8,16},{16,24},{24,32},{32,40},{40,48},{48,56},{56,6... | collective-permute-start | bytes 98312 | tf_op jit(solution)/shard_map/while/body/eval_jaxpr/ppermute | solution.py:12
  480.8 12.4 %collective-permute-start = (bf16[128,128]{1,0:T(8,128)(2,1)S(1)}, bf16[128,128]{1,0:T(8,128)(2,1)S(1)}, u32[]{:S(2)}, u32[]{:S(2)}) collective-permute-start(bf16[128,128]{1,0:T(8,128)(2,1)S(1)} %copy.56), channel_id=1, source_target_pairs={{248,0},{0,8},{8,16},{16,24},{24,32},{32,40},{40,48},{48,56},{56,6... | collective-permute-start | bytes 98312 | tf_op jit(solution)/shard_map/while/body/eval_jaxpr/ppermute | solution.py:12
  495.9 15.4 %collective-permute-start.1 = (bf16[128,128]{1,0:T(8,128)(2,1)S(1)}, bf16[128,128]{1,0:T(8,128)(2,1)S(1)}, u32[]{:S(2)}, u32[]{:S(2)}) collective-permute-start(bf16[128,128]{1,0:T(8,128)(2,1)S(1)} %copy.57), channel_id=1, source_target_pairs={{248,0},{0,8},{8,16},{16,24},{24,32},{32,40},{40,48},{48,56},{56,6... | collective-permute-start | bytes 98312 | tf_op jit(solution)/shard_map/while/body/eval_jaxpr/ppermute | solution.py:12
  498.7 12.7 %collective-permute-start = (bf16[128,128]{1,0:T(8,128)(2,1)S(1)}, bf16[128,128]{1,0:T(8,128)(2,1)S(1)}, u32[]{:S(2)}, u32[]{:S(2)}) collective-permute-start(bf16[128,128]{1,0:T(8,128)(2,1)S(1)} %copy.56), channel_id=1, source_target_pairs={{248,0},{0,8},{8,16},{16,24},{24,32},{32,40},{40,48},{48,56},{56,6... | collective-permute-start | bytes 98312 | tf_op jit(solution)/shard_map/while/body/eval_jaxpr/ppermute | solution.py:12
  (84 other events, 553.6 us)
where the time goes:
time: 592 us; the launch traced here: 589 us
  starting transfers between devices  361 us (61%)
  waiting for transfers between devices  114 us (19%)
  blocking collectives  63.8 us (11%)
  matrix products  31.8 us (5%)
  other arithmetic  8.65 us (1%)
    ppermute x126, starting transfers between devices, shifted(): return lax.ppermute(block, axis, route)  361 us
    ppermute x126, waiting for transfers between devices, shifted(): return lax.ppermute(block, axis, route)  114 us
    all_to_all x1, blocking collectives, sent_to_all(): lax.all_to_all(jnp.broadcast_to(shard[None], (size, *shard.shape)), axis,...  63.8 us
  transfers between devices with their start and end apart: 126, of which 50 were waited for; matrix products, arithmetic and copies ran while one was open for 7% of the time, Pallas kernels for 0%

commit v1 on v0

v1 whole, which is shorter than its diff:
```python
import math

import jax
import jax.numpy as jnp
from jax import lax
from jax.experimental import pallas as pl
from jax.experimental.pallas import tpu as pltpu
from jax.sharding import PartitionSpec as P

LOG2E = math.log2(math.e)
NEAR = 4


def near_groups(size):
    return [[base + i for i in range(NEAR)] for base in range(0, size, NEAR)]


def far_groups(size):
    return [list(range(first, size, NEAR)) for first in range(NEAR)]


def kernel(scale, tile, spans, own_spans, kv, qa, qb, da, db, stat_a, stat_b, dqa, dqb, dkv, acc):
    width = qa.shape[1]
    heads, toks = stat_a.shape[1], stat_a.shape[2]
    span_rows = toks // 2
    tiles = kv.shape[0] // tile
    per_tile = tile // span_rows
    token = lax.broadcasted_iota(jnp.int32, (tile, toks), 1)
    row = lax.broadcasted_iota(jnp.int32, (tile, toks), 0)
    query_span = jnp.where(token < span_rows, own_spans[0], own_spans[1])
    query_pos = query_span * span_rows + token % span_rows
    row_in_span = row % span_rows
    row_span = row // span_rows
    acc[...] = jnp.zeros_like(acc)

    def step(index, carry):
        start = pl.multiple_of(index * tile, tile)
        k = kv[pl.ds(start, tile), :width]
        v = kv[pl.ds(start, tile), width:]
        key_span = jnp.full((tile, toks), spans[index * per_tile], jnp.int32)
        for j in range(1, per_tile):
            key_span = jnp.where(row_span == j, spans[index * per_tile + j], key_span)
        visible = key_span * span_rows + row_in_span <= query_pos
        dk = jnp.zeros((tile, width), jnp.float32)
        dv = jnp.zeros((tile, width), jnp.float32)
        for half, (q_ref, d_ref, stat) in enumerate(((qa, da, stat_a), (qb, db, stat_b))):
            q = q_ref[...]
            d = d_ref[...]
            nt = (((1,), (1,)), ((), ()))
            s = lax.dot_general(k, q, nt, preferred_element_type=jnp.float32)
            g = lax.dot_general(v, d, nt, preferred_element_type=jnp.float32)
            probs, grads = [], []
            for h in range(heads):
                cols = slice(h * toks, (h + 1) * toks)
                p = jnp.exp2(s[:, cols] * (scale * LOG2E) - stat[0, h : h + 1, :])
                p = jnp.where(visible, p, 0.0)
                probs.append(p.astype(jnp.bfloat16))
                grads.append((p * (g[:, cols] - stat[1, h : h + 1, :])).astype(jnp.bfloat16))
            p = jnp.concatenate(probs, axis=1)
            ds = jnp.concatenate(grads, axis=1)
            dv = dv + jnp.dot(p, d, preferred_element_type=jnp.float32)
            dk = dk + jnp.dot(ds, q, preferred_element_type=jnp.float32)
            acc[half] += lax.dot_general(
                ds, k, (((0,), (0,)), ((), ())), preferred_element_type=jnp.float32
            )
        dkv[pl.ds(start, tile), :width] = (dk * scale).astype(jnp.bfloat16)
        dkv[pl.ds(start, tile), width:] = dv.astype(jnp.bfloat16)
        return carry

    lax.fori_loop(0, tiles, step, 0)
    dqa[...] = acc[0] * scale
    dqb[...] = (acc[1] * scale).astype(jnp.bfloat16)


def attention_grads(spans, own_spans, kv, qa, qb, da, db, stat_a, stat_b):
    rows, width = qa.shape
    keys = kv.shape[0]
    tile = min(256, keys)
    smem = pl.BlockSpec(memory_space=pltpu.SMEM)
    vmem = pl.BlockSpec(memory_space=pltpu.VMEM)

    def body(*refs):
        kernel(1.0 / math.sqrt(width), tile, *refs)

    return pl.pallas_call(
        body,
        out_shape=(
            jax.ShapeDtypeStruct((rows, width), jnp.float32),
            jax.ShapeDtypeStruct((rows, width), jnp.bfloat16),
            jax.ShapeDtypeStruct((keys, 2 * width), jnp.bfloat16),
        ),
        in_specs=[smem, smem] + [vmem] * 7,
        out_specs=(vmem, vmem, vmem),
        scratch_shapes=[pltpu.VMEM((2, rows, width), jnp.float32)],
        compiler_params=pltpu.CompilerParams(vmem_limit_bytes=32 * 1024 * 1024),
        cost_estimate=pl.CostEstimate(
            flops=2 * 5 * 2 * rows * keys * width,
            bytes_accessed=4 * keys * width * 2,
            transcendentals=2 * rows * keys,
        ),
    )(spans, own_spans, kv, qa, qb, da, db, stat_a, stat_b)


def body(queries, keys, values, out, log_total, d_out, span_order):
    size = lax.axis_size("inner")
    place = lax.axis_index("inner")
    core = lax.axis_index("head")
    toks, heads, width = queries.shape[1:]
    half = toks // 2
    far = size // NEAR
    swap = [(0, 1), (1, 0)]

    qa = jnp.transpose(queries[0], (1, 0, 2)).reshape(heads * toks, width)
    da = jnp.transpose(d_out[0], (1, 0, 2)).reshape(heads * toks, width)
    delta = jnp.transpose(
        jnp.sum(out[0].astype(jnp.float32) * d_out[0].astype(jnp.float32), axis=-1)
    )
    stat_a = jnp.stack([log_total[0] * LOG2E, delta])
    qda = jnp.concatenate([qa, da])
    qdb = lax.ppermute(qda, "head", swap)
    stat_b = lax.ppermute(stat_a, "head", swap)
    qb, db = qdb[: heads * toks], qdb[heads * toks :]

    kv = jnp.concatenate([keys[0], values[0]], axis=1)
    kv = lax.dynamic_slice_in_dim(kv, core * half, half, 0)
    kv = lax.all_gather(kv, "inner", axis_index_groups=far_groups(size), tiled=True)
    kv = jnp.broadcast_to(kv[None], (NEAR, *kv.shape)).reshape(NEAR * far * half, 2 * width)
    kv = lax.all_to_all(kv, "inner", 0, 0, axis_index_groups=near_groups(size), tiled=True)

    order = span_order[0].reshape(far, NEAR, 2)
    spans = jnp.where(core == 0, order[:, :, 0], order[:, :, 1]).T.reshape(-1)
    own_spans = lax.dynamic_slice_in_dim(span_order[0], 2 * place, 2, 0)
    dqa, dqb, dkv = attention_grads(spans, own_spans, kv, qa, qb, da, db, stat_a, stat_b)

    dq_other = lax.ppermute(dqb, "head", swap)
    dkv = lax.all_to_all(dkv, "inner", 0, 0, axis_index_groups=near_groups(size), tiled=True)
    dkv = jnp.sum(dkv.reshape(NEAR, far * half, 2 * width).astype(jnp.float32), axis=0)
    dkv = dkv.astype(jnp.bfloat16)
    dkv = lax.all_to_all(dkv, "inner", 0, 0, axis_index_groups=far_groups(size), tiled=True)
    dkv = jnp.sum(dkv.reshape(far, half, 2 * width).astype(jnp.float32), axis=0)
    dkv = dkv.astype(jnp.bfloat16)
    other = lax.ppermute(dkv, "head", swap)
    first = jnp.where(core == 0, dkv, other)
    second = jnp.where(core == 0, other, dkv)
    dkv = jnp.concatenate([first, second])

    dq = (dqa + dq_other.astype(jnp.float32)).astype(jnp.bfloat16)
    dq = jnp.transpose(dq.reshape(heads, toks, width), (1, 0, 2))
    return dq[None], dkv[None, :, :width], dkv[None, :, width:]


def solution(mesh):
    in_specs = (
        P(("groups", "outer"), "inner", "head", None),
        P(("groups", "outer"), "inner", None),
        P(("groups", "outer"), "inner", None),
        P(("groups", "outer"), "inner", "head", None),
        P(("groups", "outer"), "head", "inner"),
        P(("groups", "outer"), "inner", "head", None),
        P(("groups", "outer"), None),
    )
    out_specs = (
        P(("groups", "outer"), "inner", "head", None),
        P(("groups", "outer"), "inner", None),
        P(("groups", "outer"), "inner", None),
    )
    return jax.shard_map(body, mesh=mesh, in_specs=in_specs, out_specs=out_specs, check_vma=False)
```

time: 592 us -> 192 us (0.32)
  starting transfers between devices: 361 us -> 42.8 us
  waiting for transfers between devices: 114 us -> 35.4 us
  blocking collectives: 63.8 us -> 96 us
  matrix products: 31.8 us -> 0 us
  Pallas kernels: 0 us -> 9.21 us
    ppermute x126 -> x4, starting transfers between devices: 361 us -> 25.8 us  [the longest x1 9.91 us: body(): other = lax.ppermute(dkv, 'head', swap)]
    ppermute x126 -> x4, waiting for transfers between devices: 114 us -> 0.04 us  [the longest x1 0.03 us: body(): other = lax.ppermute(dkv, 'head', swap)]
    all_gather x0 -> x1, blocking collectives: none -> 68.6 us  [body(): lax.all_gather(kv, 'inner', axis_index_groups=far_groups(size), tiled=True)]
    all_to_all x1, blocking collectives: 63.8 us -> 27.3 us  [body(): lax.all_to_all(dkv, 'inner', 0, 0, axis_index_groups=near_groups(size), t...]
    all_to_all x0 -> x2, waiting for transfers between devices: none -> 35.4 us  [the longest x1 27.1 us: body(): lax.all_to_all(dkv, 'inner', 0, 0, axis_index_groups=far_groups(size), ti...]
    dot_general x160 -> x0, matrix products: 31.8 us -> none  [the longest x32 7.68 us: block_grads(): jnp.einsum('htu,ud->thd', grad_scores, key_rows, preferred_element_type=j...]
    all_to_all x0 -> x2, starting transfers between devices: none -> 17 us  [the longest x1 11.3 us: body(): lax.all_to_all(dkv, 'inner', 0, 0, axis_index_groups=far_groups(size), ti...]
    pallas_call x0 -> x1, Pallas kernels: none -> 9.21 us  [attention_grads(): pl.pallas_call(body, out_shape=(jax.ShapeDtypeStruct((rows, width), jnp.f...]
  transfers between devices with their start and end apart: 126 -> 6, of which waited for: 50 -> 2; matrix products, arithmetic and copies ran while one was open for 7% -> 1% of each run, Pallas kernels for 0% -> 0%
where the time goes in v1:
time: 192 us; the launch traced here: 191 us
  blocking collectives  96 us (50%)
  starting transfers between devices  42.8 us (22%)
  waiting for transfers between devices  35.4 us (18%)
  Pallas kernels  9.21 us (5%)
  local copies, waits for them, and re-layouts  3.59 us (2%)
  other arithmetic  3.33 us (2%)
    all_gather x1, blocking collectives, body(): lax.all_gather(kv, 'inner', axis_index_groups=far_groups(size), tiled=True)  68.6 us
    all_to_all x1, blocking collectives, body(): lax.all_to_all(dkv, 'inner', 0, 0, axis_index_groups=near_groups(size), t...  27.3 us
    all_to_all x1, waiting for transfers between devices, body(): lax.all_to_all(dkv, 'inner', 0, 0, axis_index_groups=far_groups(size), ti...  27.1 us
    all_to_all x1, starting transfers between devices, body(): lax.all_to_all(dkv, 'inner', 0, 0, axis_index_groups=far_groups(size), ti...  11.3 us
    ppermute x1, starting transfers between devices, body(): other = lax.ppermute(dkv, 'head', swap)  9.91 us
    pallas_call x1, Pallas kernels, attention_grads(): pl.pallas_call(body, out_shape=(jax.ShapeDtypeStruct((rows, width), jnp.f...  9.21 us
    ppermute x1, starting transfers between devices, body(): stat_b = lax.ppermute(stat_a, 'head', swap)  9.08 us
    all_to_all x1, waiting for transfers between devices, body(): lax.all_to_all(kv, 'inner', 0, 0, axis_index_groups=near_groups(size), ti...  8.23 us
  transfers between devices with their start and end apart: 6, of which 2 were waited for; matrix products, arithmetic and copies ran while one was open for 1% of the time, Pallas kernels for 0%

profile of v1, /device:TPU:33, one launch (start us, length us, event | category | flops | bytes accessed | tf_op | source)
XLA Modules:
  0.0 191.0 jit_solution(4289829914985974446)
XLA Ops:
  0.6 0.7 fusion.3
  1.4 68.6 %all_gather.3 = bf16[512,256]{1,0:T(8,128)(2,1)S(1)} all-gather(bf16[64,256]{1,0:T(8,128)(2,1)S(1)} %fusion.3), channel_id=1, replica_groups={{0,32,64,96,128,160,192,224},{8,40,72,104,136,168,200,232},{16,48,80,11..., dimensions={0}, use_global_device_ids=true | all-gather | bytes 294912 | tf_op jit(solution)/shard_map/all_gather | solution.py:126
  70.0 1.0 broadcast_in_dim.15
  71.0 0.0 copy-start
  71.0 0.0 copy-start.1
  71.1 5.7 %all-to-all-start = ((bf16[4,512,256]{2,1,0:T(8,128)(2,1)}), bf16[4,512,256]{2,1,0:T(8,128)(2,1)S(1)}, u32[]{:S(2)}, u32[]{:S(2)}) async-start(bf16[4,512,256]{2,1,0:T(8,128)(2,1)} %broadcast_in_dim.15), calls=%async_computation | async-start | bytes 2097152 | tf_op jit(solution)/shard_map/all_to_all | solution.py:128
  76.7 0.0 copy-done
  76.7 0.0 copy-done.1
  76.7 0.0 copy-start.2
  76.7 0.2 fusion
  77.0 0.0 copy-start.3
  77.0 0.1 copy.26
  77.0 0.6 copy-done.3
  77.6 9.1 %collective-permute-start.1 = (f32[2,4,128]{2,1,0:T(4,128)S(1)}, f32[2,4,128]{2,1,0:T(4,128)S(1)}, u32[]{:S(2)}, u32[]{:S(2)}) collective-permute-start(f32[2,4,128]{2,1,0:T(4,128)S(1)} %pad_maximum_fusion.2.refs_7_), channel_id=1, source_target_pairs={{0,1},{1,0},{2,3},{3,2},{4,5},{5,4},{6,7},{7,6},{8,9},{9,8},{10,11... | collective-permute-start | bytes 12296 | tf_op jit(solution)/shard_map/ppermute | solution.py:121
  86.7 0.0 copy-done.2
  86.8 2.0 %collective-permute-start = (bf16[1024,128]{1,0:T(8,128)(2,1)S(1)}, bf16[1024,128]{1,0:T(8,128)(2,1)S(1)}, u32[]{:S(2)}, u32[]{:S(2)}) collective-permute-start(bf16[1024,128]{1,0:T(8,128)(2,1)S(1)} %pad_maximum_fusion), channel_id=1, source_target_pairs={{0,1},{1,0},{2,3},{3,2},{4,5},{5,4},{6,7},{7,6},{8,9},{9,8},{10,11... | collective-permute-start | bytes 786440 | tf_op jit(solution)/shard_map/ppermute | solution.py:120
  88.8 0.0 copy-start.4
  88.8 0.5 broadcast.7
  89.3 0.1 copy-done.4
  89.5 0.7 reduce.7
  90.1 0.1 reshape_squeeze.3
  90.2 0.1 slice_select_fusion
  90.3 0.1 copy.23
  90.4 0.1 reshape.36.refs_0_
  90.5 0.1 fusion.5.refs_1_
  90.6 0.0 collective-permute-done
  90.6 0.0 collective-permute-done.1.refs_8_
  90.6 8.2 %all-to-all-done = bf16[4,512,256]{2,1,0:T(8,128)(2,1)S(1)} async-done(((bf16[4,512,256]{2,1,0:T(8,128)(2,1)}), bf16[4,512,256]{2,1,0:T(8,128)(2,1)S(1)}, u32[]{:S(2)}, u32[]{:S(2)}) %all-to-all-start) | async-done | bytes 1048608 | tf_op jit(solution)/shard_map/all_to_all | solution.py:128
  98.9 9.2 %shard_map.94 = (f32[512,128]{1,0:T(8,128)S(1)}, bf16[512,128]{1,0:T(8,128)(2,1)S(1)}, bf16[2048,256]{1,0:T(8,128)(2,1)S(1)}) custom-call(s32[32]{0:T(128)S(1)} %reshape.36.refs_0_, s32[2]{0:T(128)S(1)} %fusion.5.refs_1_, bf16[2048,256]{1,0:T(8,128)(2,1)S(1)} %bitcast.35, bf16[512,128]{1,0:T(8,128)(2,1)S(1)} %bitcast.38, ...), custom_call_target="tpu_custom_call" | custom-call | flops 2684354560 | bytes 2097152 | tf_op jit(solution)/shard_map/pallas_call | solution.py:85
  108.1 27.3 %all_to_all.26 = bf16[4,512,256]{2,1,0:T(8,128)(2,1)S(1)} all-to-all(bf16[4,512,256]{2,1,0:T(8,128)(2,1)S(1)} %bitcast.36), channel_id=1, replica_groups={{0,8,16,24},{32,40,48,56},{64,72,80,88},{96,104,112,120},{128,136,144,1..., dimensions={0} | all-to-all | bytes 2097152 | tf_op jit(solution)/shard_map/all_to_all | solution.py:136
  135.4 0.9 reduce_sum.34
  136.3 11.3 %all-to-all-start.2 = ((bf16[8,64,256]{2,1,0:T(8,128)(2,1)}), bf16[8,64,256]{2,1,0:T(8,128)(2,1)S(1)}, u32[]{:S(2)}, u32[]{:S(2)}) async-start(bf16[8,64,256]{2,1,0:T(8,128)(2,1)} %bitcast.19), calls=%async_computation.2 | async-start | bytes 524288 | tf_op jit(solution)/shard_map/all_to_all | solution.py:139
  147.6 4.8 %collective-permute-start.2 = (bf16[512,128]{1,0:T(8,128)(2,1)S(1)}, bf16[512,128]{1,0:T(8,128)(2,1)S(1)}, u32[]{:S(2)}, u32[]{:S(2)}) collective-permute-start(bf16[512,128]{1,0:T(8,128)(2,1)S(1)} %get-tuple-element.7), channel_id=1, source_target_pairs={{0,1},{1,0},{2,3},{3,2},{4,5},{5,4},{6,7},{7,6},{8,9},{9,8},{10,11... | collective-permute-start | bytes 393224 | tf_op jit(solution)/shard_map/ppermute | solution.py:135
  152.5 27.1 %all-to-all-done.2 = bf16[8,64,256]{2,1,0:T(8,128)(2,1)S(1)} async-done(((bf16[8,64,256]{2,1,0:T(8,128)(2,1)}), bf16[8,64,256]{2,1,0:T(8,128)(2,1)S(1)}, u32[]{:S(2)}, u32[]{:S(2)}) %all-to-all-start.2) | async-done | bytes 262176 | tf_op jit(solution)/shard_map/all_to_all | solution.py:139
  179.6 9.9 %collective-permute-start.3 = (bf16[64,256]{1,0:T(8,128)(2,1)S(1)}, bf16[64,256]{1,0:T(8,128)(2,1)S(1)}, u32[]{:S(2)}, u32[]{:S(2)}) collective-permute-start(bf16[64,256]{1,0:T(8,128)(2,1)S(1)} %reduce_sum.35), channel_id=1, source_target_pairs={{0,1},{1,0},{2,3},{3,2},{4,5},{5,4},{6,7},{7,6},{8,9},{9,8},{10,11... | collective-permute-start | bytes 98312 | tf_op jit(solution)/shard_map/ppermute | solution.py:142
  189.5 0.0 collective-permute-done.2
  189.6 0.8 copy.29
  190.4 0.0 collective-permute-done.3
  190.4 0.6 fusion.4
  (9 shorter events, 0.2 us)
Async XLA Ops:
  71.0 5.7 %copy-start = (bf16[1,128,4,128]{3,2,1,0:T(4,128)(2,1)S(1)}, bf16[1,128,4,128]{3,2,1,0:T(4,128)(2,1)}, u32[]{:S(2)}) copy-start(bf16[1,128,4,128]{3,2,1,0:T(4,128)(2,1)} %param.12) | copy-start | bytes 393220
  71.0 5.7 %copy-start.1 = (bf16[1,128,4,128]{3,2,1,0:T(4,128)(2,1)S(1)}, bf16[1,128,4,128]{3,2,1,0:T(4,128)(2,1)}, u32[]{:S(2)}) copy-start(bf16[1,128,4,128]{3,2,1,0:T(4,128)(2,1)} %param.10) | copy-start | bytes 393220
  71.1 27.8 %all-to-all-start = ((bf16[4,512,256]{2,1,0:T(8,128)(2,1)}), bf16[4,512,256]{2,1,0:T(8,128)(2,1)S(1)}, u32[]{:S(2)}, u32[]{:S(2)}) async-start(bf16[4,512,256]{2,1,0:T(8,128)(2,1)} %broadcast_in_dim.15), calls=%async_computation | async-start | bytes 2097152 | tf_op jit(solution)/shard_map/all_to_all | solution.py:128
  76.7 10.0 %copy-start.2 = (bf16[1,128,4,128]{3,2,1,0:T(4,128)(2,1)S(1)}, bf16[1,128,4,128]{3,2,1,0:T(4,128)(2,1)}, u32[]{:S(2)}) copy-start(bf16[1,128,4,128]{3,2,1,0:T(4,128)(2,1)} %param.7) | copy-start | bytes 393220
  77.0 0.7 copy-start.3
  77.6 13.0 %collective-permute-start.1 = (f32[2,4,128]{2,1,0:T(4,128)S(1)}, f32[2,4,128]{2,1,0:T(4,128)S(1)}, u32[]{:S(2)}, u32[]{:S(2)}) collective-permute-start(f32[2,4,128]{2,1,0:T(4,128)S(1)} %pad_maximum_fusion.2.refs_7_), channel_id=1, source_target_pairs={{0,1},{1,0},{2,3},{3,2},{4,5},{5,4},{6,7},{7,6},{8,9},{9,8},{10,11... | collective-permute-start | bytes 12296 | tf_op jit(solution)/shard_map/ppermute | solution.py:121
  86.8 3.8 %collective-permute-start = (bf16[1024,128]{1,0:T(8,128)(2,1)S(1)}, bf16[1024,128]{1,0:T(8,128)(2,1)S(1)}, u32[]{:S(2)}, u32[]{:S(2)}) collective-permute-start(bf16[1024,128]{1,0:T(8,128)(2,1)S(1)} %pad_maximum_fusion), channel_id=1, source_target_pairs={{0,1},{1,0},{2,3},{3,2},{4,5},{5,4},{6,7},{7,6},{8,9},{9,8},{10,11... | collective-permute-start | bytes 786440 | tf_op jit(solution)/shard_map/ppermute | solution.py:120
  88.8 0.7 copy-start.4
  136.3 43.3 %all-to-all-start.2 = ((bf16[8,64,256]{2,1,0:T(8,128)(2,1)}), bf16[8,64,256]{2,1,0:T(8,128)(2,1)S(1)}, u32[]{:S(2)}, u32[]{:S(2)}) async-start(bf16[8,64,256]{2,1,0:T(8,128)(2,1)} %bitcast.19), calls=%async_computation.2 | async-start | bytes 524288 | tf_op jit(solution)/shard_map/all_to_all | solution.py:139
  147.6 41.9 %collective-permute-start.2 = (bf16[512,128]{1,0:T(8,128)(2,1)S(1)}, bf16[512,128]{1,0:T(8,128)(2,1)S(1)}, u32[]{:S(2)}, u32[]{:S(2)}) collective-permute-start(bf16[512,128]{1,0:T(8,128)(2,1)S(1)} %get-tuple-element.7), channel_id=1, source_target_pairs={{0,1},{1,0},{2,3},{3,2},{4,5},{5,4},{6,7},{7,6},{8,9},{9,8},{10,11... | collective-permute-start | bytes 393224 | tf_op jit(solution)/shard_map/ppermute | solution.py:135
  179.6 10.8 %collective-permute-start.3 = (bf16[64,256]{1,0:T(8,128)(2,1)S(1)}, bf16[64,256]{1,0:T(8,128)(2,1)S(1)}, u32[]{:S(2)}, u32[]{:S(2)}) collective-permute-start(bf16[64,256]{1,0:T(8,128)(2,1)S(1)} %reduce_sum.35), channel_id=1, source_target_pairs={{0,1},{1,0},{2,3},{3,2},{4,5},{5,4},{6,7},{7,6},{8,9},{9,8},{10,11... | collective-permute-start | bytes 98312 | tf_op jit(solution)/shard_map/ppermute | solution.py:142

commit v2 on v1

v2 whole, which is shorter than its diff:
```python
import functools
import math

import jax
import jax.numpy as jnp
from jax import lax
from jax.experimental import pallas as pl
from jax.experimental.pallas import tpu as pltpu
from jax.sharding import PartitionSpec as P


LOG2E = math.log2(math.e)
PAIR = 2
CALLS = (1, 3, 4)
STAT_ROWS = 16


def split_stats(stats):
    high = lax.reduce_precision(stats, 8, 7)
    middle = lax.reduce_precision(stats - high, 8, 7)
    low = stats - high - middle
    pad = ((0, STAT_ROWS - stats.shape[0]), (0, 0))
    return [jnp.pad(a, pad).astype(jnp.bfloat16) for a in (high, middle, low)]


def kernel(first, count, heads, toks, order, where, kv_a, kv_b, *refs):
    fresh = first == 0
    payloads = refs[:4]
    dq, dkv = refs[4 if fresh else 5 :]
    rows = heads * toks
    span_rows = toks // 2
    ring = kv_a.shape[0]
    width = kv_a.shape[2] // 2
    scale = 1.0 / math.sqrt(width)
    place, core = where[0], where[1]
    step, parity = place // PAIR, place % PAIR
    token = lax.broadcasted_iota(jnp.int32, (toks, toks), 1)
    row = lax.broadcasted_iota(jnp.int32, (toks, toks), 0)
    key_row, token_row = row % span_rows, token % span_rows

    def query_pos(chip):
        span = jnp.where(token < span_rows, order[2 * chip], order[2 * chip + 1])
        return span * span_rows + token_row

    own_pos = query_pos(place)
    near_pos = query_pos(place + 1 - 2 * parity)
    nt = (((1,), (1,)), ((), ()))
    tn = (((0,), (0,)), ((), ()))
    if fresh:
        dq[...] = jnp.zeros_like(dq)
    else:
        dq[...] = refs[4][...]

    def one_block(index, carry):
        turn = first + index
        ahead = jnp.where(core == 0, turn - (ring // 2 - 1), ring // 2 - turn)
        block = lax.rem(step + ahead + ring, ring)
        chip = block * PAIR + parity
        a, b = kv_a[block], kv_b[block]
        kv = jnp.concatenate([jnp.where(core == 0, a, b), jnp.where(core == 0, b, a)])
        k, v = kv[:, :width], kv[:, width:]
        key_span = jnp.where(row < span_rows, order[2 * chip], order[2 * chip + 1])
        key_pos = key_span * span_rows + key_row
        dk = jnp.zeros((toks, width), jnp.float32)
        dv = jnp.zeros((toks, width), jnp.float32)
        for part, payload in enumerate(payloads):
            visible = key_pos <= (own_pos if part < 2 else near_pos)
            q = payload[:rows]
            d = payload[rows : 2 * rows]
            stats = [
                payload[2 * rows + i * STAT_ROWS : 2 * rows + (i + 1) * STAT_ROWS].astype(jnp.float32)
                for i in range(3)
            ]
            stat = stats[0] + stats[1] + stats[2]
            s = lax.dot_general(k, q, nt, preferred_element_type=jnp.float32)
            g = lax.dot_general(v, d, nt, preferred_element_type=jnp.float32)
            probs, grads = [], []
            for h in range(heads):
                cols = slice(h * toks, (h + 1) * toks)
                p = jnp.exp2(s[:, cols] * (scale * LOG2E) - stat[h : h + 1])
                p = jnp.where(visible, p, 0.0)
                probs.append(p.astype(jnp.bfloat16))
                ds = p * (g[:, cols] - stat[heads + h : heads + h + 1]) * scale
                grads.append(ds.astype(jnp.bfloat16))
            p = jnp.concatenate(probs, axis=1)
            ds = jnp.concatenate(grads, axis=1)
            dv = dv + jnp.dot(p, d, preferred_element_type=jnp.float32)
            dk = dk + jnp.dot(ds, q, preferred_element_type=jnp.float32)
            dq[part] += lax.dot_general(ds, k, tn, preferred_element_type=jnp.float32)
        dkv[index, :, :width] = dk
        dkv[index, :, width:] = dv
        return carry

    lax.fori_loop(0, count, one_block, 0)


def attention_grads(first, count, heads, toks, order, where, kv_a, kv_b, payloads, dq):
    width = kv_a.shape[2] // 2
    rows = heads * toks
    smem = pl.BlockSpec(memory_space=pltpu.SMEM)
    vmem = pl.BlockSpec(memory_space=pltpu.VMEM)
    operands = [order, where, kv_a, kv_b, *payloads] + ([] if dq is None else [dq])
    return pl.pallas_call(
        functools.partial(kernel, first, count, heads, toks),
        out_shape=(
            jax.ShapeDtypeStruct((4, rows, width), jnp.float32),
            jax.ShapeDtypeStruct((count, toks, 2 * width), jnp.float32),
        ),
        in_specs=[smem, smem] + [vmem] * (len(operands) - 2),
        out_specs=(vmem, vmem),
        input_output_aliases={} if dq is None else {len(operands) - 1: 0},
        compiler_params=pltpu.CompilerParams(vmem_limit_bytes=16 * 1024 * 1024),
        cost_estimate=pl.CostEstimate(
            flops=2 * 5 * 4 * rows * count * toks * width,
            bytes_accessed=8 * rows * width * 4,
            transcendentals=4 * rows * count * toks,
        ),
    )(*operands)


def body(queries, keys, values, out, log_total, d_out, span_order):
    size = lax.axis_size("inner")
    place = lax.axis_index("inner")
    core = lax.axis_index("head")
    toks, heads, width = queries.shape[1:]
    half = toks // 2
    rows = heads * toks
    both = ("inner", "head")

    def move(array, target):
        pairs = []
        for z in range(size):
            for c in range(2):
                to = target(z, c)
                if to is not None:
                    pairs.append((2 * z + c, 2 * (to[0] % size) + to[1]))
        return lax.ppermute(array, both, pairs)

    partners = (
        lambda z, c: (z, 1 - c),
        lambda z, c: (z ^ 1, c),
        lambda z, c: (z ^ 1, 1 - c),
    )

    delta = jnp.transpose(
        jnp.sum(out[0].astype(jnp.float32) * d_out[0].astype(jnp.float32), axis=-1)
    )
    stats = split_stats(jnp.concatenate([log_total[0] * LOG2E, delta]))
    payload = jnp.concatenate(
        [
            jnp.transpose(queries[0], (1, 0, 2)).reshape(rows, width),
            jnp.transpose(d_out[0], (1, 0, 2)).reshape(rows, width),
            *stats,
        ]
    )
    payloads = [payload]
    for partner in partners:
        payloads.append(move(payload, partner))

    kv = jnp.concatenate([keys[0], values[0]], axis=1)
    kv = lax.dynamic_slice_in_dim(kv, core * half, half, 0)
    groups = [list(range(first, size, PAIR)) for first in range(PAIR)]
    kv_a = lax.all_gather(kv, "inner", axis_index_groups=groups)
    kv_b = move(kv_a, partners[0])

    order = span_order[0]
    where = jnp.stack([place, core]).astype(jnp.int32)
    dq, parts, first = None, [], 0
    for count in CALLS:
        dq, part = attention_grads(
            first, count, heads, toks, order, where, kv_a, kv_b, payloads, dq
        )
        parts += [part[i] for i in range(count)]
        first += count

    total = parts[0].astype(jnp.bfloat16)
    for part in parts[1:]:
        total = move(total, lambda z, c: (z - PAIR, 0) if c == 0 else (z + PAIR, 1))
        total = (total.astype(jnp.float32) + part).astype(jnp.bfloat16)
    one = move(total, lambda z, c: (z, 1) if c == 0 else (z + PAIR, 0))
    two = move(total, lambda z, c: None if c == 0 else (z + PAIR, 1))
    two = jnp.where(core == 0, total, two)
    dkv = (one.astype(jnp.float32) + two.astype(jnp.float32)).astype(jnp.bfloat16)

    query_grad = dq[0]
    for part, partner in enumerate(partners, 1):
        query_grad = query_grad + move(dq[part].astype(jnp.bfloat16), partner).astype(jnp.float32)
    query_grad = query_grad.astype(jnp.bfloat16).reshape(heads, toks, width)
    query_grad = jnp.transpose(query_grad, (1, 0, 2))
    return query_grad[None], dkv[None, :, :width], dkv[None, :, width:]


def solution(mesh):
    in_specs = (
        P(("groups", "outer"), "inner", "head", None),
        P(("groups", "outer"), "inner", None),
        P(("groups", "outer"), "inner", None),
        P(("groups", "outer"), "inner", "head", None),
        P(("groups", "outer"), "head", "inner"),
        P(("groups", "outer"), "inner", "head", None),
        P(("groups", "outer"), None),
    )
    out_specs = (
        P(("groups", "outer"), "inner", "head", None),
        P(("groups", "outer"), "inner", None),
        P(("groups", "outer"), "inner", None),
    )
    return jax.shard_map(
        body, mesh=mesh, in_specs=in_specs, out_specs=out_specs, check_vma=False
    )
```

time: 192 us -> 176 us (0.917)
  blocking collectives: 96 us -> 70.5 us
  starting transfers between devices: 42.8 us -> 62.2 us
  waiting for transfers between devices: 35.4 us -> 24.3 us
  Pallas kernels: 9.21 us -> 12.4 us
  other arithmetic: 3.33 us -> 1.34 us
    ppermute x4 -> x16, starting transfers between devices: 25.8 us -> 62.2 us  [move(): return lax.ppermute(array, both, pairs)]
    all_to_all x2 -> x0, waiting for transfers between devices: 35.4 us -> none  [the longest x1 27.1 us: body(): lax.all_to_all(dkv, 'inner', 0, 0, axis_index_groups=far_groups(size), ti...]
    all_to_all x1 -> x0, blocking collectives: 27.3 us -> none  [body(): lax.all_to_all(dkv, 'inner', 0, 0, axis_index_groups=near_groups(size), t...]
    ppermute x4 -> x16, waiting for transfers between devices: 0.04 us -> 24.3 us  [move(): return lax.ppermute(array, both, pairs)]
    all_to_all x2 -> x0, starting transfers between devices: 17 us -> none  [the longest x1 11.3 us: body(): lax.all_to_all(dkv, 'inner', 0, 0, axis_index_groups=far_groups(size), ti...]
    pallas_call x1 -> x3, Pallas kernels: 9.21 us -> 12.4 us  [attention_grads(): pl.pallas_call(functools.partial(kernel, first, count, heads, toks), out_...]
  transfers between devices with their start and end apart: 6 -> 16, of which waited for: 2 -> 8; matrix products, arithmetic and copies ran while one was open for 1% -> 1% of each run, Pallas kernels for 0% -> 6%
where the time goes in v2:
time: 176 us; the launch traced here: 175 us
  blocking collectives  70.5 us (40%)
  starting transfers between devices  62.2 us (35%)
  waiting for transfers between devices  24.3 us (14%)
  Pallas kernels  12.4 us (7%)
  local copies, waits for them, and re-layouts  3.16 us (2%)
    all_gather x1, blocking collectives, body(): kv_a = lax.all_gather(kv, 'inner', axis_index_groups=groups)  70.5 us
    ppermute x16, starting transfers between devices, move(): return lax.ppermute(array, both, pairs)  62.2 us
    ppermute x16, waiting for transfers between devices, move(): return lax.ppermute(array, both, pairs)  24.3 us
    pallas_call x3, Pallas kernels, attention_grads(): pl.pallas_call(functools.partial(kernel, first, count, heads, toks), out_...  12.4 us
  transfers between devices with their start and end apart: 16, of which 8 were waited for; matrix products, arithmetic and copies ran while one was open for 1% of the time, Pallas kernels for 6%

profile of v2, /device:TPU:33, one launch (start us, length us, event | category | flops | bytes accessed | tf_op | source)
XLA Modules:
  0.0 174.8 jit_solution(11945104602428952104)
XLA Ops:
  0.6 0.7 fusion.11
  1.4 70.5 %all-gather = bf16[1024,256]{1,0:T(8,128)(2,1)S(1)} all-gather(bf16[64,256]{1,0:T(8,128)(2,1)S(1)} %fusion.11), channel_id=2, replica_groups={{0,16,32,48,64,80,96,112,128,144,160,176,192,208,224,240},{8,24,40,56,7..., dimensions={0}, use_global_device_ids=true | all-gather | bytes 557056 | tf_op jit(solution)/shard_map/all_gather | solution.py:163
  71.9 9.0 %collective-permute-start = (bf16[16,64,256]{2,1,0:T(8,128)(2,1)S(1)}, bf16[16,64,256]{2,1,0:T(8,128)(2,1)S(1)}, u32[]{:S(2)}, u32[]{:S(2)}) collective-permute-start(bf16[16,64,256]{2,1,0:T(8,128)(2,1)S(1)} %bitcast.75), channel_id=1, source_target_pairs={{0,1},{1,0},{8,9},{9,8},{16,17},{17,16},{24,25},{25,24},{32,33},{3... | collective-permute-start | bytes 1572872 | tf_op jit(solution)/shard_map/ppermute | solution.py:137
  80.9 0.0 copy-done.3
  80.9 0.2 fusion
  81.1 0.0 copy-start.6
  81.1 0.1 copy.17
  81.2 0.6 copy-done.6
  82.0 2.0 %collective-permute-start.1 = (bf16[1072,128]{1,0:T(8,128)(2,1)S(1)}, bf16[1072,128]{1,0:T(8,128)(2,1)S(1)}, u32[]{:S(2)}, u32[]{:S(2)}) collective-permute-start(bf16[1072,128]{1,0:T(8,128)(2,1)S(1)} %constant_dynamic-update-slice_fusion.refs_0_), channel_id=1, source_target_pairs={{0,1},{1,0},{8,9},{9,8},{16,17},{17,16},{24,25},{25,24},{32,33},{3... | collective-permute-start | bytes 823304 | tf_op jit(solution)/shard_map/ppermute | solution.py:137
  83.9 3.7 %collective-permute-start.2 = (bf16[1072,128]{1,0:T(8,128)(2,1)S(1)}, bf16[1072,128]{1,0:T(8,128)(2,1)S(1)}, u32[]{:S(2)}, u32[]{:S(2)}) collective-permute-start(bf16[1072,128]{1,0:T(8,128)(2,1)S(1)} %constant_dynamic-update-slice_fusion.refs_0_), channel_id=1, source_target_pairs={{0,8},{1,9},{8,0},{9,1},{16,24},{17,25},{24,16},{25,17},{32,40},{3... | collective-permute-start | bytes 823304 | tf_op jit(solution)/shard_map/ppermute | solution.py:137
  87.6 2.3 %collective-permute-start.3 = (bf16[1072,128]{1,0:T(8,128)(2,1)S(1)}, bf16[1072,128]{1,0:T(8,128)(2,1)S(1)}, u32[]{:S(2)}, u32[]{:S(2)}) collective-permute-start(bf16[1072,128]{1,0:T(8,128)(2,1)S(1)} %constant_dynamic-update-slice_fusion.refs_0_), channel_id=1, source_target_pairs={{0,9},{1,8},{8,1},{9,0},{16,25},{17,24},{24,17},{25,16},{32,41},{3... | collective-permute-start | bytes 823304 | tf_op jit(solution)/shard_map/ppermute | solution.py:137
  90.0 0.1 pad_add_fusion.where
  90.1 0.0 collective-permute-done.1.refs_1_
  90.1 4.0 %collective-permute-done.2.refs_2_ = bf16[1072,128]{1,0:T(8,128)(2,1)S(1)} collective-permute-done((bf16[1072,128]{1,0:T(8,128)(2,1)S(1)}, bf16[1072,128]{1,0:T(8,128)(2,1)S(1)}, u32[]{:S(2)}, u32[]{:S(2)}) %collective-permute-start.2) | collective-permute-done | bytes 274464 | tf_op jit(solution)/shard_map/ppermute | solution.py:137
  94.1 6.3 %collective-permute-done.3.refs_3_ = bf16[1072,128]{1,0:T(8,128)(2,1)S(1)} collective-permute-done((bf16[1072,128]{1,0:T(8,128)(2,1)S(1)}, bf16[1072,128]{1,0:T(8,128)(2,1)S(1)}, u32[]{:S(2)}, u32[]{:S(2)}) %collective-permute-start.3) | collective-permute-done | bytes 274464 | tf_op jit(solution)/shard_map/ppermute | solution.py:137
  100.3 0.0 collective-permute-done.kv_b
  100.3 1.8 %shard_map.94 = (f32[4,512,128]{2,1,0:T(8,128)S(1)}, f32[1,128,256]{2,1,0:T(8,128)S(1)}) custom-call(s32[64]{0:T(128)S(1)} %bitcast.79, s32[2]{0:T(128)S(1)} %pad_add_fusion.where, bf16[16,64,256]{2,1,0:T(8,128)(2,1)S(1)} %bitcast.76, bf16[16,64,256]{2,1,0:T(8,128)(2,1)S(1)} %collective-permute-done.kv_b, ...), custom_call_target="tpu_custom_call" | custom-call | flops 335544320 | bytes 2097152 | tf_op jit(solution)/shard_map/pallas_call | solution.py:103
  102.2 2.1 %collective-permute-start.7 = (bf16[128,256]{1,0:T(8,128)(2,1)S(1)}, bf16[128,256]{1,0:T(8,128)(2,1)S(1)}, u32[]{:S(2)}, u32[]{:S(2)}) collective-permute-start(bf16[128,256]{1,0:T(8,128)(2,1)S(1)} %convert_bitcast_fusion), channel_id=1, source_target_pairs={{0,240},{1,17},{8,248},{9,25},{16,0},{17,33},{24,8},{25,41},{32,16... | collective-permute-start | bytes 196616 | tf_op jit(solution)/shard_map/ppermute | solution.py:137
  104.4 0.9 copy-done.1
  105.3 4.6 %shard_map.95 = (f32[4,512,128]{2,1,0:T(8,128)S(1)}, f32[3,128,256]{2,1,0:T(8,128)S(1)}) custom-call(s32[64]{0:T(128)S(1)} %bitcast.80, s32[2]{0:T(128)S(1)} %pad_add_fusion.where, bf16[16,64,256]{2,1,0:T(8,128)(2,1)S(1)} %bitcast.77, bf16[16,64,256]{2,1,0:T(8,128)(2,1)S(1)} %collective-permute-done.kv_b, ...), custom_call_target="tpu_custom_call", output_to_operand_aliasing={{0}: (8, {})} | custom-call | flops 1006632960 | bytes 2097152 | tf_op jit(solution)/shard_map/pallas_call | solution.py:103
  109.9 0.1 collective-permute-done.7
  110.1 5.0 %collective-permute-start.8 = (bf16[128,256]{1,0:T(8,128)(2,1)S(1)}, bf16[128,256]{1,0:T(8,128)(2,1)S(1)}, u32[]{:S(2)}, u32[]{:S(2)}) collective-permute-start(bf16[128,256]{1,0:T(8,128)(2,1)S(1)} %fusion.10), channel_id=1, source_target_pairs={{0,240},{1,17},{8,248},{9,25},{16,0},{17,33},{24,8},{25,41},{32,16... | collective-permute-start | bytes 196616 | tf_op jit(solution)/shard_map/ppermute | solution.py:137
  115.1 2.2 %collective-permute-done.8 = bf16[128,256]{1,0:T(8,128)(2,1)S(1)} collective-permute-done((bf16[128,256]{1,0:T(8,128)(2,1)S(1)}, bf16[128,256]{1,0:T(8,128)(2,1)S(1)}, u32[]{:S(2)}, u32[]{:S(2)}) %collective-permute-start.8) | collective-permute-done | bytes 65568 | tf_op jit(solution)/shard_map/ppermute | solution.py:137
  117.3 3.8 %collective-permute-start.9 = (bf16[128,256]{1,0:T(8,128)(2,1)S(1)}, bf16[128,256]{1,0:T(8,128)(2,1)S(1)}, u32[]{:S(2)}, u32[]{:S(2)}) collective-permute-start(bf16[128,256]{1,0:T(8,128)(2,1)S(1)} %fusion.9), channel_id=1, source_target_pairs={{0,240},{1,17},{8,248},{9,25},{16,0},{17,33},{24,8},{25,41},{32,16... | collective-permute-start | bytes 196616 | tf_op jit(solution)/shard_map/ppermute | solution.py:137
  121.1 3.3 %collective-permute-done.9 = bf16[128,256]{1,0:T(8,128)(2,1)S(1)} collective-permute-done((bf16[128,256]{1,0:T(8,128)(2,1)S(1)}, bf16[128,256]{1,0:T(8,128)(2,1)S(1)}, u32[]{:S(2)}, u32[]{:S(2)}) %collective-permute-start.9) | collective-permute-done | bytes 65568 | tf_op jit(solution)/shard_map/ppermute | solution.py:137
  124.5 2.6 %collective-permute-start.10 = (bf16[128,256]{1,0:T(8,128)(2,1)S(1)}, bf16[128,256]{1,0:T(8,128)(2,1)S(1)}, u32[]{:S(2)}, u32[]{:S(2)}) collective-permute-start(bf16[128,256]{1,0:T(8,128)(2,1)S(1)} %fusion.8), channel_id=1, source_target_pairs={{0,240},{1,17},{8,248},{9,25},{16,0},{17,33},{24,8},{25,41},{32,16... | collective-permute-start | bytes 196616 | tf_op jit(solution)/shard_map/ppermute | solution.py:137
  127.1 5.9 %shard_map.96 = (f32[4,512,128]{2,1,0:T(8,128)S(1)}, f32[4,128,256]{2,1,0:T(8,128)S(1)}) custom-call(s32[64]{0:T(128)S(1)} %bitcast.81, s32[2]{0:T(128)S(1)} %pad_add_fusion.where, bf16[16,64,256]{2,1,0:T(8,128)(2,1)S(1)} %bitcast.78, bf16[16,64,256]{2,1,0:T(8,128)(2,1)S(1)} %collective-permute-done.kv_b, ...), custom_call_target="tpu_custom_call", output_to_operand_aliasing={{0}: (8, {})} | custom-call | flops 1342177280 | bytes 2097152 | tf_op jit(solution)/shard_map/pallas_call | solution.py:103
  133.0 0.0 collective-permute-done.10
  133.0 4.3 %collective-permute-start.11 = (bf16[128,256]{1,0:T(8,128)(2,1)S(1)}, bf16[128,256]{1,0:T(8,128)(2,1)S(1)}, u32[]{:S(2)}, u32[]{:S(2)}) collective-permute-start(bf16[128,256]{1,0:T(8,128)(2,1)S(1)} %fusion.7), channel_id=1, source_target_pairs={{0,240},{1,17},{8,248},{9,25},{16,0},{17,33},{24,8},{25,41},{32,16... | collective-permute-start | bytes 196616 | tf_op jit(solution)/shard_map/ppermute | solution.py:137
  137.4 2.8 %collective-permute-done.11 = bf16[128,256]{1,0:T(8,128)(2,1)S(1)} collective-permute-done((bf16[128,256]{1,0:T(8,128)(2,1)S(1)}, bf16[128,256]{1,0:T(8,128)(2,1)S(1)}, u32[]{:S(2)}, u32[]{:S(2)}) %collective-permute-start.11) | collective-permute-done | bytes 65568 | tf_op jit(solution)/shard_map/ppermute | solution.py:137
  140.2 3.1 %collective-permute-start.12 = (bf16[128,256]{1,0:T(8,128)(2,1)S(1)}, bf16[128,256]{1,0:T(8,128)(2,1)S(1)}, u32[]{:S(2)}, u32[]{:S(2)}) collective-permute-start(bf16[128,256]{1,0:T(8,128)(2,1)S(1)} %fusion.6), channel_id=1, source_target_pairs={{0,240},{1,17},{8,248},{9,25},{16,0},{17,33},{24,8},{25,41},{32,16... | collective-permute-start | bytes 196616 | tf_op jit(solution)/shard_map/ppermute | solution.py:137
  143.3 0.1 convert.21
  143.4 3.9 %collective-permute-done.12 = bf16[128,256]{1,0:T(8,128)(2,1)S(1)} collective-permute-done((bf16[128,256]{1,0:T(8,128)(2,1)S(1)}, bf16[128,256]{1,0:T(8,128)(2,1)S(1)}, u32[]{:S(2)}, u32[]{:S(2)}) %collective-permute-start.12) | collective-permute-done | bytes 65568 | tf_op jit(solution)/shard_map/ppermute | solution.py:137
  147.4 2.0 %collective-permute-start.13 = (bf16[128,256]{1,0:T(8,128)(2,1)S(1)}, bf16[128,256]{1,0:T(8,128)(2,1)S(1)}, u32[]{:S(2)}, u32[]{:S(2)}) collective-permute-start(bf16[128,256]{1,0:T(8,128)(2,1)S(1)} %fusion.5), channel_id=1, source_target_pairs={{0,240},{1,17},{8,248},{9,25},{16,0},{17,33},{24,8},{25,41},{32,16... | collective-permute-start | bytes 196616 | tf_op jit(solution)/shard_map/ppermute | solution.py:137
  149.4 9.8 %collective-permute-start.4 = (bf16[512,128]{1,0:T(8,128)(2,1)S(1)}, bf16[512,128]{1,0:T(8,128)(2,1)S(1)}, u32[]{:S(2)}, u32[]{:S(2)}) collective-permute-start(bf16[512,128]{1,0:T(8,128)(2,1)S(1)} %get-tuple-element.15), channel_id=1, source_target_pairs={{0,1},{1,0},{8,9},{9,8},{16,17},{17,16},{24,25},{25,24},{32,33},{3... | collective-permute-start | bytes 393224 | tf_op jit(solution)/shard_map/ppermute | solution.py:137
  159.2 3.6 %collective-permute-start.5 = (bf16[512,128]{1,0:T(8,128)(2,1)S(1)}, bf16[512,128]{1,0:T(8,128)(2,1)S(1)}, u32[]{:S(2)}, u32[]{:S(2)}) collective-permute-start(bf16[512,128]{1,0:T(8,128)(2,1)S(1)} %get-tuple-element.17), channel_id=1, source_target_pairs={{0,8},{1,9},{8,0},{9,1},{16,24},{17,25},{24,16},{25,17},{32,40},{3... | collective-permute-start | bytes 393224 | tf_op jit(solution)/shard_map/ppermute | solution.py:137
  162.7 2.0 %collective-permute-start.6 = (bf16[512,128]{1,0:T(8,128)(2,1)S(1)}, bf16[512,128]{1,0:T(8,128)(2,1)S(1)}, u32[]{:S(2)}, u32[]{:S(2)}) collective-permute-start(bf16[512,128]{1,0:T(8,128)(2,1)S(1)} %get-tuple-element.16), channel_id=1, source_target_pairs={{0,9},{1,8},{8,1},{9,0},{16,25},{17,24},{24,17},{25,16},{32,41},{3... | collective-permute-start | bytes 393224 | tf_op jit(solution)/shard_map/ppermute | solution.py:137
  164.7 0.0 collective-permute-done.13
  164.7 2.2 %collective-permute-start.14 = (bf16[128,256]{1,0:T(8,128)(2,1)S(1)}, bf16[128,256]{1,0:T(8,128)(2,1)S(1)}, u32[]{:S(2)}, u32[]{:S(2)}) collective-permute-start(bf16[128,256]{1,0:T(8,128)(2,1)S(1)} %fusion.4), channel_id=1, source_target_pairs={{0,1},{1,16},{8,9},{9,24},{16,17},{17,32},{24,25},{25,40},{32,33},... | collective-permute-start | bytes 196616 | tf_op jit(solution)/shard_map/ppermute | solution.py:137
  167.0 4.6 %collective-permute-start.15 = (bf16[128,256]{1,0:T(8,128)(2,1)S(1)}, bf16[128,256]{1,0:T(8,128)(2,1)S(1)}, u32[]{:S(2)}, u32[]{:S(2)}) collective-permute-start(bf16[128,256]{1,0:T(8,128)(2,1)S(1)} %fusion.4), channel_id=1, source_target_pairs={{1,17},{9,25},{17,33},{25,41},{33,49},{41,57},{49,65},{57,73},{65,... | collective-permute-start | bytes 196616 | tf_op jit(solution)/shard_map/ppermute | solution.py:137
  171.6 0.0 collective-permute-done.4
  171.6 0.0 collective-permute-done.5
  171.7 0.0 collective-permute-done.6
  171.7 0.1 fusion.3
  171.7 0.8 copy.20
  172.5 0.0 collective-permute-done.14
  172.5 1.7 collective-permute-done.15
  174.2 0.6 slice_bitcast_fusion.3
  (29 shorter events, 0.3 us)
Async XLA Ops:
  1.4 79.5 %copy-start.3 = (bf16[1,128,4,128]{3,2,1,0:T(4,128)(2,1)S(1)}, bf16[1,128,4,128]{3,2,1,0:T(4,128)(2,1)}, u32[]{:S(2)}) copy-start(bf16[1,128,4,128]{3,2,1,0:T(4,128)(2,1)} %param.12) | copy-start | bytes 393220
  1.4 79.5 %copy-start.4 = (bf16[1,128,4,128]{3,2,1,0:T(4,128)(2,1)S(1)}, bf16[1,128,4,128]{3,2,1,0:T(4,128)(2,1)}, u32[]{:S(2)}) copy-start(bf16[1,128,4,128]{3,2,1,0:T(4,128)(2,1)} %param.10) | copy-start | bytes 393220
  71.9 9.9 %copy-start.5 = (bf16[1,128,4,128]{3,2,1,0:T(4,128)(2,1)S(1)}, bf16[1,128,4,128]{3,2,1,0:T(4,128)(2,1)}, u32[]{:S(2)}) copy-start(bf16[1,128,4,128]{3,2,1,0:T(4,128)(2,1)} %param.7) | copy-start | bytes 393220
  71.9 28.5 %collective-permute-start = (bf16[16,64,256]{2,1,0:T(8,128)(2,1)S(1)}, bf16[16,64,256]{2,1,0:T(8,128)(2,1)S(1)}, u32[]{:S(2)}, u32[]{:S(2)}) collective-permute-start(bf16[16,64,256]{2,1,0:T(8,128)(2,1)S(1)} %bitcast.75), channel_id=1, source_target_pairs={{0,1},{1,0},{8,9},{9,8},{16,17},{17,16},{24,25},{25,24},{32,33},{3... | collective-permute-start | bytes 1572872 | tf_op jit(solution)/shard_map/ppermute | solution.py:137
  81.1 0.7 copy-start.6
  82.0 8.1 %collective-permute-start.1 = (bf16[1072,128]{1,0:T(8,128)(2,1)S(1)}, bf16[1072,128]{1,0:T(8,128)(2,1)S(1)}, u32[]{:S(2)}, u32[]{:S(2)}) collective-permute-start(bf16[1072,128]{1,0:T(8,128)(2,1)S(1)} %constant_dynamic-update-slice_fusion.refs_0_), channel_id=1, source_target_pairs={{0,1},{1,0},{8,9},{9,8},{16,17},{17,16},{24,25},{25,24},{32,33},{3... | collective-permute-start | bytes 823304 | tf_op jit(solution)/shard_map/ppermute | solution.py:137
  83.9 10.1 %collective-permute-start.2 = (bf16[1072,128]{1,0:T(8,128)(2,1)S(1)}, bf16[1072,128]{1,0:T(8,128)(2,1)S(1)}, u32[]{:S(2)}, u32[]{:S(2)}) collective-permute-start(bf16[1072,128]{1,0:T(8,128)(2,1)S(1)} %constant_dynamic-update-slice_fusion.refs_0_), channel_id=1, source_target_pairs={{0,8},{1,9},{8,0},{9,1},{16,24},{17,25},{24,16},{25,17},{32,40},{3... | collective-permute-start | bytes 823304 | tf_op jit(solution)/shard_map/ppermute | solution.py:137
  87.6 12.7 %collective-permute-start.3 = (bf16[1072,128]{1,0:T(8,128)(2,1)S(1)}, bf16[1072,128]{1,0:T(8,128)(2,1)S(1)}, u32[]{:S(2)}, u32[]{:S(2)}) collective-permute-start(bf16[1072,128]{1,0:T(8,128)(2,1)S(1)} %constant_dynamic-update-slice_fusion.refs_0_), channel_id=1, source_target_pairs={{0,9},{1,8},{8,1},{9,0},{16,25},{17,24},{24,17},{25,16},{32,41},{3... | collective-permute-start | bytes 823304 | tf_op jit(solution)/shard_map/ppermute | solution.py:137
  90.0 10.3 %copy-start.2 = (s32[1,64]{1,0:T(1,128)S(1)}, s32[1,64]{1,0:T(1,128)}, u32[]{:S(2)}) copy-start(s32[1,64]{1,0:T(1,128)} %param.13) | copy-start | bytes 772
  100.3 1.9 %copy-start = (bf16[1072,128]{1,0:T(8,128)(2,1)}, bf16[1072,128]{1,0:T(8,128)(2,1)S(1)}, u32[]{:S(2)}) copy-start(bf16[1072,128]{1,0:T(8,128)(2,1)S(1)} %collective-permute-done.3.refs_3_) | copy-start | bytes 823300
  102.2 7.8 %collective-permute-start.7 = (bf16[128,256]{1,0:T(8,128)(2,1)S(1)}, bf16[128,256]{1,0:T(8,128)(2,1)S(1)}, u32[]{:S(2)}, u32[]{:S(2)}) collective-permute-start(bf16[128,256]{1,0:T(8,128)(2,1)S(1)} %convert_bitcast_fusion), channel_id=1, source_target_pairs={{0,240},{1,17},{8,248},{9,25},{16,0},{17,33},{24,8},{25,41},{32,16... | collective-permute-start | bytes 196616 | tf_op jit(solution)/shard_map/ppermute | solution.py:137
  104.4 1.0 copy-start.1
  110.1 7.2 %collective-permute-start.8 = (bf16[128,256]{1,0:T(8,128)(2,1)S(1)}, bf16[128,256]{1,0:T(8,128)(2,1)S(1)}, u32[]{:S(2)}, u32[]{:S(2)}) collective-permute-start(bf16[128,256]{1,0:T(8,128)(2,1)S(1)} %fusion.10), channel_id=1, source_target_pairs={{0,240},{1,17},{8,248},{9,25},{16,0},{17,33},{24,8},{25,41},{32,16... | collective-permute-start | bytes 196616 | tf_op jit(solution)/shard_map/ppermute | solution.py:137
  117.3 7.2 %collective-permute-start.9 = (bf16[128,256]{1,0:T(8,128)(2,1)S(1)}, bf16[128,256]{1,0:T(8,128)(2,1)S(1)}, u32[]{:S(2)}, u32[]{:S(2)}) collective-permute-start(bf16[128,256]{1,0:T(8,128)(2,1)S(1)} %fusion.9), channel_id=1, source_target_pairs={{0,240},{1,17},{8,248},{9,25},{16,0},{17,33},{24,8},{25,41},{32,16... | collective-permute-start | bytes 196616 | tf_op jit(solution)/shard_map/ppermute | solution.py:137
  124.5 8.5 %collective-permute-start.10 = (bf16[128,256]{1,0:T(8,128)(2,1)S(1)}, bf16[128,256]{1,0:T(8,128)(2,1)S(1)}, u32[]{:S(2)}, u32[]{:S(2)}) collective-permute-start(bf16[128,256]{1,0:T(8,128)(2,1)S(1)} %fusion.8), channel_id=1, source_target_pairs={{0,240},{1,17},{8,248},{9,25},{16,0},{17,33},{24,8},{25,41},{32,16... | collective-permute-start | bytes 196616 | tf_op jit(solution)/shard_map/ppermute | solution.py:137
  133.0 7.2 %collective-permute-start.11 = (bf16[128,256]{1,0:T(8,128)(2,1)S(1)}, bf16[128,256]{1,0:T(8,128)(2,1)S(1)}, u32[]{:S(2)}, u32[]{:S(2)}) collective-permute-start(bf16[128,256]{1,0:T(8,128)(2,1)S(1)} %fusion.7), channel_id=1, source_target_pairs={{0,240},{1,17},{8,248},{9,25},{16,0},{17,33},{24,8},{25,41},{32,16... | collective-permute-start | bytes 196616 | tf_op jit(solution)/shard_map/ppermute | solution.py:137
  140.2 7.2 %collective-permute-start.12 = (bf16[128,256]{1,0:T(8,128)(2,1)S(1)}, bf16[128,256]{1,0:T(8,128)(2,1)S(1)}, u32[]{:S(2)}, u32[]{:S(2)}) collective-permute-start(bf16[128,256]{1,0:T(8,128)(2,1)S(1)} %fusion.6), channel_id=1, source_target_pairs={{0,240},{1,17},{8,248},{9,25},{16,0},{17,33},{24,8},{25,41},{32,16... | collective-permute-start | bytes 196616 | tf_op jit(solution)/shard_map/ppermute | solution.py:137
  147.4 17.3 %collective-permute-start.13 = (bf16[128,256]{1,0:T(8,128)(2,1)S(1)}, bf16[128,256]{1,0:T(8,128)(2,1)S(1)}, u32[]{:S(2)}, u32[]{:S(2)}) collective-permute-start(bf16[128,256]{1,0:T(8,128)(2,1)S(1)} %fusion.5), channel_id=1, source_target_pairs={{0,240},{1,17},{8,248},{9,25},{16,0},{17,33},{24,8},{25,41},{32,16... | collective-permute-start | bytes 196616 | tf_op jit(solution)/shard_map/ppermute | solution.py:137
  149.4 22.3 %collective-permute-start.4 = (bf16[512,128]{1,0:T(8,128)(2,1)S(1)}, bf16[512,128]{1,0:T(8,128)(2,1)S(1)}, u32[]{:S(2)}, u32[]{:S(2)}) collective-permute-start(bf16[512,128]{1,0:T(8,128)(2,1)S(1)} %get-tuple-element.15), channel_id=1, source_target_pairs={{0,1},{1,0},{8,9},{9,8},{16,17},{17,16},{24,25},{25,24},{32,33},{3... | collective-permute-start | bytes 393224 | tf_op jit(solution)/shard_map/ppermute | solution.py:137
  159.2 12.5 %collective-permute-start.5 = (bf16[512,128]{1,0:T(8,128)(2,1)S(1)}, bf16[512,128]{1,0:T(8,128)(2,1)S(1)}, u32[]{:S(2)}, u32[]{:S(2)}) collective-permute-start(bf16[512,128]{1,0:T(8,128)(2,1)S(1)} %get-tuple-element.17), channel_id=1, source_target_pairs={{0,8},{1,9},{8,0},{9,1},{16,24},{17,25},{24,16},{25,17},{32,40},{3... | collective-permute-start | bytes 393224 | tf_op jit(solution)/shard_map/ppermute | solution.py:137
  162.7 8.9 %collective-permute-start.6 = (bf16[512,128]{1,0:T(8,128)(2,1)S(1)}, bf16[512,128]{1,0:T(8,128)(2,1)S(1)}, u32[]{:S(2)}, u32[]{:S(2)}) collective-permute-start(bf16[512,128]{1,0:T(8,128)(2,1)S(1)} %get-tuple-element.16), channel_id=1, source_target_pairs={{0,9},{1,8},{8,1},{9,0},{16,25},{17,24},{24,17},{25,16},{32,41},{3... | collective-permute-start | bytes 393224 | tf_op jit(solution)/shard_map/ppermute | solution.py:137
  164.7 7.8 %collective-permute-start.14 = (bf16[128,256]{1,0:T(8,128)(2,1)S(1)}, bf16[128,256]{1,0:T(8,128)(2,1)S(1)}, u32[]{:S(2)}, u32[]{:S(2)}) collective-permute-start(bf16[128,256]{1,0:T(8,128)(2,1)S(1)} %fusion.4), channel_id=1, source_target_pairs={{0,1},{1,16},{8,9},{9,24},{16,17},{17,32},{24,25},{25,40},{32,33},... | collective-permute-start | bytes 196616 | tf_op jit(solution)/shard_map/ppermute | solution.py:137
  167.0 7.2 %collective-permute-start.15 = (bf16[128,256]{1,0:T(8,128)(2,1)S(1)}, bf16[128,256]{1,0:T(8,128)(2,1)S(1)}, u32[]{:S(2)}, u32[]{:S(2)}) collective-permute-start(bf16[128,256]{1,0:T(8,128)(2,1)S(1)} %fusion.4), channel_id=1, source_target_pairs={{1,17},{9,25},{17,33},{25,41},{33,49},{41,57},{49,65},{57,73},{65,... | collective-permute-start | bytes 196616 | tf_op jit(solution)/shard_map/ppermute | solution.py:137

commit v3 on v2

v3 whole, which is shorter than its diff:
```python
import functools
import math

import jax
import jax.numpy as jnp
from jax import lax
from jax.experimental import pallas as pl
from jax.experimental.pallas import tpu as pltpu
from jax.sharding import PartitionSpec as P


LOG2E = math.log2(math.e)
NEAR = 4
CALLS = (1, 2, 1)
STAT_ROWS = 16


def split_stats(stats):
    high = lax.reduce_precision(stats, 8, 7)
    middle = lax.reduce_precision(stats - high, 8, 7)
    low = stats - high - middle
    pad = ((0, STAT_ROWS - stats.shape[0]), (0, 0))
    return [jnp.pad(a, pad).astype(jnp.bfloat16) for a in (high, middle, low)]


def kernel(first, count, heads, toks, order, where, mine, theirs, *refs):
    fresh = first == 0
    dq, dkv = refs if fresh else refs[1:]
    rows = heads * toks
    payload = 2 * rows + 3 * STAT_ROWS
    span_rows = toks // 2
    width = mine.shape[1]
    keys = NEAR * payload
    ring = (mine.shape[0] - keys) // toks
    scale = 1.0 / math.sqrt(width)
    place, core = where[0], where[1]
    step, member = place // NEAR, place % NEAR
    token = lax.broadcasted_iota(jnp.int32, (toks, toks), 1)
    row = lax.broadcasted_iota(jnp.int32, (toks, toks), 0)
    key_row, token_row = row % span_rows, token % span_rows
    nt = (((1,), (1,)), ((), ()))
    tn = (((0,), (0,)), ((), ()))
    if fresh:
        dq[...] = jnp.zeros_like(dq)
    else:
        dq[...] = refs[0][...]

    def one_block(index, carry):
        turn = first + index
        ahead = jnp.where(core == 0, turn - (ring // 2 - 1), ring // 2 - turn)
        block = lax.rem(step + ahead + ring, ring)
        chip = block * NEAR + member
        start = pl.multiple_of(keys + block * toks, STAT_ROWS)
        a, b = mine[pl.ds(start, toks)], theirs[pl.ds(start, toks)]
        low, high = jnp.where(core == 0, a, b), jnp.where(core == 0, b, a)
        k = jnp.concatenate([low[:span_rows], high[:span_rows]])
        v = jnp.concatenate([low[span_rows:], high[span_rows:]])
        key_span = jnp.where(row < span_rows, order[2 * chip], order[2 * chip + 1])
        key_pos = key_span * span_rows + key_row
        dk = jnp.zeros((toks, width), jnp.float32)
        dv = jnp.zeros((toks, width), jnp.float32)
        for near in range(NEAR):
            near_chip = step * NEAR + (member ^ near)
            span = jnp.where(token < span_rows, order[2 * near_chip], order[2 * near_chip + 1])
            visible = key_pos <= span * span_rows + token_row
            base = near * payload
            for part, source in ((near, mine), (NEAR + near, theirs)):
                q = source[base : base + rows]
                d = source[base + rows : base + 2 * rows]
                stat = [
                    source[base + 2 * rows + i * STAT_ROWS : base + 2 * rows + (i + 1) * STAT_ROWS]
                    for i in range(3)
                ]
                stat = sum(x.astype(jnp.float32) for x in stat)
                s = lax.dot_general(k, q, nt, preferred_element_type=jnp.float32)
                g = lax.dot_general(v, d, nt, preferred_element_type=jnp.float32)
                probs, grads = [], []
                for h in range(heads):
                    cols = slice(h * toks, (h + 1) * toks)
                    p = jnp.exp2(s[:, cols] * (scale * LOG2E) - stat[h : h + 1])
                    p = jnp.where(visible, p, 0.0)
                    probs.append(p.astype(jnp.bfloat16))
                    ds = p * (g[:, cols] - stat[heads + h : heads + h + 1]) * scale
                    grads.append(ds.astype(jnp.bfloat16))
                p = jnp.concatenate(probs, axis=1)
                ds = jnp.concatenate(grads, axis=1)
                dv = dv + jnp.dot(p, d, preferred_element_type=jnp.float32)
                dk = dk + jnp.dot(ds, q, preferred_element_type=jnp.float32)
                dq[part] += lax.dot_general(ds, k, tn, preferred_element_type=jnp.float32)
        dkv[index, :, :width] = dk
        dkv[index, :, width:] = dv
        return carry

    lax.fori_loop(0, count, one_block, 0)


def attention_grads(first, count, heads, toks, order, where, mine, theirs, dq):
    width = mine.shape[1]
    rows = heads * toks
    smem = pl.BlockSpec(memory_space=pltpu.SMEM)
    vmem = pl.BlockSpec(memory_space=pltpu.VMEM)
    operands = [order, where, mine, theirs] + ([] if dq is None else [dq])
    return pl.pallas_call(
        functools.partial(kernel, first, count, heads, toks),
        out_shape=(
            jax.ShapeDtypeStruct((2 * NEAR, rows, width), jnp.float32),
            jax.ShapeDtypeStruct((count, toks, 2 * width), jnp.float32),
        ),
        in_specs=[smem, smem] + [vmem] * (len(operands) - 2),
        out_specs=(vmem, vmem),
        input_output_aliases={} if dq is None else {len(operands) - 1: 0},
        compiler_params=pltpu.CompilerParams(vmem_limit_bytes=16 * 1024 * 1024),
        cost_estimate=pl.CostEstimate(
            flops=2 * 5 * 2 * NEAR * rows * count * toks * width,
            bytes_accessed=8 * rows * width * 4,
            transcendentals=2 * NEAR * rows * count * toks,
        ),
    )(*operands)


def body(queries, keys, values, out, log_total, d_out, span_order):
    size = lax.axis_size("inner")
    place = lax.axis_index("inner")
    core = lax.axis_index("head")
    toks, heads, width = queries.shape[1:]
    half = toks // 2
    rows = heads * toks

    def move(array, target):
        pairs = []
        for z in range(size):
            for c in range(2):
                to = target(z, c)
                if to is not None:
                    pairs.append((2 * z + c, 2 * (to[0] % size) + to[1]))
        return lax.ppermute(array, ("inner", "head"), pairs)

    def swap(z, c):
        return z, 1 - c

    def near(distance):
        return lambda z, c: (z ^ distance, c)

    delta = jnp.transpose(
        jnp.sum(out[0].astype(jnp.float32) * d_out[0].astype(jnp.float32), axis=-1)
    )
    payload = jnp.concatenate(
        [
            jnp.transpose(queries[0], (1, 0, 2)).reshape(rows, width),
            jnp.transpose(d_out[0], (1, 0, 2)).reshape(rows, width),
            *split_stats(jnp.concatenate([log_total[0] * LOG2E, delta])),
        ]
    )
    payloads = [payload] + [move(payload, near(i)) for i in range(1, NEAR)]

    kv = jnp.concatenate(
        [lax.dynamic_slice_in_dim(a[0], core * half, half, 0) for a in (keys, values)]
    )
    groups = [list(range(first, size, NEAR)) for first in range(NEAR)]
    kv = lax.all_gather(kv, "inner", axis_index_groups=groups, tiled=True)
    mine = jnp.concatenate([*payloads, kv])
    theirs = move(mine, swap)

    order = span_order[0]
    where = jnp.stack([place, core]).astype(jnp.int32)
    dq, parts, first = None, [], 0
    for count in CALLS:
        dq, part = attention_grads(first, count, heads, toks, order, where, mine, theirs, dq)
        parts += [part[i] for i in range(count)]
        first += count

    total = parts[0].astype(jnp.bfloat16)
    for part in parts[1:]:
        total = move(total, lambda z, c: (z - NEAR, 0) if c == 0 else (z + NEAR, 1))
        total = (total.astype(jnp.float32) + part).astype(jnp.bfloat16)
    one = move(total, lambda z, c: (z, 1) if c == 0 else (z + NEAR, 0))
    two = move(total, lambda z, c: None if c == 0 else (z + NEAR, 1))
    two = jnp.where(core == 0, total, two)
    dkv = (one.astype(jnp.float32) + two.astype(jnp.float32)).astype(jnp.bfloat16)

    dq_theirs = move(dq[NEAR:].astype(jnp.bfloat16), swap)
    dq_mine = dq[:NEAR] + dq_theirs.astype(jnp.float32)
    dq_back = [dq_mine[i].astype(jnp.bfloat16) for i in range(1, NEAR)]
    query_grad = dq_mine[0]
    for i in range(1, NEAR):
        back = move(dq_back[i - 1], near(i))
        query_grad = query_grad + back.astype(jnp.float32)
    query_grad = query_grad.astype(jnp.bfloat16).reshape(heads, toks, width)
    query_grad = jnp.transpose(query_grad, (1, 0, 2))
    return query_grad[None], dkv[None, :, :width], dkv[None, :, width:]


def solution(mesh):
    in_specs = (
        P(("groups", "outer"), "inner", "head", None),
        P(("groups", "outer"), "inner", None),
        P(("groups", "outer"), "inner", None),
        P(("groups", "outer"), "inner", "head", None),
        P(("groups", "outer"), "head", "inner"),
        P(("groups", "outer"), "inner", "head", None),
        P(("groups", "outer"), None),
    )
    out_specs = (
        P(("groups", "outer"), "inner", "head", None),
        P(("groups", "outer"), "inner", None),
        P(("groups", "outer"), "inner", None),
    )
    return jax.shard_map(body, mesh=mesh, in_specs=in_specs, out_specs=out_specs, check_vma=False)
```

time: 176 us -> 184 us (1.045)
  starting transfers between devices: 62.2 us -> 68.6 us
  waiting for transfers between devices: 24.3 us -> 20.4 us
  blocking collectives: 70.5 us -> 73.6 us
  local copies, waits for them, and re-layouts: 3.16 us -> 6.11 us
    ppermute x16 -> x13, starting transfers between devices: 62.2 us -> 68.6 us  [move(): return lax.ppermute(array, ('inner', 'head'), pairs)]
    ppermute x16 -> x13, waiting for transfers between devices: 24.3 us -> 20.4 us  [move(): return lax.ppermute(array, ('inner', 'head'), pairs)]
    all_gather x1, blocking collectives: 70.5 us -> 73.6 us  [body(): kv = lax.all_gather(kv, 'inner', axis_index_groups=groups, tiled=True)]
  transfers between devices with their start and end apart: 16 -> 13, of which waited for: 8 -> 5; matrix products, arithmetic and copies ran while one was open for 1% -> 0% of each run, Pallas kernels for 6% -> 5%
where the time goes in v3:
time: 184 us; the launch traced here: 183 us
  blocking collectives  73.6 us (40%)
  starting transfers between devices  68.6 us (37%)
  waiting for transfers between devices  20.4 us (11%)
  Pallas kernels  11.5 us (6%)
  local copies, waits for them, and re-layouts  6.11 us (3%)
  other arithmetic  2.28 us (1%)
    all_gather x1, blocking collectives, body(): kv = lax.all_gather(kv, 'inner', axis_index_groups=groups, tiled=True)  73.6 us
    ppermute x13, starting transfers between devices, move(): return lax.ppermute(array, ('inner', 'head'), pairs)  68.6 us
    ppermute x13, waiting for transfers between devices, move(): return lax.ppermute(array, ('inner', 'head'), pairs)  20.4 us
    pallas_call x3, Pallas kernels, attention_grads(): pl.pallas_call(functools.partial(kernel, first, count, heads, toks), out_...  11.5 us
  transfers between devices with their start and end apart: 13, of which 5 were waited for; matrix products, arithmetic and copies ran while one was open for 0% of the time, Pallas kernels for 5%

profile of v3, /device:TPU:33, one launch (start us, length us, event | category | flops | bytes accessed | tf_op | source)
XLA Modules:
  0.0 183.5 jit_solution(11736235984320949253)
XLA Ops:
  0.6 0.0 copy-start.4
  0.6 0.0 copy-start.3
  0.7 0.9 copy.15
  1.6 0.9 copy.16
  2.5 1.2 fusion.4
  3.7 0.1 copy.17
  3.8 0.7 multiply_bitcast_fusion
  4.6 0.0 copy-start.2
  4.6 5.3 %collective-permute-start = (bf16[1072,128]{1,0:T(8,128)(2,1)S(1)}, bf16[1072,128]{1,0:T(8,128)(2,1)S(1)}, u32[]{:S(2)}, u32[]{:S(2)}) collective-permute-start(bf16[1072,128]{1,0:T(8,128)(2,1)S(1)} %get-tuple-element.29), channel_id=1, source_target_pairs={{0,8},{1,9},{8,0},{9,1},{16,24},{17,25},{24,16},{25,17},{32,40},{3... | collective-permute-start | bytes 823304 | tf_op jit(solution)/shard_map/ppermute | solution.py:136
  9.9 6.6 %collective-permute-start.1 = (bf16[1072,128]{1,0:T(8,128)(2,1)S(1)}, bf16[1072,128]{1,0:T(8,128)(2,1)S(1)}, u32[]{:S(2)}, u32[]{:S(2)}) collective-permute-start(bf16[1072,128]{1,0:T(8,128)(2,1)S(1)} %get-tuple-element.29), channel_id=1, source_target_pairs={{0,16},{1,17},{8,24},{9,25},{16,0},{17,1},{24,8},{25,9},{32,48},{3... | collective-permute-start | bytes 823304 | tf_op jit(solution)/shard_map/ppermute | solution.py:136
  16.5 2.0 %collective-permute-start.2 = (bf16[1072,128]{1,0:T(8,128)(2,1)S(1)}, bf16[1072,128]{1,0:T(8,128)(2,1)S(1)}, u32[]{:S(2)}, u32[]{:S(2)}) collective-permute-start(bf16[1072,128]{1,0:T(8,128)(2,1)S(1)} %get-tuple-element.29), channel_id=1, source_target_pairs={{0,24},{1,25},{8,16},{9,17},{16,8},{17,9},{24,0},{25,1},{32,56},{3... | collective-permute-start | bytes 823304 | tf_op jit(solution)/shard_map/ppermute | solution.py:136
  18.5 0.0 copy-done.4
  18.5 0.0 copy-done.3
  18.5 73.6 %all_gather.3 = bf16[1024,128]{1,0:T(8,128)(2,1)S(1)} all-gather(bf16[128,128]{1,0:T(8,128)(2,1)S(1)} %pad_maximum_fusion), channel_id=1, replica_groups={{0,32,64,96,128,160,192,224},{8,40,72,104,136,168,200,232},{16,48,80,11..., dimensions={0}, use_global_device_ids=true | all-gather | bytes 294912 | tf_op jit(solution)/shard_map/all_gather | solution.py:160
  92.2 0.0 collective-permute-done
  92.2 0.0 collective-permute-done.1
  92.3 0.0 collective-permute-done.2
  92.4 9.4 %collective-permute-start.3 = (bf16[5312,128]{1,0:T(8,128)(2,1)S(1)}, bf16[5312,128]{1,0:T(8,128)(2,1)S(1)}, u32[]{:S(2)}, u32[]{:S(2)}) collective-permute-start(bf16[5312,128]{1,0:T(8,128)(2,1)S(1)} %constant_dynamic-update-slice_fusion.5.mine), channel_id=1, source_target_pairs={{0,1},{1,0},{8,9},{9,8},{16,17},{17,16},{24,25},{25,24},{32,33},{3... | collective-permute-start | bytes 4079624 | tf_op jit(solution)/shard_map/ppermute | solution.py:136
  101.7 0.1 pad_add_fusion.where
  101.8 2.6 %collective-permute-done.3.theirs = bf16[5312,128]{1,0:T(8,128)(2,1)S(1)} collective-permute-done((bf16[5312,128]{1,0:T(8,128)(2,1)S(1)}, bf16[5312,128]{1,0:T(8,128)(2,1)S(1)}, u32[]{:S(2)}, u32[]{:S(2)}) %collective-permute-start.3) | collective-permute-done | bytes 1359904 | tf_op jit(solution)/shard_map/ppermute | solution.py:136
  104.5 1.1 copy-done
  105.6 1.3 copy-done.1
  106.9 2.9 %shard_map.94 = (f32[8,512,128]{2,1,0:T(8,128)S(1)}, f32[1,128,256]{2,1,0:T(8,128)S(1)}) custom-call(s32[64]{0:T(128)S(1)} %bitcast.62, s32[2]{0:T(128)S(1)} %pad_add_fusion.where, bf16[5312,128]{1,0:T(8,128)(2,1)S(1)} %constant_dynamic-update-slice_fusion.5.mine, bf16[5312,128]{1,0:T(8,128)(2,1)S(1)} %copy-done.1), custom_call_target="tpu_custom_call" | custom-call | flops 671088640 | bytes 2097152 | tf_op jit(solution)/shard_map/pallas_call | solution.py:103
  109.8 2.0 %collective-permute-start.8 = (bf16[128,256]{1,0:T(8,128)(2,1)S(1)}, bf16[128,256]{1,0:T(8,128)(2,1)S(1)}, u32[]{:S(2)}, u32[]{:S(2)}) collective-permute-start(bf16[128,256]{1,0:T(8,128)(2,1)S(1)} %convert_bitcast_fusion), channel_id=1, source_target_pairs={{0,224},{1,33},{8,232},{9,41},{16,240},{17,49},{24,248},{25,57},{3... | collective-permute-start | bytes 196616 | tf_op jit(solution)/shard_map/ppermute | solution.py:136
  111.8 5.6 %shard_map.95 = (f32[8,512,128]{2,1,0:T(8,128)S(1)}, f32[2,128,256]{2,1,0:T(8,128)S(1)}) custom-call(s32[64]{0:T(128)S(1)} %bitcast.63, s32[2]{0:T(128)S(1)} %pad_add_fusion.where, bf16[5312,128]{1,0:T(8,128)(2,1)S(1)} %constant_dynamic-update-slice_fusion.5.mine, bf16[5312,128]{1,0:T(8,128)(2,1)S(1)} %copy-done.1, ...), custom_call_target="tpu_custom_call", output_to_operand_aliasing={{0}: (4, {})} | custom-call | flops 1342177280 | bytes 2097152 | tf_op jit(solution)/shard_map/pallas_call | solution.py:103
  117.4 2.1 %collective-permute-done.8 = bf16[128,256]{1,0:T(8,128)(2,1)S(1)} collective-permute-done((bf16[128,256]{1,0:T(8,128)(2,1)S(1)}, bf16[128,256]{1,0:T(8,128)(2,1)S(1)}, u32[]{:S(2)}, u32[]{:S(2)}) %collective-permute-start.8) | collective-permute-done | bytes 65568 | tf_op jit(solution)/shard_map/ppermute | solution.py:136
  119.5 4.7 %collective-permute-start.9 = (bf16[128,256]{1,0:T(8,128)(2,1)S(1)}, bf16[128,256]{1,0:T(8,128)(2,1)S(1)}, u32[]{:S(2)}, u32[]{:S(2)}) collective-permute-start(bf16[128,256]{1,0:T(8,128)(2,1)S(1)} %fusion.7), channel_id=1, source_target_pairs={{0,224},{1,33},{8,232},{9,41},{16,240},{17,49},{24,248},{25,57},{3... | collective-permute-start | bytes 196616 | tf_op jit(solution)/shard_map/ppermute | solution.py:136
  124.2 5.8 %collective-permute-done.9 = bf16[128,256]{1,0:T(8,128)(2,1)S(1)} collective-permute-done((bf16[128,256]{1,0:T(8,128)(2,1)S(1)}, bf16[128,256]{1,0:T(8,128)(2,1)S(1)}, u32[]{:S(2)}, u32[]{:S(2)}) %collective-permute-start.9) | collective-permute-done | bytes 65568 | tf_op jit(solution)/shard_map/ppermute | solution.py:136
  130.1 3.2 %collective-permute-start.10 = (bf16[128,256]{1,0:T(8,128)(2,1)S(1)}, bf16[128,256]{1,0:T(8,128)(2,1)S(1)}, u32[]{:S(2)}, u32[]{:S(2)}) collective-permute-start(bf16[128,256]{1,0:T(8,128)(2,1)S(1)} %fusion.6), channel_id=1, source_target_pairs={{0,224},{1,33},{8,232},{9,41},{16,240},{17,49},{24,248},{25,57},{3... | collective-permute-start | bytes 196616 | tf_op jit(solution)/shard_map/ppermute | solution.py:136
  133.2 3.0 %shard_map.96 = (f32[8,512,128]{2,1,0:T(8,128)S(1)}, f32[1,128,256]{2,1,0:T(8,128)S(1)}) custom-call(s32[64]{0:T(128)S(1)} %bitcast.64, s32[2]{0:T(128)S(1)} %pad_add_fusion.where, bf16[5312,128]{1,0:T(8,128)(2,1)S(1)} %constant_dynamic-update-slice_fusion.5.mine, bf16[5312,128]{1,0:T(8,128)(2,1)S(1)} %copy-done.1, ...), custom_call_target="tpu_custom_call", output_to_operand_aliasing={{0}: (4, {})} | custom-call | flops 671088640 | bytes 2097152 | tf_op jit(solution)/shard_map/pallas_call | solution.py:103
  136.2 0.1 slice.69
  136.3 4.7 %collective-permute-start.4 = (bf16[4,512,128]{2,1,0:T(8,128)(2,1)S(1)}, bf16[4,512,128]{2,1,0:T(8,128)(2,1)S(1)}, u32[]{:S(2)}, u32[]{:S(2)}) collective-permute-start(bf16[4,512,128]{2,1,0:T(8,128)(2,1)S(1)} %slice.69), channel_id=1, source_target_pairs={{0,1},{1,0},{8,9},{9,8},{16,17},{17,16},{24,25},{25,24},{32,33},{3... | collective-permute-start | bytes 1572872 | tf_op jit(solution)/shard_map/ppermute | solution.py:136
  141.0 0.0 collective-permute-done.10
  141.0 4.7 %collective-permute-start.11 = (bf16[128,256]{1,0:T(8,128)(2,1)S(1)}, bf16[128,256]{1,0:T(8,128)(2,1)S(1)}, u32[]{:S(2)}, u32[]{:S(2)}) collective-permute-start(bf16[128,256]{1,0:T(8,128)(2,1)S(1)} %fusion.5), channel_id=1, source_target_pairs={{0,1},{1,32},{8,9},{9,40},{16,17},{17,48},{24,25},{25,56},{32,33},... | collective-permute-start | bytes 196616 | tf_op jit(solution)/shard_map/ppermute | solution.py:136
  145.7 4.5 %collective-permute-start.12 = (bf16[128,256]{1,0:T(8,128)(2,1)S(1)}, bf16[128,256]{1,0:T(8,128)(2,1)S(1)}, u32[]{:S(2)}, u32[]{:S(2)}) collective-permute-start(bf16[128,256]{1,0:T(8,128)(2,1)S(1)} %fusion.5), channel_id=1, source_target_pairs={{1,33},{9,41},{17,49},{25,57},{33,65},{41,73},{49,81},{57,89},{65,... | collective-permute-start | bytes 196616 | tf_op jit(solution)/shard_map/ppermute | solution.py:136
  150.2 0.0 collective-permute-done.11
  150.2 4.6 %collective-permute-done.12 = bf16[128,256]{1,0:T(8,128)(2,1)S(1)} collective-permute-done((bf16[128,256]{1,0:T(8,128)(2,1)S(1)}, bf16[128,256]{1,0:T(8,128)(2,1)S(1)}, u32[]{:S(2)}, u32[]{:S(2)}) %collective-permute-start.12) | collective-permute-done | bytes 65568 | tf_op jit(solution)/shard_map/ppermute | solution.py:136
  154.8 0.0 collective-permute-done.4
  154.8 0.1 fusion.9
  155.0 15.7 %collective-permute-start.5 = (bf16[512,128]{1,0:T(8,128)(2,1)S(1)}, bf16[512,128]{1,0:T(8,128)(2,1)S(1)}, u32[]{:S(2)}, u32[]{:S(2)}) collective-permute-start(bf16[512,128]{1,0:T(8,128)(2,1)S(1)} %get-tuple-element.17), channel_id=1, source_target_pairs={{0,8},{1,9},{8,0},{9,1},{16,24},{17,25},{24,16},{25,17},{32,40},{3... | collective-permute-start | bytes 393224 | tf_op jit(solution)/shard_map/ppermute | solution.py:136
  170.7 2.2 %collective-permute-start.6 = (bf16[512,128]{1,0:T(8,128)(2,1)S(1)}, bf16[512,128]{1,0:T(8,128)(2,1)S(1)}, u32[]{:S(2)}, u32[]{:S(2)}) collective-permute-start(bf16[512,128]{1,0:T(8,128)(2,1)S(1)} %get-tuple-element.19), channel_id=1, source_target_pairs={{0,16},{1,17},{8,24},{9,25},{16,0},{17,1},{24,8},{25,9},{32,48},{3... | collective-permute-start | bytes 393224 | tf_op jit(solution)/shard_map/ppermute | solution.py:136
  172.9 3.8 %collective-permute-start.7 = (bf16[512,128]{1,0:T(8,128)(2,1)S(1)}, bf16[512,128]{1,0:T(8,128)(2,1)S(1)}, u32[]{:S(2)}, u32[]{:S(2)}) collective-permute-start(bf16[512,128]{1,0:T(8,128)(2,1)S(1)} %get-tuple-element.18), channel_id=1, source_target_pairs={{0,24},{1,25},{8,16},{9,17},{16,8},{17,9},{24,0},{25,1},{32,56},{3... | collective-permute-start | bytes 393224 | tf_op jit(solution)/shard_map/ppermute | solution.py:136
  176.7 0.6 slice_bitcast_fusion.4
  177.4 0.0 collective-permute-done.5
  177.4 5.3 %collective-permute-done.6 = bf16[512,128]{1,0:T(8,128)(2,1)S(1)} collective-permute-done((bf16[512,128]{1,0:T(8,128)(2,1)S(1)}, bf16[512,128]{1,0:T(8,128)(2,1)S(1)}, u32[]{:S(2)}, u32[]{:S(2)}) %collective-permute-start.6) | collective-permute-done | bytes 131104 | tf_op jit(solution)/shard_map/ppermute | solution.py:136
  182.6 0.0 collective-permute-done.7
  182.6 0.1 fusion.3
  182.7 0.8 copy.20
  (21 shorter events, 0.4 us)
Async XLA Ops:
  0.6 17.9 %copy-start.4 = (bf16[1,128,128]{2,1,0:T(8,128)(2,1)S(1)}, bf16[1,128,128]{2,1,0:T(8,128)(2,1)}, u32[]{:S(2)}) copy-start(bf16[1,128,128]{2,1,0:T(8,128)(2,1)} %param.8) | copy-start | bytes 98308
  0.6 17.9 %copy-start.3 = (bf16[1,128,128]{2,1,0:T(8,128)(2,1)S(1)}, bf16[1,128,128]{2,1,0:T(8,128)(2,1)}, u32[]{:S(2)}) copy-start(bf16[1,128,128]{2,1,0:T(8,128)(2,1)} %param.9) | copy-start | bytes 98308
  4.6 101.0 %copy-start.2 = (s32[1,64]{1,0:T(1,128)S(1)}, s32[1,64]{1,0:T(1,128)}, u32[]{:S(2)}) copy-start(s32[1,64]{1,0:T(1,128)} %param.13) | copy-start | bytes 772
  4.6 87.6 %collective-permute-start = (bf16[1072,128]{1,0:T(8,128)(2,1)S(1)}, bf16[1072,128]{1,0:T(8,128)(2,1)S(1)}, u32[]{:S(2)}, u32[]{:S(2)}) collective-permute-start(bf16[1072,128]{1,0:T(8,128)(2,1)S(1)} %get-tuple-element.29), channel_id=1, source_target_pairs={{0,8},{1,9},{8,0},{9,1},{16,24},{17,25},{24,16},{25,17},{32,40},{3... | collective-permute-start | bytes 823304 | tf_op jit(solution)/shard_map/ppermute | solution.py:136
  9.9 82.4 %collective-permute-start.1 = (bf16[1072,128]{1,0:T(8,128)(2,1)S(1)}, bf16[1072,128]{1,0:T(8,128)(2,1)S(1)}, u32[]{:S(2)}, u32[]{:S(2)}) collective-permute-start(bf16[1072,128]{1,0:T(8,128)(2,1)S(1)} %get-tuple-element.29), channel_id=1, source_target_pairs={{0,16},{1,17},{8,24},{9,25},{16,0},{17,1},{24,8},{25,9},{32,48},{3... | collective-permute-start | bytes 823304 | tf_op jit(solution)/shard_map/ppermute | solution.py:136
  16.5 75.8 %collective-permute-start.2 = (bf16[1072,128]{1,0:T(8,128)(2,1)S(1)}, bf16[1072,128]{1,0:T(8,128)(2,1)S(1)}, u32[]{:S(2)}, u32[]{:S(2)}) collective-permute-start(bf16[1072,128]{1,0:T(8,128)(2,1)S(1)} %get-tuple-element.29), channel_id=1, source_target_pairs={{0,24},{1,25},{8,16},{9,17},{16,8},{17,9},{24,0},{25,1},{32,56},{3... | collective-permute-start | bytes 823304 | tf_op jit(solution)/shard_map/ppermute | solution.py:136
  92.4 12.1 %collective-permute-start.3 = (bf16[5312,128]{1,0:T(8,128)(2,1)S(1)}, bf16[5312,128]{1,0:T(8,128)(2,1)S(1)}, u32[]{:S(2)}, u32[]{:S(2)}) collective-permute-start(bf16[5312,128]{1,0:T(8,128)(2,1)S(1)} %constant_dynamic-update-slice_fusion.5.mine), channel_id=1, source_target_pairs={{0,1},{1,0},{8,9},{9,8},{16,17},{17,16},{24,25},{25,24},{32,33},{3... | collective-permute-start | bytes 4079624 | tf_op jit(solution)/shard_map/ppermute | solution.py:136
  104.5 1.1 copy-start
  105.6 1.3 copy-start.1
  109.8 9.6 %collective-permute-start.8 = (bf16[128,256]{1,0:T(8,128)(2,1)S(1)}, bf16[128,256]{1,0:T(8,128)(2,1)S(1)}, u32[]{:S(2)}, u32[]{:S(2)}) collective-permute-start(bf16[128,256]{1,0:T(8,128)(2,1)S(1)} %convert_bitcast_fusion), channel_id=1, source_target_pairs={{0,224},{1,33},{8,232},{9,41},{16,240},{17,49},{24,248},{25,57},{3... | collective-permute-start | bytes 196616 | tf_op jit(solution)/shard_map/ppermute | solution.py:136
  119.5 10.5 %collective-permute-start.9 = (bf16[128,256]{1,0:T(8,128)(2,1)S(1)}, bf16[128,256]{1,0:T(8,128)(2,1)S(1)}, u32[]{:S(2)}, u32[]{:S(2)}) collective-permute-start(bf16[128,256]{1,0:T(8,128)(2,1)S(1)} %fusion.7), channel_id=1, source_target_pairs={{0,224},{1,33},{8,232},{9,41},{16,240},{17,49},{24,248},{25,57},{3... | collective-permute-start | bytes 196616 | tf_op jit(solution)/shard_map/ppermute | solution.py:136
  130.1 11.0 %collective-permute-start.10 = (bf16[128,256]{1,0:T(8,128)(2,1)S(1)}, bf16[128,256]{1,0:T(8,128)(2,1)S(1)}, u32[]{:S(2)}, u32[]{:S(2)}) collective-permute-start(bf16[128,256]{1,0:T(8,128)(2,1)S(1)} %fusion.6), channel_id=1, source_target_pairs={{0,224},{1,33},{8,232},{9,41},{16,240},{17,49},{24,248},{25,57},{3... | collective-permute-start | bytes 196616 | tf_op jit(solution)/shard_map/ppermute | solution.py:136
  136.3 18.5 %collective-permute-start.4 = (bf16[4,512,128]{2,1,0:T(8,128)(2,1)S(1)}, bf16[4,512,128]{2,1,0:T(8,128)(2,1)S(1)}, u32[]{:S(2)}, u32[]{:S(2)}) collective-permute-start(bf16[4,512,128]{2,1,0:T(8,128)(2,1)S(1)} %slice.69), channel_id=1, source_target_pairs={{0,1},{1,0},{8,9},{9,8},{16,17},{17,16},{24,25},{25,24},{32,33},{3... | collective-permute-start | bytes 1572872 | tf_op jit(solution)/shard_map/ppermute | solution.py:136
  141.0 9.2 %collective-permute-start.11 = (bf16[128,256]{1,0:T(8,128)(2,1)S(1)}, bf16[128,256]{1,0:T(8,128)(2,1)S(1)}, u32[]{:S(2)}, u32[]{:S(2)}) collective-permute-start(bf16[128,256]{1,0:T(8,128)(2,1)S(1)} %fusion.5), channel_id=1, source_target_pairs={{0,1},{1,32},{8,9},{9,40},{16,17},{17,48},{24,25},{25,56},{32,33},... | collective-permute-start | bytes 196616 | tf_op jit(solution)/shard_map/ppermute | solution.py:136
  145.7 9.0 %collective-permute-start.12 = (bf16[128,256]{1,0:T(8,128)(2,1)S(1)}, bf16[128,256]{1,0:T(8,128)(2,1)S(1)}, u32[]{:S(2)}, u32[]{:S(2)}) collective-permute-start(bf16[128,256]{1,0:T(8,128)(2,1)S(1)} %fusion.5), channel_id=1, source_target_pairs={{1,33},{9,41},{17,49},{25,57},{33,65},{41,73},{49,81},{57,89},{65,... | collective-permute-start | bytes 196616 | tf_op jit(solution)/shard_map/ppermute | solution.py:136
  155.0 22.4 %collective-permute-start.5 = (bf16[512,128]{1,0:T(8,128)(2,1)S(1)}, bf16[512,128]{1,0:T(8,128)(2,1)S(1)}, u32[]{:S(2)}, u32[]{:S(2)}) collective-permute-start(bf16[512,128]{1,0:T(8,128)(2,1)S(1)} %get-tuple-element.17), channel_id=1, source_target_pairs={{0,8},{1,9},{8,0},{9,1},{16,24},{17,25},{24,16},{25,17},{32,40},{3... | collective-permute-start | bytes 393224 | tf_op jit(solution)/shard_map/ppermute | solution.py:136
  170.7 11.9 %collective-permute-start.6 = (bf16[512,128]{1,0:T(8,128)(2,1)S(1)}, bf16[512,128]{1,0:T(8,128)(2,1)S(1)}, u32[]{:S(2)}, u32[]{:S(2)}) collective-permute-start(bf16[512,128]{1,0:T(8,128)(2,1)S(1)} %get-tuple-element.19), channel_id=1, source_target_pairs={{0,16},{1,17},{8,24},{9,25},{16,0},{17,1},{24,8},{25,9},{32,48},{3... | collective-permute-start | bytes 393224 | tf_op jit(solution)/shard_map/ppermute | solution.py:136
  172.9 9.7 %collective-permute-start.7 = (bf16[512,128]{1,0:T(8,128)(2,1)S(1)}, bf16[512,128]{1,0:T(8,128)(2,1)S(1)}, u32[]{:S(2)}, u32[]{:S(2)}) collective-permute-start(bf16[512,128]{1,0:T(8,128)(2,1)S(1)} %get-tuple-element.18), channel_id=1, source_target_pairs={{0,24},{1,25},{8,16},{9,17},{16,8},{17,9},{24,0},{25,1},{32,56},{3... | collective-permute-start | bytes 393224 | tf_op jit(solution)/shard_map/ppermute | solution.py:136

commit v4 on v3

--- a/solution.py
+++ b/solution.py
@@ -10,8 +10,9 @@
 
 
 LOG2E = math.log2(math.e)
-NEAR = 4
-CALLS = (1, 2, 1)
+NEAR = 2
+BUNDLE = 2
+CALLS = (2, 4, 2)
 STAT_ROWS = 16
 
 
@@ -166,13 +167,19 @@
     dq, parts, first = None, [], 0
     for count in CALLS:
         dq, part = attention_grads(first, count, heads, toks, order, where, mine, theirs, dq)
-        parts += [part[i] for i in range(count)]
+        parts += [part[i : i + BUNDLE] for i in range(0, count, BUNDLE)]
         first += count
+
+    def hop(blocks):
+        return lambda z, c: (z - blocks * NEAR, 0) if c == 0 else (z + blocks * NEAR, 1)
 
     total = parts[0].astype(jnp.bfloat16)
     for part in parts[1:]:
-        total = move(total, lambda z, c: (z - NEAR, 0) if c == 0 else (z + NEAR, 1))
-        total = (total.astype(jnp.float32) + part).astype(jnp.bfloat16)
+        total = move(total, hop(BUNDLE))
+        sums = total.astype(jnp.float32) + part
+        total = sums.astype(jnp.bfloat16)
+    total = move(total[0], hop(1)).astype(jnp.float32) + sums[1]
+    total = total.astype(jnp.bfloat16)
     one = move(total, lambda z, c: (z, 1) if c == 0 else (z + NEAR, 0))
     two = move(total, lambda z, c: None if c == 0 else (z + NEAR, 1))
     two = jnp.where(core == 0, total, two)
@@ -181,10 +188,8 @@
     dq_theirs = move(dq[NEAR:].astype(jnp.bfloat16), swap)
     dq_mine = dq[:NEAR] + dq_theirs.astype(jnp.float32)
     dq_back = [dq_mine[i].astype(jnp.bfloat16) for i in range(1, NEAR)]
-    query_grad = dq_mine[0]
-    for i in range(1, NEAR):
-        back = move(dq_back[i - 1], near(i))
-        query_grad = query_grad + back.astype(jnp.float32)
+    backs = [move(dq_back[i - 1], near(i)) for i in range(1, NEAR)]
+    query_grad = dq_mine[0] + sum(back.astype(jnp.float32) for back in backs)
     query_grad = query_grad.astype(jnp.bfloat16).reshape(heads, toks, width)
     query_grad = jnp.transpose(query_grad, (1, 0, 2))
     return query_grad[None], dkv[None, :, :width], dkv[None, :, width:]

time: 184 us -> 155 us (0.84)
  starting transfers between devices: 68.6 us -> 51 us
  waiting for transfers between devices: 20.4 us -> 13.1 us
  blocking collectives: 73.6 us -> 70.3 us
  local copies, waits for them, and re-layouts: 6.11 us -> 3.61 us
    ppermute x13 -> x10, starting transfers between devices: 68.6 us -> 51 us  [move(): return lax.ppermute(array, ('inner', 'head'), pairs)]
    ppermute x13 -> x10, waiting for transfers between devices: 20.4 us -> 13.1 us  [move(): return lax.ppermute(array, ('inner', 'head'), pairs)]
    all_gather x1, blocking collectives: 73.6 us -> 70.3 us  [body(): kv = lax.all_gather(kv, 'inner', axis_index_groups=groups, tiled=True)]
    unnamed x17 -> x15, local copies, waits for them, and re-layouts: 2.64 us -> 0.14 us
  transfers between devices with their start and end apart: 13 -> 10, of which waited for: 5 -> 4; matrix products, arithmetic and copies ran while one was open for 0% -> 1% of each run, Pallas kernels for 5% -> 6%
where the time goes in v4:
time: 155 us
  blocking collectives  70.3 us (45%)
  starting transfers between devices  51 us (33%)
  waiting for transfers between devices  13.1 us (8%)
  Pallas kernels  12.5 us (8%)
  local copies, waits for them, and re-layouts  3.61 us (2%)
  other arithmetic  3.23 us (2%)
    all_gather x1, blocking collectives, body(): kv = lax.all_gather(kv, 'inner', axis_index_groups=groups, tiled=True)  70.3 us
    ppermute x10, starting transfers between devices, move(): return lax.ppermute(array, ('inner', 'head'), pairs)  51 us
    ppermute x10, waiting for transfers between devices, move(): return lax.ppermute(array, ('inner', 'head'), pairs)  13.1 us
    pallas_call x3, Pallas kernels, attention_grads(): pl.pallas_call(functools.partial(kernel, first, count, heads, toks), out_...  12.5 us
  transfers between devices with their start and end apart: 10, of which 4 were waited for; matrix products, arithmetic and copies ran while one was open for 1% of the time, Pallas kernels for 6%

profile of v4, /device:TPU:33, one launch (start us, length us, event | category | flops | bytes accessed | tf_op | source)
XLA Modules:
  0.0 154.7 jit_solution(13382481089951506888)
XLA Ops:
  0.6 0.0 copy-start.4
  0.6 0.0 copy-start.3
  0.7 0.0 copy-start.2
  0.7 0.9 copy.15
  1.6 0.9 copy.16
  2.6 1.2 fusion.2
  3.8 0.1 copy.17
  3.8 0.0 copy-done.4
  3.9 5.3 %collective-permute-start = (bf16[1072,128]{1,0:T(8,128)(2,1)S(1)}, bf16[1072,128]{1,0:T(8,128)(2,1)S(1)}, u32[]{:S(2)}, u32[]{:S(2)}) collective-permute-start(bf16[1072,128]{1,0:T(8,128)(2,1)S(1)} %get-tuple-element.24), channel_id=1, source_target_pairs={{0,8},{1,9},{8,0},{9,1},{16,24},{17,25},{24,16},{25,17},{32,40},{3... | collective-permute-start | bytes 823304 | tf_op jit(solution)/shard_map/ppermute | solution.py:137
  9.2 0.0 copy-done.3
  9.2 0.0 copy-done.2
  9.3 0.0 copy-start.1
  9.3 70.3 %all_gather.3 = bf16[2048,128]{1,0:T(8,128)(2,1)S(1)} all-gather(bf16[128,128]{1,0:T(8,128)(2,1)S(1)} %pad_maximum_fusion), channel_id=1, replica_groups={{0,16,32,48,64,80,96,112,128,144,160,176,192,208,224,240},{8,24,40,56,7..., dimensions={0}, use_global_device_ids=true | all-gather | bytes 557056 | tf_op jit(solution)/shard_map/all_gather | solution.py:161
  79.5 0.0 collective-permute-done
  79.6 0.1 constant_dynamic-update-slice_fusion.5.mine
  79.7 8.6 %collective-permute-start.1 = (bf16[4192,128]{1,0:T(8,128)(2,1)S(1)}, bf16[4192,128]{1,0:T(8,128)(2,1)S(1)}, u32[]{:S(2)}, u32[]{:S(2)}) collective-permute-start(bf16[4192,128]{1,0:T(8,128)(2,1)S(1)} %constant_dynamic-update-slice_fusion.5.mine), channel_id=1, source_target_pairs={{0,1},{1,0},{8,9},{9,8},{16,17},{17,16},{24,25},{25,24},{32,33},{3... | collective-permute-start | bytes 3219464 | tf_op jit(solution)/shard_map/ppermute | solution.py:137
  88.3 0.1 pad_add_fusion.where
  88.3 2.2 %collective-permute-done.1.theirs = bf16[4192,128]{1,0:T(8,128)(2,1)S(1)} collective-permute-done((bf16[4192,128]{1,0:T(8,128)(2,1)S(1)}, bf16[4192,128]{1,0:T(8,128)(2,1)S(1)}, u32[]{:S(2)}, u32[]{:S(2)}) %collective-permute-start.1) | collective-permute-done | bytes 1073184 | tf_op jit(solution)/shard_map/ppermute | solution.py:137
  90.6 0.0 copy-done.1
  90.6 3.2 %shard_map.94 = (f32[4,512,128]{2,1,0:T(8,128)S(1)}, f32[2,128,256]{2,1,0:T(8,128)S(1)}) custom-call(s32[64]{0:T(128)S(1)} %bitcast.48, s32[2]{0:T(128)S(1)} %pad_add_fusion.where, bf16[4192,128]{1,0:T(8,128)(2,1)S(1)} %constant_dynamic-update-slice_fusion.5.mine, bf16[4192,128]{1,0:T(8,128)(2,1)S(1)} %collective-permute-done.1.theirs), custom_call_target="tpu_custom_call" | custom-call | flops 671088640 | bytes 2097152 | tf_op jit(solution)/shard_map/pallas_call | solution.py:104
  93.8 4.0 %collective-permute-start.4 = (bf16[2,128,256]{2,1,0:T(8,128)(2,1)S(1)}, bf16[2,128,256]{2,1,0:T(8,128)(2,1)S(1)}, u32[]{:S(2)}, u32[]{:S(2)}) collective-permute-start(bf16[2,128,256]{2,1,0:T(8,128)(2,1)S(1)} %convert_element_type.73), channel_id=1, source_target_pairs={{0,224},{1,33},{8,232},{9,41},{16,240},{17,49},{24,248},{25,57},{3... | collective-permute-start | bytes 393224 | tf_op jit(solution)/shard_map/ppermute | solution.py:137
  97.8 5.9 %shard_map.95 = (f32[4,512,128]{2,1,0:T(8,128)S(1)}, f32[4,128,256]{2,1,0:T(8,128)S(1)}) custom-call(s32[64]{0:T(128)S(1)} %bitcast.49, s32[2]{0:T(128)S(1)} %pad_add_fusion.where, bf16[4192,128]{1,0:T(8,128)(2,1)S(1)} %constant_dynamic-update-slice_fusion.5.mine, ...), custom_call_target="tpu_custom_call", output_to_operand_aliasing={{0}: (4, {})} | custom-call | flops 1342177280 | bytes 2097152 | tf_op jit(solution)/shard_map/pallas_call | solution.py:104
  103.7 0.0 copy-start
  103.8 0.1 collective-permute-done.4
  103.8 0.8 add_convert_fusion.1
  104.6 3.9 %collective-permute-start.5 = (bf16[2,128,256]{2,1,0:T(8,128)(2,1)}, bf16[2,128,256]{2,1,0:T(8,128)(2,1)}, u32[]{:S(2)}, u32[]{:S(2)}) collective-permute-start(bf16[2,128,256]{2,1,0:T(8,128)(2,1)} %add_convert_fusion.1), channel_id=1, source_target_pairs={{0,224},{1,33},{8,232},{9,41},{16,240},{17,49},{24,248},{25,57},{3... | collective-permute-start | bytes 393224 | tf_op jit(solution)/shard_map/ppermute | solution.py:137
  108.5 0.0 copy-done
  108.5 3.3 %shard_map.96 = (f32[4,512,128]{2,1,0:T(8,128)S(1)}, f32[2,128,256]{2,1,0:T(8,128)S(1)}) custom-call(s32[64]{0:T(128)S(1)} %bitcast.50, s32[2]{0:T(128)S(1)} %pad_add_fusion.where, bf16[4192,128]{1,0:T(8,128)(2,1)S(1)} %constant_dynamic-update-slice_fusion.5.mine, ...), custom_call_target="tpu_custom_call", output_to_operand_aliasing={{0}: (4, {})} | custom-call | flops 671088640 | bytes 2097152 | tf_op jit(solution)/shard_map/pallas_call | solution.py:104
  111.8 6.0 %collective-permute-start.2 = (bf16[2,512,128]{2,1,0:T(8,128)(2,1)S(1)}, bf16[2,512,128]{2,1,0:T(8,128)(2,1)S(1)}, u32[]{:S(2)}, u32[]{:S(2)}) collective-permute-start(bf16[2,512,128]{2,1,0:T(8,128)(2,1)S(1)} %slice.71), channel_id=1, source_target_pairs={{0,1},{1,0},{8,9},{9,8},{16,17},{17,16},{24,25},{25,24},{32,33},{3... | collective-permute-start | bytes 786440 | tf_op jit(solution)/shard_map/ppermute | solution.py:137
  117.9 0.0 collective-permute-done.5
  117.9 1.0 add_convert_fusion
  118.9 4.6 %collective-permute-start.6 = (bf16[2,128,256]{2,1,0:T(8,128)(2,1)S(1)}, bf16[2,128,256]{2,1,0:T(8,128)(2,1)S(1)}, u32[]{:S(2)}, u32[]{:S(2)}) collective-permute-start(bf16[2,128,256]{2,1,0:T(8,128)(2,1)S(1)} %add_convert_fusion), channel_id=1, source_target_pairs={{0,224},{1,33},{8,232},{9,41},{16,240},{17,49},{24,248},{25,57},{3... | collective-permute-start | bytes 393224 | tf_op jit(solution)/shard_map/ppermute | solution.py:137
  123.6 0.0 collective-permute-done.2
  123.6 6.1 %collective-permute-done.6 = bf16[2,128,256]{2,1,0:T(8,128)(2,1)S(1)} collective-permute-done((bf16[2,128,256]{2,1,0:T(8,128)(2,1)S(1)}, bf16[2,128,256]{2,1,0:T(8,128)(2,1)S(1)}, u32[]{:S(2)}, u32[]{:S(2)}) %collective-permute-start.6) | collective-permute-done | bytes 131104 | tf_op jit(solution)/shard_map/ppermute | solution.py:137
  129.8 5.2 %collective-permute-start.7 = (bf16[128,256]{1,0:T(8,128)(2,1)S(1)}, bf16[128,256]{1,0:T(8,128)(2,1)S(1)}, u32[]{:S(2)}, u32[]{:S(2)}) collective-permute-start(bf16[128,256]{1,0:T(8,128)(2,1)S(1)} %fusion.6), channel_id=1, source_target_pairs={{0,240},{1,17},{8,248},{9,25},{16,0},{17,33},{24,8},{25,41},{32,16... | collective-permute-start | bytes 196616 | tf_op jit(solution)/shard_map/ppermute | solution.py:137
  135.0 4.0 %collective-permute-start.3 = (bf16[512,128]{1,0:T(8,128)(2,1)S(1)}, bf16[512,128]{1,0:T(8,128)(2,1)S(1)}, u32[]{:S(2)}, u32[]{:S(2)}) collective-permute-start(bf16[512,128]{1,0:T(8,128)(2,1)S(1)} %fusion.3), channel_id=1, source_target_pairs={{0,8},{1,9},{8,0},{9,1},{16,24},{17,25},{24,16},{25,17},{32,40},{3... | collective-permute-start | bytes 393224 | tf_op jit(solution)/shard_map/ppermute | solution.py:137
  139.0 0.0 collective-permute-done.7
  139.0 7.5 %collective-permute-start.8 = (bf16[128,256]{1,0:T(8,128)(2,1)S(1)}, bf16[128,256]{1,0:T(8,128)(2,1)S(1)}, u32[]{:S(2)}, u32[]{:S(2)}) collective-permute-start(bf16[128,256]{1,0:T(8,128)(2,1)S(1)} %fusion.5), channel_id=1, source_target_pairs={{0,1},{1,16},{8,9},{9,24},{16,17},{17,32},{24,25},{25,40},{32,33},... | collective-permute-start | bytes 196616 | tf_op jit(solution)/shard_map/ppermute | solution.py:137
  146.5 2.0 %collective-permute-start.9 = (bf16[128,256]{1,0:T(8,128)(2,1)S(1)}, bf16[128,256]{1,0:T(8,128)(2,1)S(1)}, u32[]{:S(2)}, u32[]{:S(2)}) collective-permute-start(bf16[128,256]{1,0:T(8,128)(2,1)S(1)} %fusion.5), channel_id=1, source_target_pairs={{1,17},{9,25},{17,33},{25,41},{33,49},{41,57},{49,65},{57,73},{65,... | collective-permute-start | bytes 196616 | tf_op jit(solution)/shard_map/ppermute | solution.py:137
  148.5 0.0 collective-permute-done.3
  148.5 0.8 copy.20
  149.3 0.0 collective-permute-done.8
  149.3 4.7 %collective-permute-done.9 = bf16[128,256]{1,0:T(8,128)(2,1)S(1)} collective-permute-done((bf16[128,256]{1,0:T(8,128)(2,1)S(1)}, bf16[128,256]{1,0:T(8,128)(2,1)S(1)}, u32[]{:S(2)}, u32[]{:S(2)}) %collective-permute-start.9) | collective-permute-done | bytes 65568 | tf_op jit(solution)/shard_map/ppermute | solution.py:137
  154.1 0.6 slice_bitcast_fusion.2
  (19 shorter events, 0.4 us)
Async XLA Ops:
  0.6 3.2 %copy-start.4 = (f32[1,4,128]{2,1,0:T(4,128)S(1)}, f32[1,4,128]{2,1,0:T(4,128)}, u32[]{:S(2)}) copy-start(f32[1,4,128]{2,1,0:T(4,128)} %param.11) | copy-start | bytes 6148
  0.6 8.6 %copy-start.3 = (bf16[1,128,128]{2,1,0:T(8,128)(2,1)S(1)}, bf16[1,128,128]{2,1,0:T(8,128)(2,1)}, u32[]{:S(2)}) copy-start(bf16[1,128,128]{2,1,0:T(8,128)(2,1)} %param.8) | copy-start | bytes 98308
  0.7 8.6 %copy-start.2 = (bf16[1,128,128]{2,1,0:T(8,128)(2,1)S(1)}, bf16[1,128,128]{2,1,0:T(8,128)(2,1)}, u32[]{:S(2)}) copy-start(bf16[1,128,128]{2,1,0:T(8,128)(2,1)} %param.9) | copy-start | bytes 98308
  3.9 75.6 %collective-permute-start = (bf16[1072,128]{1,0:T(8,128)(2,1)S(1)}, bf16[1072,128]{1,0:T(8,128)(2,1)S(1)}, u32[]{:S(2)}, u32[]{:S(2)}) collective-permute-start(bf16[1072,128]{1,0:T(8,128)(2,1)S(1)} %get-tuple-element.24), channel_id=1, source_target_pairs={{0,8},{1,9},{8,0},{9,1},{16,24},{17,25},{24,16},{25,17},{32,40},{3... | collective-permute-start | bytes 823304 | tf_op jit(solution)/shard_map/ppermute | solution.py:137
  9.3 81.3 %copy-start.1 = (s32[1,64]{1,0:T(1,128)S(1)}, s32[1,64]{1,0:T(1,128)}, u32[]{:S(2)}) copy-start(s32[1,64]{1,0:T(1,128)} %param.13) | copy-start | bytes 772
  79.7 10.9 %collective-permute-start.1 = (bf16[4192,128]{1,0:T(8,128)(2,1)S(1)}, bf16[4192,128]{1,0:T(8,128)(2,1)S(1)}, u32[]{:S(2)}, u32[]{:S(2)}) collective-permute-start(bf16[4192,128]{1,0:T(8,128)(2,1)S(1)} %constant_dynamic-update-slice_fusion.5.mine), channel_id=1, source_target_pairs={{0,1},{1,0},{8,9},{9,8},{16,17},{17,16},{24,25},{25,24},{32,33},{3... | collective-permute-start | bytes 3219464 | tf_op jit(solution)/shard_map/ppermute | solution.py:137
  93.8 10.0 %collective-permute-start.4 = (bf16[2,128,256]{2,1,0:T(8,128)(2,1)S(1)}, bf16[2,128,256]{2,1,0:T(8,128)(2,1)S(1)}, u32[]{:S(2)}, u32[]{:S(2)}) collective-permute-start(bf16[2,128,256]{2,1,0:T(8,128)(2,1)S(1)} %convert_element_type.73), channel_id=1, source_target_pairs={{0,224},{1,33},{8,232},{9,41},{16,240},{17,49},{24,248},{25,57},{3... | collective-permute-start | bytes 393224 | tf_op jit(solution)/shard_map/ppermute | solution.py:137
  103.7 4.7 %copy-start = (f32[4,128,256]{2,1,0:T(8,128)}, f32[4,128,256]{2,1,0:T(8,128)S(1)}, u32[]{:S(2)}) copy-start(f32[4,128,256]{2,1,0:T(8,128)S(1)} %get-tuple-element.13) | copy-start | bytes 1572868
  104.6 13.3 %collective-permute-start.5 = (bf16[2,128,256]{2,1,0:T(8,128)(2,1)}, bf16[2,128,256]{2,1,0:T(8,128)(2,1)}, u32[]{:S(2)}, u32[]{:S(2)}) collective-permute-start(bf16[2,128,256]{2,1,0:T(8,128)(2,1)} %add_convert_fusion.1), channel_id=1, source_target_pairs={{0,224},{1,33},{8,232},{9,41},{16,240},{17,49},{24,248},{25,57},{3... | collective-permute-start | bytes 393224 | tf_op jit(solution)/shard_map/ppermute | solution.py:137
  111.8 11.7 %collective-permute-start.2 = (bf16[2,512,128]{2,1,0:T(8,128)(2,1)S(1)}, bf16[2,512,128]{2,1,0:T(8,128)(2,1)S(1)}, u32[]{:S(2)}, u32[]{:S(2)}) collective-permute-start(bf16[2,512,128]{2,1,0:T(8,128)(2,1)S(1)} %slice.71), channel_id=1, source_target_pairs={{0,1},{1,0},{8,9},{9,8},{16,17},{17,16},{24,25},{25,24},{32,33},{3... | collective-permute-start | bytes 786440 | tf_op jit(solution)/shard_map/ppermute | solution.py:137
  118.9 10.8 %collective-permute-start.6 = (bf16[2,128,256]{2,1,0:T(8,128)(2,1)S(1)}, bf16[2,128,256]{2,1,0:T(8,128)(2,1)S(1)}, u32[]{:S(2)}, u32[]{:S(2)}) collective-permute-start(bf16[2,128,256]{2,1,0:T(8,128)(2,1)S(1)} %add_convert_fusion), channel_id=1, source_target_pairs={{0,224},{1,33},{8,232},{9,41},{16,240},{17,49},{24,248},{25,57},{3... | collective-permute-start | bytes 393224 | tf_op jit(solution)/shard_map/ppermute | solution.py:137
  129.8 9.2 %collective-permute-start.7 = (bf16[128,256]{1,0:T(8,128)(2,1)S(1)}, bf16[128,256]{1,0:T(8,128)(2,1)S(1)}, u32[]{:S(2)}, u32[]{:S(2)}) collective-permute-start(bf16[128,256]{1,0:T(8,128)(2,1)S(1)} %fusion.6), channel_id=1, source_target_pairs={{0,240},{1,17},{8,248},{9,25},{16,0},{17,33},{24,8},{25,41},{32,16... | collective-permute-start | bytes 196616 | tf_op jit(solution)/shard_map/ppermute | solution.py:137
  135.0 13.5 %collective-permute-start.3 = (bf16[512,128]{1,0:T(8,128)(2,1)S(1)}, bf16[512,128]{1,0:T(8,128)(2,1)S(1)}, u32[]{:S(2)}, u32[]{:S(2)}) collective-permute-start(bf16[512,128]{1,0:T(8,128)(2,1)S(1)} %fusion.3), channel_id=1, source_target_pairs={{0,8},{1,9},{8,0},{9,1},{16,24},{17,25},{24,16},{25,17},{32,40},{3... | collective-permute-start | bytes 393224 | tf_op jit(solution)/shard_map/ppermute | solution.py:137
  139.0 10.3 %collective-permute-start.8 = (bf16[128,256]{1,0:T(8,128)(2,1)S(1)}, bf16[128,256]{1,0:T(8,128)(2,1)S(1)}, u32[]{:S(2)}, u32[]{:S(2)}) collective-permute-start(bf16[128,256]{1,0:T(8,128)(2,1)S(1)} %fusion.5), channel_id=1, source_target_pairs={{0,1},{1,16},{8,9},{9,24},{16,17},{17,32},{24,25},{25,40},{32,33},... | collective-permute-start | bytes 196616 | tf_op jit(solution)/shard_map/ppermute | solution.py:137
  146.5 7.5 %collective-permute-start.9 = (bf16[128,256]{1,0:T(8,128)(2,1)S(1)}, bf16[128,256]{1,0:T(8,128)(2,1)S(1)}, u32[]{:S(2)}, u32[]{:S(2)}) collective-permute-start(bf16[128,256]{1,0:T(8,128)(2,1)S(1)} %fusion.5), channel_id=1, source_target_pairs={{1,17},{9,25},{17,33},{25,41},{33,49},{41,57},{49,65},{57,73},{65,... | collective-permute-start | bytes 196616 | tf_op jit(solution)/shard_map/ppermute | solution.py:137

commit v5 on v4

--- a/solution.py
+++ b/solution.py
@@ -36,6 +36,7 @@
     scale = 1.0 / math.sqrt(width)
     place, core = where[0], where[1]
     step, member = place // NEAR, place % NEAR
+    role = lax.rem(core + step // BUNDLE, 2)
     token = lax.broadcasted_iota(jnp.int32, (toks, toks), 1)
     row = lax.broadcasted_iota(jnp.int32, (toks, toks), 0)
     key_row, token_row = row % span_rows, token % span_rows
@@ -46,24 +47,29 @@
     else:
         dq[...] = refs[0][...]
 
-    def one_block(index, carry):
-        turn = first + index
-        ahead = jnp.where(core == 0, turn - (ring // 2 - 1), ring // 2 - turn)
-        block = lax.rem(step + ahead + ring, ring)
-        chip = block * NEAR + member
-        start = pl.multiple_of(keys + block * toks, STAT_ROWS)
-        a, b = mine[pl.ds(start, toks)], theirs[pl.ds(start, toks)]
-        low, high = jnp.where(core == 0, a, b), jnp.where(core == 0, b, a)
-        k = jnp.concatenate([low[:span_rows], high[:span_rows]])
-        v = jnp.concatenate([low[span_rows:], high[span_rows:]])
-        key_span = jnp.where(row < span_rows, order[2 * chip], order[2 * chip + 1])
-        key_pos = key_span * span_rows + key_row
-        dk = jnp.zeros((toks, width), jnp.float32)
-        dv = jnp.zeros((toks, width), jnp.float32)
+    def one_bundle(index, carry):
+        ks, vs, positions = [], [], []
+        for j in range(BUNDLE):
+            turn = first + index * BUNDLE + j
+            ahead = jnp.where(role == 0, turn - (ring // 2 - 1), ring // 2 - turn)
+            block = lax.rem(step + ahead + ring, ring)
+            chip = block * NEAR + member
+            start = pl.multiple_of(keys + block * toks, STAT_ROWS)
+            a, b = mine[pl.ds(start, toks)], theirs[pl.ds(start, toks)]
+            first_span = lax.rem(block + step + core, 2) == 0
+            low, high = jnp.where(first_span, a, b), jnp.where(first_span, b, a)
+            ks += [low[:span_rows], high[:span_rows]]
+            vs += [low[span_rows:], high[span_rows:]]
+            key_span = jnp.where(row < span_rows, order[2 * chip], order[2 * chip + 1])
+            positions.append(key_span * span_rows + key_row)
+        k, v, key_pos = jnp.concatenate(ks), jnp.concatenate(vs), jnp.concatenate(positions)
+        dk = jnp.zeros((BUNDLE * toks, width), jnp.float32)
+        dv = jnp.zeros((BUNDLE * toks, width), jnp.float32)
         for near in range(NEAR):
             near_chip = step * NEAR + (member ^ near)
             span = jnp.where(token < span_rows, order[2 * near_chip], order[2 * near_chip + 1])
-            visible = key_pos <= span * span_rows + token_row
+            query_pos = span * span_rows + token_row
+            visible = key_pos <= jnp.concatenate([query_pos] * BUNDLE)
             base = near * payload
             for part, source in ((near, mine), (NEAR + near, theirs)):
                 q = source[base : base + rows]
@@ -88,11 +94,12 @@
                 dv = dv + jnp.dot(p, d, preferred_element_type=jnp.float32)
                 dk = dk + jnp.dot(ds, q, preferred_element_type=jnp.float32)
                 dq[part] += lax.dot_general(ds, k, tn, preferred_element_type=jnp.float32)
-        dkv[index, :, :width] = dk
-        dkv[index, :, width:] = dv
+        for j in range(BUNDLE):
+            dkv[index * BUNDLE + j, :, :width] = dk[j * toks : (j + 1) * toks]
+            dkv[index * BUNDLE + j, :, width:] = dv[j * toks : (j + 1) * toks]
         return carry
 
-    lax.fori_loop(0, count, one_block, 0)
+    lax.fori_loop(0, count // BUNDLE, one_bundle, 0)
 
 
 def attention_grads(first, count, heads, toks, order, where, mine, theirs, dq):
@@ -157,8 +164,12 @@
     kv = jnp.concatenate(
         [lax.dynamic_slice_in_dim(a[0], core * half, half, 0) for a in (keys, values)]
     )
-    groups = [list(range(first, size, NEAR)) for first in range(NEAR)]
-    kv = lax.all_gather(kv, "inner", axis_index_groups=groups, tiled=True)
+    groups = [
+        [2 * z + (z // NEAR + first) % 2 for z in range(chip, size, NEAR)]
+        for chip in range(NEAR)
+        for first in range(2)
+    ]
+    kv = lax.all_gather(kv, ("inner", "head"), axis_index_groups=groups, tiled=True)
     mine = jnp.concatenate([*payloads, kv])
     theirs = move(mine, swap)
 
@@ -170,8 +181,23 @@
         parts += [part[i : i + BUNDLE] for i in range(0, count, BUNDLE)]
         first += count
 
+    def role_of(z, c):
+        return (c + z // NEAR // BUNDLE) % 2
+
     def hop(blocks):
-        return lambda z, c: (z - blocks * NEAR, 0) if c == 0 else (z + blocks * NEAR, 1)
+        def target(z, c):
+            role = role_of(z, c)
+            z = (z + (blocks if role else -blocks) * NEAR) % size
+            return z, role_of(z, role)
+
+        return target
+
+    def last_one(z, c):
+        after = (z + NEAR) % size
+        return (after, role_of(after, 0)) if role_of(z, c) else (z, 1 - c)
+
+    def last_two(z, c):
+        return hop(1)(z, c) if role_of(z, c) else None
 
     total = parts[0].astype(jnp.bfloat16)
     for part in parts[1:]:
@@ -180,9 +206,9 @@
         total = sums.astype(jnp.bfloat16)
     total = move(total[0], hop(1)).astype(jnp.float32) + sums[1]
     total = total.astype(jnp.bfloat16)
-    one = move(total, lambda z, c: (z, 1) if c == 0 else (z + NEAR, 0))
-    two = move(total, lambda z, c: None if c == 0 else (z + NEAR, 1))
-    two = jnp.where(core == 0, total, two)
+    one = move(total, last_one)
+    two = move(total, last_two)
+    two = jnp.where(role_of(place, core) == 0, total, two)
     dkv = (one.astype(jnp.float32) + two.astype(jnp.float32)).astype(jnp.bfloat16)
 
     dq_theirs = move(dq[NEAR:].astype(jnp.bfloat16), swap)

time: 155 us -> 152 us (0.981); the launches traced: 155 us -> 149 us
  starting transfers between devices: 51 us -> 38 us
  waiting for transfers between devices: 13.1 us -> 19.8 us
  blocking collectives: 70.3 us -> 74.8 us
  Pallas kernels: 12.5 us -> 9.15 us
    ppermute x10, starting transfers between devices: 51 us -> 38 us  [move(): return lax.ppermute(array, ('inner', 'head'), pairs)]
    ppermute x10, waiting for transfers between devices: 13.1 us -> 19.8 us  [move(): return lax.ppermute(array, ('inner', 'head'), pairs)]
    all_gather x1, blocking collectives: 70.3 us -> 74.8 us  [body(): lax.all_gather(kv, ('inner', 'head'), axis_index_groups=groups, tiled=True)]
    pallas_call x3, Pallas kernels: 12.5 us -> 9.15 us  [attention_grads(): pl.pallas_call(functools.partial(kernel, first, count, heads, toks), out_...]
  transfers between devices with their start and end apart: 10 -> 10, of which waited for: 4 -> 6; matrix products, arithmetic and copies ran while one was open for 1% -> 1% of each run, Pallas kernels for 6% -> 5%
where the time goes in v5:
time: 152 us; the launch traced here: 149 us
  blocking collectives  74.8 us (49%)
  starting transfers between devices  38 us (25%)
  waiting for transfers between devices  19.8 us (13%)
  Pallas kernels  9.15 us (6%)
  local copies, waits for them, and re-layouts  3.61 us (2%)
  other arithmetic  3.17 us (2%)
    all_gather x1, blocking collectives, body(): lax.all_gather(kv, ('inner', 'head'), axis_index_groups=groups, tiled=True)  74.8 us
    ppermute x10, starting transfers between devices, move(): return lax.ppermute(array, ('inner', 'head'), pairs)  38 us
    ppermute x10, waiting for transfers between devices, move(): return lax.ppermute(array, ('inner', 'head'), pairs)  19.8 us
    pallas_call x3, Pallas kernels, attention_grads(): pl.pallas_call(functools.partial(kernel, first, count, heads, toks), out_...  9.15 us
  transfers between devices with their start and end apart: 10, of which 6 were waited for; matrix products, arithmetic and copies ran while one was open for 1% of the time, Pallas kernels for 5%

profile of v5, /device:TPU:33, one launch (start us, length us, event | category | flops | bytes accessed | tf_op | source)
XLA Modules:
  0.0 149.4 jit_solution(6740779216540160589)
XLA Ops:
  0.6 0.0 copy-start.4
  0.6 0.0 copy-start.3
  0.7 0.0 copy-start.2
  0.7 0.9 copy.15
  1.6 0.9 copy.16
  2.6 1.2 fusion.2
  3.8 0.1 copy.17
  3.8 0.0 copy-done.4
  3.9 5.3 %collective-permute-start = (bf16[1072,128]{1,0:T(8,128)(2,1)S(1)}, bf16[1072,128]{1,0:T(8,128)(2,1)S(1)}, u32[]{:S(2)}, u32[]{:S(2)}) collective-permute-start(bf16[1072,128]{1,0:T(8,128)(2,1)S(1)} %get-tuple-element.24), channel_id=1, source_target_pairs={{0,8},{1,9},{8,0},{9,1},{16,24},{17,25},{24,16},{25,17},{32,40},{3... | collective-permute-start | bytes 823304 | tf_op jit(solution)/shard_map/ppermute | solution.py:144
  9.2 0.0 copy-done.3
  9.2 0.0 copy-done.2
  9.3 0.0 copy-start.1
  9.3 74.8 %all_gather.3 = bf16[2048,128]{1,0:T(8,128)(2,1)S(1)} all-gather(bf16[128,128]{1,0:T(8,128)(2,1)S(1)} %pad_maximum_fusion), channel_id=1, replica_groups={{0,17,32,49,64,81,96,113,128,145,160,177,192,209,224,241},{1,16,33,48,6..., dimensions={0}, use_global_device_ids=true | all-gather | bytes 557056 | tf_op jit(solution)/shard_map/all_gather | solution.py:172
  84.0 0.0 collective-permute-done
  84.1 0.1 constant_dynamic-update-slice_fusion.5.mine
  84.2 2.0 %collective-permute-start.1 = (bf16[4192,128]{1,0:T(8,128)(2,1)S(1)}, bf16[4192,128]{1,0:T(8,128)(2,1)S(1)}, u32[]{:S(2)}, u32[]{:S(2)}) collective-permute-start(bf16[4192,128]{1,0:T(8,128)(2,1)S(1)} %constant_dynamic-update-slice_fusion.5.mine), channel_id=1, source_target_pairs={{0,1},{1,0},{8,9},{9,8},{16,17},{17,16},{24,25},{25,24},{32,33},{3... | collective-permute-start | bytes 3219464 | tf_op jit(solution)/shard_map/ppermute | solution.py:144
  86.1 0.1 pad_add_fusion.where
  86.2 2.6 %collective-permute-done.1.theirs = bf16[4192,128]{1,0:T(8,128)(2,1)S(1)} collective-permute-done((bf16[4192,128]{1,0:T(8,128)(2,1)S(1)}, bf16[4192,128]{1,0:T(8,128)(2,1)S(1)}, u32[]{:S(2)}, u32[]{:S(2)}) %collective-permute-start.1) | collective-permute-done | bytes 1073184 | tf_op jit(solution)/shard_map/ppermute | solution.py:144
  88.8 0.0 copy-done.1
  88.8 2.3 %shard_map.94 = (f32[4,512,128]{2,1,0:T(8,128)S(1)}, f32[2,128,256]{2,1,0:T(8,128)S(1)}) custom-call(s32[64]{0:T(128)S(1)} %bitcast.48, s32[2]{0:T(128)S(1)} %pad_add_fusion.where, bf16[4192,128]{1,0:T(8,128)(2,1)S(1)} %constant_dynamic-update-slice_fusion.5.mine, bf16[4192,128]{1,0:T(8,128)(2,1)S(1)} %collective-permute-done.1.theirs), custom_call_target="tpu_custom_call" | custom-call | flops 671088640 | bytes 2097152 | tf_op jit(solution)/shard_map/pallas_call | solution.py:111
  91.2 4.1 %collective-permute-start.4 = (bf16[2,128,256]{2,1,0:T(8,128)(2,1)S(1)}, bf16[2,128,256]{2,1,0:T(8,128)(2,1)S(1)}, u32[]{:S(2)}, u32[]{:S(2)}) collective-permute-start(bf16[2,128,256]{2,1,0:T(8,128)(2,1)S(1)} %convert_element_type.73), channel_id=1, source_target_pairs={{0,225},{1,32},{8,233},{9,40},{16,241},{17,48},{24,249},{25,56},{3... | collective-permute-start | bytes 393224 | tf_op jit(solution)/shard_map/ppermute | solution.py:144
  95.3 4.4 %shard_map.95 = (f32[4,512,128]{2,1,0:T(8,128)S(1)}, f32[4,128,256]{2,1,0:T(8,128)S(1)}) custom-call(s32[64]{0:T(128)S(1)} %bitcast.49, s32[2]{0:T(128)S(1)} %pad_add_fusion.where, bf16[4192,128]{1,0:T(8,128)(2,1)S(1)} %constant_dynamic-update-slice_fusion.5.mine, ...), custom_call_target="tpu_custom_call", output_to_operand_aliasing={{0}: (4, {})} | custom-call | flops 1342177280 | bytes 2097152 | tf_op jit(solution)/shard_map/pallas_call | solution.py:111
  99.6 0.0 copy-start
  99.6 3.3 %collective-permute-done.4 = bf16[2,128,256]{2,1,0:T(8,128)(2,1)S(1)} collective-permute-done((bf16[2,128,256]{2,1,0:T(8,128)(2,1)S(1)}, bf16[2,128,256]{2,1,0:T(8,128)(2,1)S(1)}, u32[]{:S(2)}, u32[]{:S(2)}) %collective-permute-start.4) | collective-permute-done | bytes 131104 | tf_op jit(solution)/shard_map/ppermute | solution.py:144
  102.9 0.7 add_convert_fusion.1
  103.6 2.7 %collective-permute-start.5 = (bf16[2,128,256]{2,1,0:T(8,128)(2,1)}, bf16[2,128,256]{2,1,0:T(8,128)(2,1)}, u32[]{:S(2)}, u32[]{:S(2)}) collective-permute-start(bf16[2,128,256]{2,1,0:T(8,128)(2,1)} %add_convert_fusion.1), channel_id=1, source_target_pairs={{0,225},{1,32},{8,233},{9,40},{16,241},{17,48},{24,249},{25,56},{3... | collective-permute-start | bytes 393224 | tf_op jit(solution)/shard_map/ppermute | solution.py:144
  106.3 0.0 copy-done
  106.3 2.4 %shard_map.96 = (f32[4,512,128]{2,1,0:T(8,128)S(1)}, f32[2,128,256]{2,1,0:T(8,128)S(1)}) custom-call(s32[64]{0:T(128)S(1)} %bitcast.50, s32[2]{0:T(128)S(1)} %pad_add_fusion.where, bf16[4192,128]{1,0:T(8,128)(2,1)S(1)} %constant_dynamic-update-slice_fusion.5.mine, ...), custom_call_target="tpu_custom_call", output_to_operand_aliasing={{0}: (4, {})} | custom-call | flops 671088640 | bytes 2097152 | tf_op jit(solution)/shard_map/pallas_call | solution.py:111
  108.8 4.3 %collective-permute-start.2 = (bf16[2,512,128]{2,1,0:T(8,128)(2,1)S(1)}, bf16[2,512,128]{2,1,0:T(8,128)(2,1)S(1)}, u32[]{:S(2)}, u32[]{:S(2)}) collective-permute-start(bf16[2,512,128]{2,1,0:T(8,128)(2,1)S(1)} %slice.71), channel_id=1, source_target_pairs={{0,1},{1,0},{8,9},{9,8},{16,17},{17,16},{24,25},{25,24},{32,33},{3... | collective-permute-start | bytes 786440 | tf_op jit(solution)/shard_map/ppermute | solution.py:144
  113.2 1.0 collective-permute-done.5
  114.1 1.0 add_convert_fusion
  115.1 5.7 %collective-permute-start.6 = (bf16[2,128,256]{2,1,0:T(8,128)(2,1)S(1)}, bf16[2,128,256]{2,1,0:T(8,128)(2,1)S(1)}, u32[]{:S(2)}, u32[]{:S(2)}) collective-permute-start(bf16[2,128,256]{2,1,0:T(8,128)(2,1)S(1)} %add_convert_fusion), channel_id=1, source_target_pairs={{0,225},{1,32},{8,233},{9,40},{16,241},{17,48},{24,249},{25,56},{3... | collective-permute-start | bytes 393224 | tf_op jit(solution)/shard_map/ppermute | solution.py:144
  120.8 0.0 collective-permute-done.2
  120.9 7.6 %collective-permute-done.6 = bf16[2,128,256]{2,1,0:T(8,128)(2,1)S(1)} collective-permute-done((bf16[2,128,256]{2,1,0:T(8,128)(2,1)S(1)}, bf16[2,128,256]{2,1,0:T(8,128)(2,1)S(1)}, u32[]{:S(2)}, u32[]{:S(2)}) %collective-permute-start.6) | collective-permute-done | bytes 131104 | tf_op jit(solution)/shard_map/ppermute | solution.py:144
  128.6 6.6 %collective-permute-start.7 = (bf16[128,256]{1,0:T(8,128)(2,1)S(1)}, bf16[128,256]{1,0:T(8,128)(2,1)S(1)}, u32[]{:S(2)}, u32[]{:S(2)}) collective-permute-start(bf16[128,256]{1,0:T(8,128)(2,1)S(1)} %fusion.6), channel_id=1, source_target_pairs={{0,241},{1,17},{8,249},{9,25},{16,0},{17,32},{24,8},{25,40},{32,48... | collective-permute-start | bytes 196616 | tf_op jit(solution)/shard_map/ppermute | solution.py:144
  135.2 2.0 %collective-permute-start.3 = (bf16[512,128]{1,0:T(8,128)(2,1)S(1)}, bf16[512,128]{1,0:T(8,128)(2,1)S(1)}, u32[]{:S(2)}, u32[]{:S(2)}) collective-permute-start(bf16[512,128]{1,0:T(8,128)(2,1)S(1)} %fusion.3), channel_id=1, source_target_pairs={{0,8},{1,9},{8,0},{9,1},{16,24},{17,25},{24,16},{25,17},{32,40},{3... | collective-permute-start | bytes 393224 | tf_op jit(solution)/shard_map/ppermute | solution.py:144
  137.1 0.4 collective-permute-done.7
  137.5 3.5 %collective-permute-start.8 = (bf16[128,256]{1,0:T(8,128)(2,1)S(1)}, bf16[128,256]{1,0:T(8,128)(2,1)S(1)}, u32[]{:S(2)}, u32[]{:S(2)}) collective-permute-start(bf16[128,256]{1,0:T(8,128)(2,1)S(1)} %fusion.5), channel_id=1, source_target_pairs={{0,1},{1,16},{8,9},{9,24},{16,17},{17,33},{24,25},{25,41},{32,49},... | collective-permute-start | bytes 196616 | tf_op jit(solution)/shard_map/ppermute | solution.py:144
  141.1 2.0 %collective-permute-start.9 = (bf16[128,256]{1,0:T(8,128)(2,1)S(1)}, bf16[128,256]{1,0:T(8,128)(2,1)S(1)}, u32[]{:S(2)}, u32[]{:S(2)}) collective-permute-start(bf16[128,256]{1,0:T(8,128)(2,1)S(1)} %fusion.5), channel_id=1, source_target_pairs={{1,17},{9,25},{17,32},{25,40},{32,48},{40,56},{48,65},{56,73},{65,... | collective-permute-start | bytes 196616 | tf_op jit(solution)/shard_map/ppermute | solution.py:144
  143.1 0.0 collective-permute-done.3
  143.1 0.8 copy.20
  143.9 0.0 collective-permute-done.8
  143.9 4.9 %collective-permute-done.9 = bf16[128,256]{1,0:T(8,128)(2,1)S(1)} collective-permute-done((bf16[128,256]{1,0:T(8,128)(2,1)S(1)}, bf16[128,256]{1,0:T(8,128)(2,1)S(1)}, u32[]{:S(2)}, u32[]{:S(2)}) %collective-permute-start.9) | collective-permute-done | bytes 65568 | tf_op jit(solution)/shard_map/ppermute | solution.py:144
  148.8 0.6 slice_bitcast_fusion.2
  (19 shorter events, 0.4 us)
Async XLA Ops:
  0.6 3.2 %copy-start.4 = (f32[1,4,128]{2,1,0:T(4,128)S(1)}, f32[1,4,128]{2,1,0:T(4,128)}, u32[]{:S(2)}) copy-start(f32[1,4,128]{2,1,0:T(4,128)} %param.11) | copy-start | bytes 6148
  0.6 8.6 %copy-start.3 = (bf16[1,128,128]{2,1,0:T(8,128)(2,1)S(1)}, bf16[1,128,128]{2,1,0:T(8,128)(2,1)}, u32[]{:S(2)}) copy-start(bf16[1,128,128]{2,1,0:T(8,128)(2,1)} %param.8) | copy-start | bytes 98308
  0.7 8.6 %copy-start.2 = (bf16[1,128,128]{2,1,0:T(8,128)(2,1)S(1)}, bf16[1,128,128]{2,1,0:T(8,128)(2,1)}, u32[]{:S(2)}) copy-start(bf16[1,128,128]{2,1,0:T(8,128)(2,1)} %param.9) | copy-start | bytes 98308
  3.9 80.1 %collective-permute-start = (bf16[1072,128]{1,0:T(8,128)(2,1)S(1)}, bf16[1072,128]{1,0:T(8,128)(2,1)S(1)}, u32[]{:S(2)}, u32[]{:S(2)}) collective-permute-start(bf16[1072,128]{1,0:T(8,128)(2,1)S(1)} %get-tuple-element.24), channel_id=1, source_target_pairs={{0,8},{1,9},{8,0},{9,1},{16,24},{17,25},{24,16},{25,17},{32,40},{3... | collective-permute-start | bytes 823304 | tf_op jit(solution)/shard_map/ppermute | solution.py:144
  9.3 79.5 %copy-start.1 = (s32[1,64]{1,0:T(1,128)S(1)}, s32[1,64]{1,0:T(1,128)}, u32[]{:S(2)}) copy-start(s32[1,64]{1,0:T(1,128)} %param.13) | copy-start | bytes 772
  84.2 4.6 %collective-permute-start.1 = (bf16[4192,128]{1,0:T(8,128)(2,1)S(1)}, bf16[4192,128]{1,0:T(8,128)(2,1)S(1)}, u32[]{:S(2)}, u32[]{:S(2)}) collective-permute-start(bf16[4192,128]{1,0:T(8,128)(2,1)S(1)} %constant_dynamic-update-slice_fusion.5.mine), channel_id=1, source_target_pairs={{0,1},{1,0},{8,9},{9,8},{16,17},{17,16},{24,25},{25,24},{32,33},{3... | collective-permute-start | bytes 3219464 | tf_op jit(solution)/shard_map/ppermute | solution.py:144
  91.2 11.7 %collective-permute-start.4 = (bf16[2,128,256]{2,1,0:T(8,128)(2,1)S(1)}, bf16[2,128,256]{2,1,0:T(8,128)(2,1)S(1)}, u32[]{:S(2)}, u32[]{:S(2)}) collective-permute-start(bf16[2,128,256]{2,1,0:T(8,128)(2,1)S(1)} %convert_element_type.73), channel_id=1, source_target_pairs={{0,225},{1,32},{8,233},{9,40},{16,241},{17,48},{24,249},{25,56},{3... | collective-permute-start | bytes 393224 | tf_op jit(solution)/shard_map/ppermute | solution.py:144
  99.6 6.7 %copy-start = (f32[4,128,256]{2,1,0:T(8,128)}, f32[4,128,256]{2,1,0:T(8,128)S(1)}, u32[]{:S(2)}) copy-start(f32[4,128,256]{2,1,0:T(8,128)S(1)} %get-tuple-element.13) | copy-start | bytes 1572868
  103.6 10.6 %collective-permute-start.5 = (bf16[2,128,256]{2,1,0:T(8,128)(2,1)}, bf16[2,128,256]{2,1,0:T(8,128)(2,1)}, u32[]{:S(2)}, u32[]{:S(2)}) collective-permute-start(bf16[2,128,256]{2,1,0:T(8,128)(2,1)} %add_convert_fusion.1), channel_id=1, source_target_pairs={{0,225},{1,32},{8,233},{9,40},{16,241},{17,48},{24,249},{25,56},{3... | collective-permute-start | bytes 393224 | tf_op jit(solution)/shard_map/ppermute | solution.py:144
  108.8 12.0 %collective-permute-start.2 = (bf16[2,512,128]{2,1,0:T(8,128)(2,1)S(1)}, bf16[2,512,128]{2,1,0:T(8,128)(2,1)S(1)}, u32[]{:S(2)}, u32[]{:S(2)}) collective-permute-start(bf16[2,512,128]{2,1,0:T(8,128)(2,1)S(1)} %slice.71), channel_id=1, source_target_pairs={{0,1},{1,0},{8,9},{9,8},{16,17},{17,16},{24,25},{25,24},{32,33},{3... | collective-permute-start | bytes 786440 | tf_op jit(solution)/shard_map/ppermute | solution.py:144
  115.1 13.4 %collective-permute-start.6 = (bf16[2,128,256]{2,1,0:T(8,128)(2,1)S(1)}, bf16[2,128,256]{2,1,0:T(8,128)(2,1)S(1)}, u32[]{:S(2)}, u32[]{:S(2)}) collective-permute-start(bf16[2,128,256]{2,1,0:T(8,128)(2,1)S(1)} %add_convert_fusion), channel_id=1, source_target_pairs={{0,225},{1,32},{8,233},{9,40},{16,241},{17,48},{24,249},{25,56},{3... | collective-permute-start | bytes 393224 | tf_op jit(solution)/shard_map/ppermute | solution.py:144
  128.6 9.0 %collective-permute-start.7 = (bf16[128,256]{1,0:T(8,128)(2,1)S(1)}, bf16[128,256]{1,0:T(8,128)(2,1)S(1)}, u32[]{:S(2)}, u32[]{:S(2)}) collective-permute-start(bf16[128,256]{1,0:T(8,128)(2,1)S(1)} %fusion.6), channel_id=1, source_target_pairs={{0,241},{1,17},{8,249},{9,25},{16,0},{17,32},{24,8},{25,40},{32,48... | collective-permute-start | bytes 196616 | tf_op jit(solution)/shard_map/ppermute | solution.py:144
  135.2 7.9 %collective-permute-start.3 = (bf16[512,128]{1,0:T(8,128)(2,1)S(1)}, bf16[512,128]{1,0:T(8,128)(2,1)S(1)}, u32[]{:S(2)}, u32[]{:S(2)}) collective-permute-start(bf16[512,128]{1,0:T(8,128)(2,1)S(1)} %fusion.3), channel_id=1, source_target_pairs={{0,8},{1,9},{8,0},{9,1},{16,24},{17,25},{24,16},{25,17},{32,40},{3... | collective-permute-start | bytes 393224 | tf_op jit(solution)/shard_map/ppermute | solution.py:144
  137.5 6.3 %collective-permute-start.8 = (bf16[128,256]{1,0:T(8,128)(2,1)S(1)}, bf16[128,256]{1,0:T(8,128)(2,1)S(1)}, u32[]{:S(2)}, u32[]{:S(2)}) collective-permute-start(bf16[128,256]{1,0:T(8,128)(2,1)S(1)} %fusion.5), channel_id=1, source_target_pairs={{0,1},{1,16},{8,9},{9,24},{16,17},{17,33},{24,25},{25,41},{32,49},... | collective-permute-start | bytes 196616 | tf_op jit(solution)/shard_map/ppermute | solution.py:144
  141.1 7.7 %collective-permute-start.9 = (bf16[128,256]{1,0:T(8,128)(2,1)S(1)}, bf16[128,256]{1,0:T(8,128)(2,1)S(1)}, u32[]{:S(2)}, u32[]{:S(2)}) collective-permute-start(bf16[128,256]{1,0:T(8,128)(2,1)S(1)} %fusion.5), channel_id=1, source_target_pairs={{1,17},{9,25},{17,32},{25,40},{32,48},{40,56},{48,65},{56,73},{65,... | collective-permute-start | bytes 196616 | tf_op jit(solution)/shard_map/ppermute | solution.py:144

commit v6 on v5

--- a/solution.py
+++ b/solution.py
@@ -192,24 +192,34 @@
 
         return target
 
-    def last_one(z, c):
-        after = (z + NEAR) % size
-        return (after, role_of(after, 0)) if role_of(z, c) else (z, 1 - c)
-
-    def last_two(z, c):
-        return hop(1)(z, c) if role_of(z, c) else None
-
     total = parts[0].astype(jnp.bfloat16)
     for part in parts[1:]:
         total = move(total, hop(BUNDLE))
-        sums = total.astype(jnp.float32) + part
-        total = sums.astype(jnp.bfloat16)
-    total = move(total[0], hop(1)).astype(jnp.float32) + sums[1]
-    total = total.astype(jnp.bfloat16)
-    one = move(total, last_one)
-    two = move(total, last_two)
-    two = jnp.where(role_of(place, core) == 0, total, two)
-    dkv = (one.astype(jnp.float32) + two.astype(jnp.float32)).astype(jnp.bfloat16)
+        total = (total.astype(jnp.float32) + part).astype(jnp.bfloat16)
+
+    def home(role0, role1):
+        def target(z, c):
+            to = role1 if role_of(z, c) else role0
+            if to is None:
+                return None
+            z = (z + to[0] * NEAR) % size
+            return z, role_of(z, to[1])
+
+        return target
+
+    down = role_of(place, core) == 0
+    away, beside = total[0], total[1]
+    first = move(away, home((-1, 1), (2, 0)))
+    second = move(away, home((-1, 0), (2, 1)))
+    third = move(beside, home((0, 1), (1, 0)))
+    fourth = move(beside, home(None, (1, 1)))
+    pieces = (
+        jnp.where(down, beside, third),
+        jnp.where(down, second, first),
+        jnp.where(down, third, fourth),
+        jnp.where(down, first, second),
+    )
+    dkv = sum(piece.astype(jnp.float32) for piece in pieces).astype(jnp.bfloat16)
 
     dq_theirs = move(dq[NEAR:].astype(jnp.bfloat16), swap)
     dq_mine = dq[:NEAR] + dq_theirs.astype(jnp.float32)

time: 152 us -> 152 us (level)
  waiting for transfers between devices: 19.8 us -> 13.2 us
  starting transfers between devices: 38 us -> 43.9 us
    ppermute x10 -> x11, waiting for transfers between devices: 19.8 us -> 13.2 us  [move(): return lax.ppermute(array, ('inner', 'head'), pairs)]
    ppermute x10 -> x11, starting transfers between devices: 38 us -> 43.9 us  [move(): return lax.ppermute(array, ('inner', 'head'), pairs)]
  transfers between devices with their start and end apart: 10 -> 11, of which waited for: 6 -> 5; matrix products, arithmetic and copies ran while one was open for 1% -> 1% of each run, Pallas kernels for 5% -> 5%
where the time goes in v6:
time: 152 us; the launch traced here: 149 us
  blocking collectives  74.8 us (49%)
  starting transfers between devices  43.9 us (29%)
  waiting for transfers between devices  13.2 us (9%)
  Pallas kernels  9.15 us (6%)
  local copies, waits for them, and re-layouts  3.61 us (2%)
  other arithmetic  3.18 us (2%)
    all_gather x1, blocking collectives, body(): lax.all_gather(kv, ('inner', 'head'), axis_index_groups=groups, tiled=True)  74.8 us
    ppermute x11, starting transfers between devices, move(): return lax.ppermute(array, ('inner', 'head'), pairs)  43.9 us
    ppermute x11, waiting for transfers between devices, move(): return lax.ppermute(array, ('inner', 'head'), pairs)  13.2 us
    pallas_call x3, Pallas kernels, attention_grads(): pl.pallas_call(functools.partial(kernel, first, count, heads, toks), out_...  9.15 us
  transfers between devices with their start and end apart: 11, of which 5 were waited for; matrix products, arithmetic and copies ran while one was open for 1% of the time, Pallas kernels for 5%

profile of v6, /device:TPU:33, one launch (start us, length us, event | category | flops | bytes accessed | tf_op | source)
XLA Modules:
  0.0 148.9 jit_solution(527152800067488708)
XLA Ops:
  0.6 0.0 copy-start.4
  0.6 0.0 copy-start.3
  0.7 0.0 copy-start.2
  0.7 0.9 copy.15
  1.6 0.9 copy.16
  2.6 1.2 fusion.2
  3.8 0.1 copy.17
  3.8 0.0 copy-done.4
  3.9 5.3 %collective-permute-start = (bf16[1072,128]{1,0:T(8,128)(2,1)S(1)}, bf16[1072,128]{1,0:T(8,128)(2,1)S(1)}, u32[]{:S(2)}, u32[]{:S(2)}) collective-permute-start(bf16[1072,128]{1,0:T(8,128)(2,1)S(1)} %get-tuple-element.26), channel_id=1, source_target_pairs={{0,8},{1,9},{8,0},{9,1},{16,24},{17,25},{24,16},{25,17},{32,40},{3... | collective-permute-start | bytes 823304 | tf_op jit(solution)/shard_map/ppermute | solution.py:144
  9.2 0.0 copy-done.3
  9.2 0.0 copy-done.2
  9.3 0.0 copy-start.1
  9.3 74.8 %all_gather.3 = bf16[2048,128]{1,0:T(8,128)(2,1)S(1)} all-gather(bf16[128,128]{1,0:T(8,128)(2,1)S(1)} %pad_maximum_fusion), channel_id=1, replica_groups={{0,17,32,49,64,81,96,113,128,145,160,177,192,209,224,241},{1,16,33,48,6..., dimensions={0}, use_global_device_ids=true | all-gather | bytes 557056 | tf_op jit(solution)/shard_map/all_gather | solution.py:172
  84.0 0.0 collective-permute-done
  84.1 0.1 constant_dynamic-update-slice_fusion.5.mine
  84.2 2.0 %collective-permute-start.1 = (bf16[4192,128]{1,0:T(8,128)(2,1)S(1)}, bf16[4192,128]{1,0:T(8,128)(2,1)S(1)}, u32[]{:S(2)}, u32[]{:S(2)}) collective-permute-start(bf16[4192,128]{1,0:T(8,128)(2,1)S(1)} %constant_dynamic-update-slice_fusion.5.mine), channel_id=1, source_target_pairs={{0,1},{1,0},{8,9},{9,8},{16,17},{17,16},{24,25},{25,24},{32,33},{3... | collective-permute-start | bytes 3219464 | tf_op jit(solution)/shard_map/ppermute | solution.py:144
  86.1 0.1 pad_add_fusion.where
  86.2 2.6 %collective-permute-done.1.theirs = bf16[4192,128]{1,0:T(8,128)(2,1)S(1)} collective-permute-done((bf16[4192,128]{1,0:T(8,128)(2,1)S(1)}, bf16[4192,128]{1,0:T(8,128)(2,1)S(1)}, u32[]{:S(2)}, u32[]{:S(2)}) %collective-permute-start.1) | collective-permute-done | bytes 1073184 | tf_op jit(solution)/shard_map/ppermute | solution.py:144
  88.8 0.0 copy-done.1
  88.8 2.3 %shard_map.94 = (f32[4,512,128]{2,1,0:T(8,128)S(1)}, f32[2,128,256]{2,1,0:T(8,128)S(1)}) custom-call(s32[64]{0:T(128)S(1)} %bitcast.46, s32[2]{0:T(128)S(1)} %pad_add_fusion.where, bf16[4192,128]{1,0:T(8,128)(2,1)S(1)} %constant_dynamic-update-slice_fusion.5.mine, bf16[4192,128]{1,0:T(8,128)(2,1)S(1)} %collective-permute-done.1.theirs), custom_call_target="tpu_custom_call" | custom-call | flops 671088640 | bytes 2097152 | tf_op jit(solution)/shard_map/pallas_call | solution.py:111
  91.2 4.1 %collective-permute-start.4 = (bf16[2,128,256]{2,1,0:T(8,128)(2,1)S(1)}, bf16[2,128,256]{2,1,0:T(8,128)(2,1)S(1)}, u32[]{:S(2)}, u32[]{:S(2)}) collective-permute-start(bf16[2,128,256]{2,1,0:T(8,128)(2,1)S(1)} %convert_element_type.73), channel_id=1, source_target_pairs={{0,225},{1,32},{8,233},{9,40},{16,241},{17,48},{24,249},{25,56},{3... | collective-permute-start | bytes 393224 | tf_op jit(solution)/shard_map/ppermute | solution.py:144
  95.3 4.4 %shard_map.95 = (f32[4,512,128]{2,1,0:T(8,128)S(1)}, f32[4,128,256]{2,1,0:T(8,128)S(1)}) custom-call(s32[64]{0:T(128)S(1)} %bitcast.47, s32[2]{0:T(128)S(1)} %pad_add_fusion.where, bf16[4192,128]{1,0:T(8,128)(2,1)S(1)} %constant_dynamic-update-slice_fusion.5.mine, ...), custom_call_target="tpu_custom_call", output_to_operand_aliasing={{0}: (4, {})} | custom-call | flops 1342177280 | bytes 2097152 | tf_op jit(solution)/shard_map/pallas_call | solution.py:111
  99.6 0.0 copy-start
  99.6 3.3 %collective-permute-done.4 = bf16[2,128,256]{2,1,0:T(8,128)(2,1)S(1)} collective-permute-done((bf16[2,128,256]{2,1,0:T(8,128)(2,1)S(1)}, bf16[2,128,256]{2,1,0:T(8,128)(2,1)S(1)}, u32[]{:S(2)}, u32[]{:S(2)}) %collective-permute-start.4) | collective-permute-done | bytes 131104 | tf_op jit(solution)/shard_map/ppermute | solution.py:144
  102.9 0.7 add_convert_fusion.2
  103.6 2.7 %collective-permute-start.5 = (bf16[2,128,256]{2,1,0:T(8,128)(2,1)}, bf16[2,128,256]{2,1,0:T(8,128)(2,1)}, u32[]{:S(2)}, u32[]{:S(2)}) collective-permute-start(bf16[2,128,256]{2,1,0:T(8,128)(2,1)} %add_convert_fusion.2), channel_id=1, source_target_pairs={{0,225},{1,32},{8,233},{9,40},{16,241},{17,48},{24,249},{25,56},{3... | collective-permute-start | bytes 393224 | tf_op jit(solution)/shard_map/ppermute | solution.py:144
  106.3 0.0 copy-done
  106.3 2.4 %shard_map.96 = (f32[4,512,128]{2,1,0:T(8,128)S(1)}, f32[2,128,256]{2,1,0:T(8,128)S(1)}) custom-call(s32[64]{0:T(128)S(1)} %bitcast.48, s32[2]{0:T(128)S(1)} %pad_add_fusion.where, bf16[4192,128]{1,0:T(8,128)(2,1)S(1)} %constant_dynamic-update-slice_fusion.5.mine, ...), custom_call_target="tpu_custom_call", output_to_operand_aliasing={{0}: (4, {})} | custom-call | flops 671088640 | bytes 2097152 | tf_op jit(solution)/shard_map/pallas_call | solution.py:111
  108.8 4.3 %collective-permute-start.2 = (bf16[2,512,128]{2,1,0:T(8,128)(2,1)S(1)}, bf16[2,512,128]{2,1,0:T(8,128)(2,1)S(1)}, u32[]{:S(2)}, u32[]{:S(2)}) collective-permute-start(bf16[2,512,128]{2,1,0:T(8,128)(2,1)S(1)} %slice.67), channel_id=1, source_target_pairs={{0,1},{1,0},{8,9},{9,8},{16,17},{17,16},{24,25},{25,24},{32,33},{3... | collective-permute-start | bytes 786440 | tf_op jit(solution)/shard_map/ppermute | solution.py:144
  113.2 1.0 collective-permute-done.5
  114.1 1.0 add_convert_fusion.1
  115.1 5.7 %collective-permute-start.6 = (bf16[2,128,256]{2,1,0:T(8,128)(2,1)S(1)}, bf16[2,128,256]{2,1,0:T(8,128)(2,1)S(1)}, u32[]{:S(2)}, u32[]{:S(2)}) collective-permute-start(bf16[2,128,256]{2,1,0:T(8,128)(2,1)S(1)} %add_convert_fusion.1), channel_id=1, source_target_pairs={{0,225},{1,32},{8,233},{9,40},{16,241},{17,48},{24,249},{25,56},{3... | collective-permute-start | bytes 393224 | tf_op jit(solution)/shard_map/ppermute | solution.py:144
  120.8 0.0 collective-permute-done.2
  120.9 4.4 %collective-permute-start.3 = (bf16[512,128]{1,0:T(8,128)(2,1)S(1)}, bf16[512,128]{1,0:T(8,128)(2,1)S(1)}, u32[]{:S(2)}, u32[]{:S(2)}) collective-permute-start(bf16[512,128]{1,0:T(8,128)(2,1)S(1)} %fusion.3), channel_id=1, source_target_pairs={{0,8},{1,9},{8,0},{9,1},{16,24},{17,25},{24,16},{25,17},{32,40},{3... | collective-permute-start | bytes 393224 | tf_op jit(solution)/shard_map/ppermute | solution.py:144
  125.4 4.8 %collective-permute-done.6 = bf16[2,128,256]{2,1,0:T(8,128)(2,1)S(1)} collective-permute-done((bf16[2,128,256]{2,1,0:T(8,128)(2,1)S(1)}, bf16[2,128,256]{2,1,0:T(8,128)(2,1)S(1)}, u32[]{:S(2)}, u32[]{:S(2)}) %collective-permute-start.6) | collective-permute-done | bytes 131104 | tf_op jit(solution)/shard_map/ppermute | solution.py:144
  130.2 6.0 %collective-permute-start.10 = (bf16[128,256]{1,0:T(8,128)(2,1)S(1)}, bf16[128,256]{1,0:T(8,128)(2,1)S(1)}, u32[]{:S(2)}, u32[]{:S(2)}) collective-permute-start(bf16[128,256]{1,0:T(8,128)(2,1)S(1)} %get-tuple-element.15), channel_id=1, source_target_pairs={{1,17},{9,25},{17,32},{25,40},{32,48},{40,56},{48,65},{56,73},{65,... | collective-permute-start | bytes 196616 | tf_op jit(solution)/shard_map/ppermute | solution.py:144
  136.3 2.0 %collective-permute-start.7 = (bf16[128,256]{1,0:T(8,128)(2,1)S(1)}, bf16[128,256]{1,0:T(8,128)(2,1)S(1)}, u32[]{:S(2)}, u32[]{:S(2)}) collective-permute-start(bf16[128,256]{1,0:T(8,128)(2,1)S(1)} %get-tuple-element.15), channel_id=1, source_target_pairs={{0,1},{1,16},{8,9},{9,24},{16,17},{17,33},{24,25},{25,41},{32,49},... | collective-permute-start | bytes 196616 | tf_op jit(solution)/shard_map/ppermute | solution.py:144
  138.2 3.5 %collective-permute-start.8 = (bf16[128,256]{1,0:T(8,128)(2,1)S(1)}, bf16[128,256]{1,0:T(8,128)(2,1)S(1)}, u32[]{:S(2)}, u32[]{:S(2)}) collective-permute-start(bf16[128,256]{1,0:T(8,128)(2,1)S(1)} %get-tuple-element.16), channel_id=1, source_target_pairs={{0,241},{1,32},{8,249},{9,40},{16,0},{17,48},{24,8},{25,56},{32,65... | collective-permute-start | bytes 196616 | tf_op jit(solution)/shard_map/ppermute | solution.py:144
  141.7 4.1 %collective-permute-start.9 = (bf16[128,256]{1,0:T(8,128)(2,1)S(1)}, bf16[128,256]{1,0:T(8,128)(2,1)S(1)}, u32[]{:S(2)}, u32[]{:S(2)}) collective-permute-start(bf16[128,256]{1,0:T(8,128)(2,1)S(1)} %get-tuple-element.16), channel_id=1, source_target_pairs={{0,240},{1,33},{8,248},{9,41},{16,1},{17,49},{24,9},{25,57},{32,64... | collective-permute-start | bytes 196616 | tf_op jit(solution)/shard_map/ppermute | solution.py:144
  145.8 0.0 collective-permute-done.3
  145.8 0.8 copy.20
  146.6 0.0 collective-permute-done.10
  146.6 0.0 collective-permute-done.7
  146.6 1.6 %collective-permute-done.8 = bf16[128,256]{1,0:T(8,128)(2,1)S(1)} collective-permute-done((bf16[128,256]{1,0:T(8,128)(2,1)S(1)}, bf16[128,256]{1,0:T(8,128)(2,1)S(1)}, u32[]{:S(2)}, u32[]{:S(2)}) %collective-permute-start.8) | collective-permute-done | bytes 65568 | tf_op jit(solution)/shard_map/ppermute | solution.py:144
  148.2 0.0 collective-permute-done.9
  148.2 0.1 add_convert_fusion.3
  148.3 0.6 slice_bitcast_fusion.3
  (17 shorter events, 0.4 us)
Async XLA Ops:
  0.6 3.2 %copy-start.4 = (f32[1,4,128]{2,1,0:T(4,128)S(1)}, f32[1,4,128]{2,1,0:T(4,128)}, u32[]{:S(2)}) copy-start(f32[1,4,128]{2,1,0:T(4,128)} %param.11) | copy-start | bytes 6148
  0.6 8.6 %copy-start.3 = (bf16[1,128,128]{2,1,0:T(8,128)(2,1)S(1)}, bf16[1,128,128]{2,1,0:T(8,128)(2,1)}, u32[]{:S(2)}) copy-start(bf16[1,128,128]{2,1,0:T(8,128)(2,1)} %param.8) | copy-start | bytes 98308
  0.7 8.6 %copy-start.2 = (bf16[1,128,128]{2,1,0:T(8,128)(2,1)S(1)}, bf16[1,128,128]{2,1,0:T(8,128)(2,1)}, u32[]{:S(2)}) copy-start(bf16[1,128,128]{2,1,0:T(8,128)(2,1)} %param.9) | copy-start | bytes 98308
  3.9 80.1 %collective-permute-start = (bf16[1072,128]{1,0:T(8,128)(2,1)S(1)}, bf16[1072,128]{1,0:T(8,128)(2,1)S(1)}, u32[]{:S(2)}, u32[]{:S(2)}) collective-permute-start(bf16[1072,128]{1,0:T(8,128)(2,1)S(1)} %get-tuple-element.26), channel_id=1, source_target_pairs={{0,8},{1,9},{8,0},{9,1},{16,24},{17,25},{24,16},{25,17},{32,40},{3... | collective-permute-start | bytes 823304 | tf_op jit(solution)/shard_map/ppermute | solution.py:144
  9.3 79.5 %copy-start.1 = (s32[1,64]{1,0:T(1,128)S(1)}, s32[1,64]{1,0:T(1,128)}, u32[]{:S(2)}) copy-start(s32[1,64]{1,0:T(1,128)} %param.13) | copy-start | bytes 772
  84.2 4.6 %collective-permute-start.1 = (bf16[4192,128]{1,0:T(8,128)(2,1)S(1)}, bf16[4192,128]{1,0:T(8,128)(2,1)S(1)}, u32[]{:S(2)}, u32[]{:S(2)}) collective-permute-start(bf16[4192,128]{1,0:T(8,128)(2,1)S(1)} %constant_dynamic-update-slice_fusion.5.mine), channel_id=1, source_target_pairs={{0,1},{1,0},{8,9},{9,8},{16,17},{17,16},{24,25},{25,24},{32,33},{3... | collective-permute-start | bytes 3219464 | tf_op jit(solution)/shard_map/ppermute | solution.py:144
  91.2 11.7 %collective-permute-start.4 = (bf16[2,128,256]{2,1,0:T(8,128)(2,1)S(1)}, bf16[2,128,256]{2,1,0:T(8,128)(2,1)S(1)}, u32[]{:S(2)}, u32[]{:S(2)}) collective-permute-start(bf16[2,128,256]{2,1,0:T(8,128)(2,1)S(1)} %convert_element_type.73), channel_id=1, source_target_pairs={{0,225},{1,32},{8,233},{9,40},{16,241},{17,48},{24,249},{25,56},{3... | collective-permute-start | bytes 393224 | tf_op jit(solution)/shard_map/ppermute | solution.py:144
  99.6 6.7 %copy-start = (f32[4,128,256]{2,1,0:T(8,128)}, f32[4,128,256]{2,1,0:T(8,128)S(1)}, u32[]{:S(2)}) copy-start(f32[4,128,256]{2,1,0:T(8,128)S(1)} %get-tuple-element.13) | copy-start | bytes 1572868
  103.6 10.6 %collective-permute-start.5 = (bf16[2,128,256]{2,1,0:T(8,128)(2,1)}, bf16[2,128,256]{2,1,0:T(8,128)(2,1)}, u32[]{:S(2)}, u32[]{:S(2)}) collective-permute-start(bf16[2,128,256]{2,1,0:T(8,128)(2,1)} %add_convert_fusion.2), channel_id=1, source_target_pairs={{0,225},{1,32},{8,233},{9,40},{16,241},{17,48},{24,249},{25,56},{3... | collective-permute-start | bytes 393224 | tf_op jit(solution)/shard_map/ppermute | solution.py:144
  108.8 12.0 %collective-permute-start.2 = (bf16[2,512,128]{2,1,0:T(8,128)(2,1)S(1)}, bf16[2,512,128]{2,1,0:T(8,128)(2,1)S(1)}, u32[]{:S(2)}, u32[]{:S(2)}) collective-permute-start(bf16[2,512,128]{2,1,0:T(8,128)(2,1)S(1)} %slice.67), channel_id=1, source_target_pairs={{0,1},{1,0},{8,9},{9,8},{16,17},{17,16},{24,25},{25,24},{32,33},{3... | collective-permute-start | bytes 786440 | tf_op jit(solution)/shard_map/ppermute | solution.py:144
  115.1 15.0 %collective-permute-start.6 = (bf16[2,128,256]{2,1,0:T(8,128)(2,1)S(1)}, bf16[2,128,256]{2,1,0:T(8,128)(2,1)S(1)}, u32[]{:S(2)}, u32[]{:S(2)}) collective-permute-start(bf16[2,128,256]{2,1,0:T(8,128)(2,1)S(1)} %add_convert_fusion.1), channel_id=1, source_target_pairs={{0,225},{1,32},{8,233},{9,40},{16,241},{17,48},{24,249},{25,56},{3... | collective-permute-start | bytes 393224 | tf_op jit(solution)/shard_map/ppermute | solution.py:144
  120.9 24.9 %collective-permute-start.3 = (bf16[512,128]{1,0:T(8,128)(2,1)S(1)}, bf16[512,128]{1,0:T(8,128)(2,1)S(1)}, u32[]{:S(2)}, u32[]{:S(2)}) collective-permute-start(bf16[512,128]{1,0:T(8,128)(2,1)S(1)} %fusion.3), channel_id=1, source_target_pairs={{0,8},{1,9},{8,0},{9,1},{16,24},{17,25},{24,16},{25,17},{32,40},{3... | collective-permute-start | bytes 393224 | tf_op jit(solution)/shard_map/ppermute | solution.py:144
  130.2 16.4 %collective-permute-start.10 = (bf16[128,256]{1,0:T(8,128)(2,1)S(1)}, bf16[128,256]{1,0:T(8,128)(2,1)S(1)}, u32[]{:S(2)}, u32[]{:S(2)}) collective-permute-start(bf16[128,256]{1,0:T(8,128)(2,1)S(1)} %get-tuple-element.15), channel_id=1, source_target_pairs={{1,17},{9,25},{17,32},{25,40},{32,48},{40,56},{48,65},{56,73},{65,... | collective-permute-start | bytes 196616 | tf_op jit(solution)/shard_map/ppermute | solution.py:144
  136.3 10.4 %collective-permute-start.7 = (bf16[128,256]{1,0:T(8,128)(2,1)S(1)}, bf16[128,256]{1,0:T(8,128)(2,1)S(1)}, u32[]{:S(2)}, u32[]{:S(2)}) collective-permute-start(bf16[128,256]{1,0:T(8,128)(2,1)S(1)} %get-tuple-element.15), channel_id=1, source_target_pairs={{0,1},{1,16},{8,9},{9,24},{16,17},{17,33},{24,25},{25,41},{32,49},... | collective-permute-start | bytes 196616 | tf_op jit(solution)/shard_map/ppermute | solution.py:144
  138.2 10.0 %collective-permute-start.8 = (bf16[128,256]{1,0:T(8,128)(2,1)S(1)}, bf16[128,256]{1,0:T(8,128)(2,1)S(1)}, u32[]{:S(2)}, u32[]{:S(2)}) collective-permute-start(bf16[128,256]{1,0:T(8,128)(2,1)S(1)} %get-tuple-element.16), channel_id=1, source_target_pairs={{0,241},{1,32},{8,249},{9,40},{16,0},{17,48},{24,8},{25,56},{32,65... | collective-permute-start | bytes 196616 | tf_op jit(solution)/shard_map/ppermute | solution.py:144
  141.7 6.5 %collective-permute-start.9 = (bf16[128,256]{1,0:T(8,128)(2,1)S(1)}, bf16[128,256]{1,0:T(8,128)(2,1)S(1)}, u32[]{:S(2)}, u32[]{:S(2)}) collective-permute-start(bf16[128,256]{1,0:T(8,128)(2,1)S(1)} %get-tuple-element.16), channel_id=1, source_target_pairs={{0,240},{1,33},{8,248},{9,41},{16,1},{17,49},{24,9},{25,57},{32,64... | collective-permute-start | bytes 196616 | tf_op jit(solution)/shard_map/ppermute | solution.py:144

commit v7 on v5

--- a/solution.py
+++ b/solution.py
@@ -26,7 +26,7 @@
 
 def kernel(first, count, heads, toks, order, where, mine, theirs, *refs):
     fresh = first == 0
-    dq, dkv = refs if fresh else refs[1:]
+    dq, *parts = refs if fresh else refs[1:]
     rows = heads * toks
     payload = 2 * rows + 3 * STAT_ROWS
     span_rows = toks // 2
@@ -47,7 +47,7 @@
     else:
         dq[...] = refs[0][...]
 
-    def one_bundle(index, carry):
+    def one_bundle(index):
         ks, vs, positions = [], [], []
         for j in range(BUNDLE):
             turn = first + index * BUNDLE + j
@@ -95,11 +95,11 @@
                 dk = dk + jnp.dot(ds, q, preferred_element_type=jnp.float32)
                 dq[part] += lax.dot_general(ds, k, tn, preferred_element_type=jnp.float32)
         for j in range(BUNDLE):
-            dkv[index * BUNDLE + j, :, :width] = dk[j * toks : (j + 1) * toks]
-            dkv[index * BUNDLE + j, :, width:] = dv[j * toks : (j + 1) * toks]
-        return carry
-
-    lax.fori_loop(0, count // BUNDLE, one_bundle, 0)
+            parts[index * BUNDLE + j][:, :width] = dk[j * toks : (j + 1) * toks]
+            parts[index * BUNDLE + j][:, width:] = dv[j * toks : (j + 1) * toks]
+
+    for index in range(count // BUNDLE):
+        one_bundle(index)
 
 
 def attention_grads(first, count, heads, toks, order, where, mine, theirs, dq):
@@ -112,10 +112,10 @@
         functools.partial(kernel, first, count, heads, toks),
         out_shape=(
             jax.ShapeDtypeStruct((2 * NEAR, rows, width), jnp.float32),
-            jax.ShapeDtypeStruct((count, toks, 2 * width), jnp.float32),
+            *[jax.ShapeDtypeStruct((toks, 2 * width), jnp.float32)] * count,
         ),
         in_specs=[smem, smem] + [vmem] * (len(operands) - 2),
-        out_specs=(vmem, vmem),
+        out_specs=(vmem,) * (1 + count),
         input_output_aliases={} if dq is None else {len(operands) - 1: 0},
         compiler_params=pltpu.CompilerParams(vmem_limit_bytes=16 * 1024 * 1024),
         cost_estimate=pl.CostEstimate(
@@ -177,8 +177,8 @@
     where = jnp.stack([place, core]).astype(jnp.int32)
     dq, parts, first = None, [], 0
     for count in CALLS:
-        dq, part = attention_grads(first, count, heads, toks, order, where, mine, theirs, dq)
-        parts += [part[i : i + BUNDLE] for i in range(0, count, BUNDLE)]
+        dq, *part = attention_grads(first, count, heads, toks, order, where, mine, theirs, dq)
+        parts += part
         first += count
 
     def role_of(z, c):
@@ -199,12 +199,14 @@
     def last_two(z, c):
         return hop(1)(z, c) if role_of(z, c) else None
 
-    total = parts[0].astype(jnp.bfloat16)
-    for part in parts[1:]:
-        total = move(total, hop(BUNDLE))
-        sums = total.astype(jnp.float32) + part
-        total = sums.astype(jnp.bfloat16)
-    total = move(total[0], hop(1)).astype(jnp.float32) + sums[1]
+    totals = [parts[j].astype(jnp.bfloat16) for j in range(BUNDLE)]
+    for turn in range(len(parts) // BUNDLE - 1):
+        moved = [move(totals[j], hop(BUNDLE)) for j in range(BUNDLE)]
+        for j in range(BUNDLE):
+            sums = moved[j].astype(jnp.float32) + parts[(turn + 1) * BUNDLE + j]
+            totals[j] = sums.astype(jnp.bfloat16)
+    sums = lax.optimization_barrier(sums)
+    total = move(totals[0], hop(1)).astype(jnp.float32) + sums
     total = total.astype(jnp.bfloat16)
     one = move(total, last_one)
     two = move(total, last_two)

time: 152 us -> 152 us (level); the launches traced: 149 us -> 152 us
  starting transfers between devices: 38 us -> 48.4 us
  waiting for transfers between devices: 19.8 us -> 12.7 us
    ppermute x10 -> x13, starting transfers between devices: 38 us -> 48.4 us  [move(): return lax.ppermute(array, ('inner', 'head'), pairs)]
    ppermute x10 -> x13, waiting for transfers between devices: 19.8 us -> 12.7 us  [move(): return lax.ppermute(array, ('inner', 'head'), pairs)]
    convert_element_type x3 -> x7, other arithmetic: 1.71 us -> 0.09 us  [the longest x5 0.07 us: body(): totals[j] = sums.astype(jnp.bfloat16)]
  transfers between devices with their start and end apart: 10 -> 13, of which waited for: 6 -> 7; matrix products, arithmetic and copies ran while one was open for 1% -> 1% of each run, Pallas kernels for 5% -> 4%
where the time goes in v7:
time: 152 us
  blocking collectives  74.8 us (49%)
  starting transfers between devices  48.4 us (32%)
  waiting for transfers between devices  12.7 us (8%)
  Pallas kernels  8.86 us (6%)
  local copies, waits for them, and re-layouts  3.6 us (2%)
  other arithmetic  2.2 us (1%)
    all_gather x1, blocking collectives, body(): lax.all_gather(kv, ('inner', 'head'), axis_index_groups=groups, tiled=True)  74.8 us
    ppermute x13, starting transfers between devices, move(): return lax.ppermute(array, ('inner', 'head'), pairs)  48.4 us
    ppermute x13, waiting for transfers between devices, move(): return lax.ppermute(array, ('inner', 'head'), pairs)  12.7 us
    pallas_call x3, Pallas kernels, attention_grads(): pl.pallas_call(functools.partial(kernel, first, count, heads, toks), out_...  8.86 us
  transfers between devices with their start and end apart: 13, of which 7 were waited for; matrix products, arithmetic and copies ran while one was open for 1% of the time, Pallas kernels for 4%

profile of v7, /device:TPU:33, one launch (start us, length us, event | category | flops | bytes accessed | tf_op | source)
XLA Modules:
  0.0 151.6 jit_solution(7641915248563113242)
XLA Ops:
  0.6 0.0 copy-start.1
  0.6 0.0 copy-start.2
  0.7 0.7 multiply_bitcast_fusion
  1.3 1.2 fusion.2
  2.5 0.1 copy.17
  2.6 0.9 copy.15
  3.5 0.9 copy.16
  4.6 5.3 %collective-permute-start = (bf16[1072,128]{1,0:T(8,128)(2,1)S(1)}, bf16[1072,128]{1,0:T(8,128)(2,1)S(1)}, u32[]{:S(2)}, u32[]{:S(2)}) collective-permute-start(bf16[1072,128]{1,0:T(8,128)(2,1)S(1)} %get-tuple-element.34), channel_id=1, source_target_pairs={{0,8},{1,9},{8,0},{9,1},{16,24},{17,25},{24,16},{25,17},{32,40},{3... | collective-permute-start | bytes 823304 | tf_op jit(solution)/shard_map/ppermute | solution.py:144
  9.9 0.0 copy-done.1
  9.9 0.0 copy-done.2
  9.9 0.0 copy-start
  9.9 74.8 %all_gather.3 = bf16[2048,128]{1,0:T(8,128)(2,1)S(1)} all-gather(bf16[128,128]{1,0:T(8,128)(2,1)S(1)} %pad_maximum_fusion), channel_id=1, replica_groups={{0,17,32,49,64,81,96,113,128,145,160,177,192,209,224,241},{1,16,33,48,6..., dimensions={0}, use_global_device_ids=true | all-gather | bytes 557056 | tf_op jit(solution)/shard_map/all_gather | solution.py:172
  84.7 0.0 collective-permute-done
  84.7 0.1 constant_dynamic-update-slice_fusion.5.mine
  84.8 2.0 %collective-permute-start.1 = (bf16[4192,128]{1,0:T(8,128)(2,1)S(1)}, bf16[4192,128]{1,0:T(8,128)(2,1)S(1)}, u32[]{:S(2)}, u32[]{:S(2)}) collective-permute-start(bf16[4192,128]{1,0:T(8,128)(2,1)S(1)} %constant_dynamic-update-slice_fusion.5.mine), channel_id=1, source_target_pairs={{0,1},{1,0},{8,9},{9,8},{16,17},{17,16},{24,25},{25,24},{32,33},{3... | collective-permute-start | bytes 3219464 | tf_op jit(solution)/shard_map/ppermute | solution.py:144
  86.8 0.1 pad_add_fusion.where
  86.9 2.5 %collective-permute-done.1.theirs = bf16[4192,128]{1,0:T(8,128)(2,1)S(1)} collective-permute-done((bf16[4192,128]{1,0:T(8,128)(2,1)S(1)}, bf16[4192,128]{1,0:T(8,128)(2,1)S(1)}, u32[]{:S(2)}, u32[]{:S(2)}) %collective-permute-start.1) | collective-permute-done | bytes 1073184 | tf_op jit(solution)/shard_map/ppermute | solution.py:144
  89.4 0.0 copy-done
  89.4 2.3 %shard_map.94 = (f32[4,512,128]{2,1,0:T(8,128)S(1)}, f32[128,256]{1,0:T(8,128)S(1)}, f32[128,256]{1,0:T(8,128)S(1)}) custom-call(s32[64]{0:T(128)S(1)} %bitcast.40, s32[2]{0:T(128)S(1)} %pad_add_fusion.where, bf16[4192,128]{1,0:T(8,128)(2,1)S(1)} %constant_dynamic-update-slice_fusion.5.mine, bf16[4192,128]{1,0:T(8,128)(2,1)S(1)} %collective-permute-done.1.theirs), custom_call_target="tpu_custom_call" | custom-call | flops 671088640 | bytes 2097152 | tf_op jit(solution)/shard_map/pallas_call | solution.py:111
  91.8 4.1 %collective-permute-start.8 = (bf16[128,256]{1,0:T(8,128)(2,1)S(1)}, bf16[128,256]{1,0:T(8,128)(2,1)S(1)}, u32[]{:S(2)}, u32[]{:S(2)}) collective-permute-start(bf16[128,256]{1,0:T(8,128)(2,1)S(1)} %convert_element_type.99), channel_id=1, source_target_pairs={{0,225},{1,32},{8,233},{9,40},{16,241},{17,48},{24,249},{25,56},{3... | collective-permute-start | bytes 196616 | tf_op jit(solution)/shard_map/ppermute | solution.py:144
  96.0 4.0 %collective-permute-start.4 = (bf16[128,256]{1,0:T(8,128)(2,1)S(1)}, bf16[128,256]{1,0:T(8,128)(2,1)S(1)}, u32[]{:S(2)}, u32[]{:S(2)}) collective-permute-start(bf16[128,256]{1,0:T(8,128)(2,1)S(1)} %convert_element_type.91), channel_id=1, source_target_pairs={{0,225},{1,32},{8,233},{9,40},{16,241},{17,48},{24,249},{25,56},{3... | collective-permute-start | bytes 196616 | tf_op jit(solution)/shard_map/ppermute | solution.py:144
  99.9 4.1 %shard_map.95 = (f32[4,512,128]{2,1,0:T(8,128)S(1)}, f32[128,256]{1,0:T(8,128)S(1)}, f32[128,256]{1,0:T(8,128)S(1)}, f32[128,256]{1,0:T(8,128)S(1)}, f32[128,256]{1,0:T(8,128)S(1)}) custom-call(s32[64]{0:T(128)S(1)} %bitcast.41, s32[2]{0:T(128)S(1)} %pad_add_fusion.where, ...), custom_call_target="tpu_custom_call", output_to_operand_aliasing={{0}: (4, {})} | custom-call | flops 1342177280 | bytes 2097152 | tf_op jit(solution)/shard_map/pallas_call | solution.py:111
  104.0 2.4 %shard_map.96 = (f32[4,512,128]{2,1,0:T(8,128)S(1)}, f32[128,256]{1,0:T(8,128)S(1)}, f32[128,256]{1,0:T(8,128)S(1)}) custom-call(s32[64]{0:T(128)S(1)} %bitcast.42, s32[2]{0:T(128)S(1)} %pad_add_fusion.where, bf16[4192,128]{1,0:T(8,128)(2,1)S(1)} %constant_dynamic-update-slice_fusion.5.mine, ...), custom_call_target="tpu_custom_call", output_to_operand_aliasing={{0}: (4, {})} | custom-call | flops 671088640 | bytes 2097152 | tf_op jit(solution)/shard_map/pallas_call | solution.py:111
  106.5 3.6 %collective-permute-start.2 = (bf16[2,512,128]{2,1,0:T(8,128)(2,1)S(1)}, bf16[2,512,128]{2,1,0:T(8,128)(2,1)S(1)}, u32[]{:S(2)}, u32[]{:S(2)}) collective-permute-start(bf16[2,512,128]{2,1,0:T(8,128)(2,1)S(1)} %slice.43), channel_id=1, source_target_pairs={{0,1},{1,0},{8,9},{9,8},{16,17},{17,16},{24,25},{25,24},{32,33},{3... | collective-permute-start | bytes 786440 | tf_op jit(solution)/shard_map/ppermute | solution.py:144
  110.1 0.0 collective-permute-done.4
  110.2 4.3 %collective-permute-start.5 = (bf16[128,256]{1,0:T(8,128)(2,1)S(1)}, bf16[128,256]{1,0:T(8,128)(2,1)S(1)}, u32[]{:S(2)}, u32[]{:S(2)}) collective-permute-start(bf16[128,256]{1,0:T(8,128)(2,1)S(1)} %add_convert_fusion.6), channel_id=1, source_target_pairs={{0,225},{1,32},{8,233},{9,40},{16,241},{17,48},{24,249},{25,56},{3... | collective-permute-start | bytes 196616 | tf_op jit(solution)/shard_map/ppermute | solution.py:144
  114.5 0.0 collective-permute-done.8
  114.5 5.1 %collective-permute-start.9 = (bf16[128,256]{1,0:T(8,128)(2,1)S(1)}, bf16[128,256]{1,0:T(8,128)(2,1)S(1)}, u32[]{:S(2)}, u32[]{:S(2)}) collective-permute-start(bf16[128,256]{1,0:T(8,128)(2,1)S(1)} %add_convert_fusion.3), channel_id=1, source_target_pairs={{0,225},{1,32},{8,233},{9,40},{16,241},{17,48},{24,249},{25,56},{3... | collective-permute-start | bytes 196616 | tf_op jit(solution)/shard_map/ppermute | solution.py:144
  119.6 0.7 collective-permute-done.5
  120.4 3.8 %collective-permute-start.6 = (bf16[128,256]{1,0:T(8,128)(2,1)S(1)}, bf16[128,256]{1,0:T(8,128)(2,1)S(1)}, u32[]{:S(2)}, u32[]{:S(2)}) collective-permute-start(bf16[128,256]{1,0:T(8,128)(2,1)S(1)} %add_convert_fusion.5), channel_id=1, source_target_pairs={{0,225},{1,32},{8,233},{9,40},{16,241},{17,48},{24,249},{25,56},{3... | collective-permute-start | bytes 196616 | tf_op jit(solution)/shard_map/ppermute | solution.py:144
  124.2 1.3 collective-permute-done.9
  125.5 3.7 %collective-permute-start.10 = (bf16[128,256]{1,0:T(8,128)(2,1)S(1)}, bf16[128,256]{1,0:T(8,128)(2,1)S(1)}, u32[]{:S(2)}, u32[]{:S(2)}) collective-permute-start(bf16[128,256]{1,0:T(8,128)(2,1)S(1)} %add_convert_fusion.2), channel_id=1, source_target_pairs={{0,225},{1,32},{8,233},{9,40},{16,241},{17,48},{24,249},{25,56},{3... | collective-permute-start | bytes 196616 | tf_op jit(solution)/shard_map/ppermute | solution.py:144
  129.2 1.7 %collective-permute-done.6 = bf16[128,256]{1,0:T(8,128)(2,1)S(1)} collective-permute-done((bf16[128,256]{1,0:T(8,128)(2,1)S(1)}, bf16[128,256]{1,0:T(8,128)(2,1)S(1)}, u32[]{:S(2)}, u32[]{:S(2)}) %collective-permute-start.6) | collective-permute-done | bytes 65568 | tf_op jit(solution)/shard_map/ppermute | solution.py:144
  131.0 4.9 %collective-permute-start.7 = (bf16[128,256]{1,0:T(8,128)(2,1)S(1)}, bf16[128,256]{1,0:T(8,128)(2,1)S(1)}, u32[]{:S(2)}, u32[]{:S(2)}) collective-permute-start(bf16[128,256]{1,0:T(8,128)(2,1)S(1)} %add_convert_fusion.4), channel_id=1, source_target_pairs={{0,241},{1,17},{8,249},{9,25},{16,0},{17,32},{24,8},{25,40},{32,48... | collective-permute-start | bytes 196616 | tf_op jit(solution)/shard_map/ppermute | solution.py:144
  135.9 0.0 collective-permute-done.10
  135.9 0.0 collective-permute-done.2
  136.0 2.8 %collective-permute-done.7 = bf16[128,256]{1,0:T(8,128)(2,1)S(1)} collective-permute-done((bf16[128,256]{1,0:T(8,128)(2,1)S(1)}, bf16[128,256]{1,0:T(8,128)(2,1)S(1)}, u32[]{:S(2)}, u32[]{:S(2)}) %collective-permute-start.7) | collective-permute-done | bytes 65568 | tf_op jit(solution)/shard_map/ppermute | solution.py:144
  138.8 3.5 %collective-permute-start.12 = (bf16[128,256]{1,0:T(8,128)(2,1)S(1)}, bf16[128,256]{1,0:T(8,128)(2,1)S(1)}, u32[]{:S(2)}, u32[]{:S(2)}) collective-permute-start(bf16[128,256]{1,0:T(8,128)(2,1)S(1)} %add_convert_fusion.1), channel_id=1, source_target_pairs={{1,17},{9,25},{17,32},{25,40},{32,48},{40,56},{48,65},{56,73},{65,... | collective-permute-start | bytes 196616 | tf_op jit(solution)/shard_map/ppermute | solution.py:144
  142.3 2.0 %collective-permute-start.11 = (bf16[128,256]{1,0:T(8,128)(2,1)S(1)}, bf16[128,256]{1,0:T(8,128)(2,1)S(1)}, u32[]{:S(2)}, u32[]{:S(2)}) collective-permute-start(bf16[128,256]{1,0:T(8,128)(2,1)S(1)} %add_convert_fusion.1), channel_id=1, source_target_pairs={{0,1},{1,16},{8,9},{9,24},{16,17},{17,33},{24,25},{25,41},{32,49},... | collective-permute-start | bytes 196616 | tf_op jit(solution)/shard_map/ppermute | solution.py:144
  144.3 2.2 %collective-permute-start.3 = (bf16[512,128]{1,0:T(8,128)(2,1)S(1)}, bf16[512,128]{1,0:T(8,128)(2,1)S(1)}, u32[]{:S(2)}, u32[]{:S(2)}) collective-permute-start(bf16[512,128]{1,0:T(8,128)(2,1)S(1)} %fusion.3), channel_id=1, source_target_pairs={{0,8},{1,9},{8,0},{9,1},{16,24},{17,25},{24,16},{25,17},{32,40},{3... | collective-permute-start | bytes 393224 | tf_op jit(solution)/shard_map/ppermute | solution.py:144
  146.5 0.1 collective-permute-done.12
  146.6 0.0 collective-permute-done.11
  146.7 0.6 slice_bitcast_fusion.1
  147.3 3.5 %collective-permute-done.3 = bf16[512,128]{1,0:T(8,128)(2,1)S(1)} collective-permute-done((bf16[512,128]{1,0:T(8,128)(2,1)S(1)}, bf16[512,128]{1,0:T(8,128)(2,1)S(1)}, u32[]{:S(2)}, u32[]{:S(2)}) %collective-permute-start.3) | collective-permute-done | bytes 131104 | tf_op jit(solution)/shard_map/ppermute | solution.py:144
  150.8 0.8 copy.20
  (23 shorter events, 0.4 us)
Async XLA Ops:
  0.6 9.2 %copy-start.1 = (bf16[1,128,128]{2,1,0:T(8,128)(2,1)S(1)}, bf16[1,128,128]{2,1,0:T(8,128)(2,1)}, u32[]{:S(2)}) copy-start(bf16[1,128,128]{2,1,0:T(8,128)(2,1)} %param.9) | copy-start | bytes 98308
  0.6 9.2 %copy-start.2 = (bf16[1,128,128]{2,1,0:T(8,128)(2,1)S(1)}, bf16[1,128,128]{2,1,0:T(8,128)(2,1)}, u32[]{:S(2)}) copy-start(bf16[1,128,128]{2,1,0:T(8,128)(2,1)} %param.8) | copy-start | bytes 98308
  4.6 80.1 %collective-permute-start = (bf16[1072,128]{1,0:T(8,128)(2,1)S(1)}, bf16[1072,128]{1,0:T(8,128)(2,1)S(1)}, u32[]{:S(2)}, u32[]{:S(2)}) collective-permute-start(bf16[1072,128]{1,0:T(8,128)(2,1)S(1)} %get-tuple-element.34), channel_id=1, source_target_pairs={{0,8},{1,9},{8,0},{9,1},{16,24},{17,25},{24,16},{25,17},{32,40},{3... | collective-permute-start | bytes 823304 | tf_op jit(solution)/shard_map/ppermute | solution.py:144
  9.9 79.5 %copy-start = (s32[1,64]{1,0:T(1,128)S(1)}, s32[1,64]{1,0:T(1,128)}, u32[]{:S(2)}) copy-start(s32[1,64]{1,0:T(1,128)} %param.13) | copy-start | bytes 772
  84.8 4.6 %collective-permute-start.1 = (bf16[4192,128]{1,0:T(8,128)(2,1)S(1)}, bf16[4192,128]{1,0:T(8,128)(2,1)S(1)}, u32[]{:S(2)}, u32[]{:S(2)}) collective-permute-start(bf16[4192,128]{1,0:T(8,128)(2,1)S(1)} %constant_dynamic-update-slice_fusion.5.mine), channel_id=1, source_target_pairs={{0,1},{1,0},{8,9},{9,8},{16,17},{17,16},{24,25},{25,24},{32,33},{3... | collective-permute-start | bytes 3219464 | tf_op jit(solution)/shard_map/ppermute | solution.py:144
  91.8 22.7 %collective-permute-start.8 = (bf16[128,256]{1,0:T(8,128)(2,1)S(1)}, bf16[128,256]{1,0:T(8,128)(2,1)S(1)}, u32[]{:S(2)}, u32[]{:S(2)}) collective-permute-start(bf16[128,256]{1,0:T(8,128)(2,1)S(1)} %convert_element_type.99), channel_id=1, source_target_pairs={{0,225},{1,32},{8,233},{9,40},{16,241},{17,48},{24,249},{25,56},{3... | collective-permute-start | bytes 196616 | tf_op jit(solution)/shard_map/ppermute | solution.py:144
  96.0 14.2 %collective-permute-start.4 = (bf16[128,256]{1,0:T(8,128)(2,1)S(1)}, bf16[128,256]{1,0:T(8,128)(2,1)S(1)}, u32[]{:S(2)}, u32[]{:S(2)}) collective-permute-start(bf16[128,256]{1,0:T(8,128)(2,1)S(1)} %convert_element_type.91), channel_id=1, source_target_pairs={{0,225},{1,32},{8,233},{9,40},{16,241},{17,48},{24,249},{25,56},{3... | collective-permute-start | bytes 196616 | tf_op jit(solution)/shard_map/ppermute | solution.py:144
  106.5 29.5 %collective-permute-start.2 = (bf16[2,512,128]{2,1,0:T(8,128)(2,1)S(1)}, bf16[2,512,128]{2,1,0:T(8,128)(2,1)S(1)}, u32[]{:S(2)}, u32[]{:S(2)}) collective-permute-start(bf16[2,512,128]{2,1,0:T(8,128)(2,1)S(1)} %slice.43), channel_id=1, source_target_pairs={{0,1},{1,0},{8,9},{9,8},{16,17},{17,16},{24,25},{25,24},{32,33},{3... | collective-permute-start | bytes 786440 | tf_op jit(solution)/shard_map/ppermute | solution.py:144
  110.2 10.2 %collective-permute-start.5 = (bf16[128,256]{1,0:T(8,128)(2,1)S(1)}, bf16[128,256]{1,0:T(8,128)(2,1)S(1)}, u32[]{:S(2)}, u32[]{:S(2)}) collective-permute-start(bf16[128,256]{1,0:T(8,128)(2,1)S(1)} %add_convert_fusion.6), channel_id=1, source_target_pairs={{0,225},{1,32},{8,233},{9,40},{16,241},{17,48},{24,249},{25,56},{3... | collective-permute-start | bytes 196616 | tf_op jit(solution)/shard_map/ppermute | solution.py:144
  114.5 11.0 %collective-permute-start.9 = (bf16[128,256]{1,0:T(8,128)(2,1)S(1)}, bf16[128,256]{1,0:T(8,128)(2,1)S(1)}, u32[]{:S(2)}, u32[]{:S(2)}) collective-permute-start(bf16[128,256]{1,0:T(8,128)(2,1)S(1)} %add_convert_fusion.3), channel_id=1, source_target_pairs={{0,225},{1,32},{8,233},{9,40},{16,241},{17,48},{24,249},{25,56},{3... | collective-permute-start | bytes 196616 | tf_op jit(solution)/shard_map/ppermute | solution.py:144
  120.4 10.6 %collective-permute-start.6 = (bf16[128,256]{1,0:T(8,128)(2,1)S(1)}, bf16[128,256]{1,0:T(8,128)(2,1)S(1)}, u32[]{:S(2)}, u32[]{:S(2)}) collective-permute-start(bf16[128,256]{1,0:T(8,128)(2,1)S(1)} %add_convert_fusion.5), channel_id=1, source_target_pairs={{0,225},{1,32},{8,233},{9,40},{16,241},{17,48},{24,249},{25,56},{3... | collective-permute-start | bytes 196616 | tf_op jit(solution)/shard_map/ppermute | solution.py:144
  125.5 10.4 %collective-permute-start.10 = (bf16[128,256]{1,0:T(8,128)(2,1)S(1)}, bf16[128,256]{1,0:T(8,128)(2,1)S(1)}, u32[]{:S(2)}, u32[]{:S(2)}) collective-permute-start(bf16[128,256]{1,0:T(8,128)(2,1)S(1)} %add_convert_fusion.2), channel_id=1, source_target_pairs={{0,225},{1,32},{8,233},{9,40},{16,241},{17,48},{24,249},{25,56},{3... | collective-permute-start | bytes 196616 | tf_op jit(solution)/shard_map/ppermute | solution.py:144
  131.0 7.8 %collective-permute-start.7 = (bf16[128,256]{1,0:T(8,128)(2,1)S(1)}, bf16[128,256]{1,0:T(8,128)(2,1)S(1)}, u32[]{:S(2)}, u32[]{:S(2)}) collective-permute-start(bf16[128,256]{1,0:T(8,128)(2,1)S(1)} %add_convert_fusion.4), channel_id=1, source_target_pairs={{0,241},{1,17},{8,249},{9,25},{16,0},{17,32},{24,8},{25,40},{32,48... | collective-permute-start | bytes 196616 | tf_op jit(solution)/shard_map/ppermute | solution.py:144
  138.8 7.8 %collective-permute-start.12 = (bf16[128,256]{1,0:T(8,128)(2,1)S(1)}, bf16[128,256]{1,0:T(8,128)(2,1)S(1)}, u32[]{:S(2)}, u32[]{:S(2)}) collective-permute-start(bf16[128,256]{1,0:T(8,128)(2,1)S(1)} %add_convert_fusion.1), channel_id=1, source_target_pairs={{1,17},{9,25},{17,32},{25,40},{32,48},{40,56},{48,65},{56,73},{65,... | collective-permute-start | bytes 196616 | tf_op jit(solution)/shard_map/ppermute | solution.py:144
  142.3 4.3 %collective-permute-start.11 = (bf16[128,256]{1,0:T(8,128)(2,1)S(1)}, bf16[128,256]{1,0:T(8,128)(2,1)S(1)}, u32[]{:S(2)}, u32[]{:S(2)}) collective-permute-start(bf16[128,256]{1,0:T(8,128)(2,1)S(1)} %add_convert_fusion.1), channel_id=1, source_target_pairs={{0,1},{1,16},{8,9},{9,24},{16,17},{17,33},{24,25},{25,41},{32,49},... | collective-permute-start | bytes 196616 | tf_op jit(solution)/shard_map/ppermute | solution.py:144
  144.3 6.5 %collective-permute-start.3 = (bf16[512,128]{1,0:T(8,128)(2,1)S(1)}, bf16[512,128]{1,0:T(8,128)(2,1)S(1)}, u32[]{:S(2)}, u32[]{:S(2)}) collective-permute-start(bf16[512,128]{1,0:T(8,128)(2,1)S(1)} %fusion.3), channel_id=1, source_target_pairs={{0,8},{1,9},{8,0},{9,1},{16,24},{17,25},{24,16},{25,17},{32,40},{3... | collective-permute-start | bytes 393224 | tf_op jit(solution)/shard_map/ppermute | solution.py:144

commit v8 on v5

--- a/solution.py
+++ b/solution.py
@@ -16,12 +16,50 @@
 STAT_ROWS = 16
 
 
-def split_stats(stats):
-    high = lax.reduce_precision(stats, 8, 7)
-    middle = lax.reduce_precision(stats - high, 8, 7)
-    low = stats - high - middle
-    pad = ((0, STAT_ROWS - stats.shape[0]), (0, 0))
-    return [jnp.pad(a, pad).astype(jnp.bfloat16) for a in (high, middle, low)]
+def rows_kernel(*refs):
+    sources, payload, held, sems = refs[:4], refs[4], refs[5:9], refs[9]
+    copies = [
+        pltpu.make_async_copy(source, target, sems.at[i])
+        for i, (source, target) in enumerate(zip(sources, held))
+    ]
+    for copy in copies:
+        copy.start()
+    for copy in copies:
+        copy.wait()
+    queries, d_out, out, log_total = held
+    toks, heads, width = queries.shape
+    rows = heads * toks
+    deltas = []
+    for h in range(heads):
+        grad = d_out[:, h, :]
+        payload[h * toks : (h + 1) * toks] = queries[:, h, :]
+        payload[rows + h * toks : rows + (h + 1) * toks] = grad
+        product = out[:, h, :].astype(jnp.float32) * grad.astype(jnp.float32)
+        deltas.append(jnp.sum(product.T, axis=0, keepdims=True))
+    rest = jnp.concatenate([log_total[...] * LOG2E, *deltas])
+    rest = jnp.concatenate([rest, jnp.zeros((STAT_ROWS - 2 * heads, width), jnp.float32)])
+    for i in range(3):
+        term = rest.astype(jnp.bfloat16)
+        payload[2 * rows + i * STAT_ROWS : 2 * rows + (i + 1) * STAT_ROWS] = term
+        rest = rest - term.astype(jnp.float32)
+
+
+def own_rows(*arrays):
+    toks, heads, width = arrays[0].shape
+    return pl.pallas_call(
+        rows_kernel,
+        out_shape=jax.ShapeDtypeStruct((2 * heads * toks + 3 * STAT_ROWS, width), jnp.bfloat16),
+        in_specs=[pl.BlockSpec(memory_space=pltpu.HBM)] * len(arrays),
+        out_specs=pl.BlockSpec(memory_space=pltpu.VMEM),
+        scratch_shapes=[pltpu.VMEM(a.shape, a.dtype) for a in arrays]
+        + [pltpu.SemaphoreType.DMA((len(arrays),))],
+        compiler_params=pltpu.CompilerParams(vmem_limit_bytes=63 * 1024 * 1024),
+        cost_estimate=pl.CostEstimate(
+            flops=4 * heads * toks * width,
+            bytes_accessed=10 * heads * toks * width,
+            transcendentals=0,
+        ),
+    )(*arrays)
 
 
 def kernel(first, count, heads, toks, order, where, mine, theirs, *refs):
@@ -42,12 +80,8 @@
     key_row, token_row = row % span_rows, token % span_rows
     nt = (((1,), (1,)), ((), ()))
     tn = (((0,), (0,)), ((), ()))
-    if fresh:
-        dq[...] = jnp.zeros_like(dq)
-    else:
-        dq[...] = refs[0][...]
-
-    def one_bundle(index, carry):
+
+    def one_bundle(index):
         ks, vs, positions = [], [], []
         for j in range(BUNDLE):
             turn = first + index * BUNDLE + j
@@ -93,13 +127,18 @@
                 ds = jnp.concatenate(grads, axis=1)
                 dv = dv + jnp.dot(p, d, preferred_element_type=jnp.float32)
                 dk = dk + jnp.dot(ds, q, preferred_element_type=jnp.float32)
-                dq[part] += lax.dot_general(ds, k, tn, preferred_element_type=jnp.float32)
+                dq_part = lax.dot_general(ds, k, tn, preferred_element_type=jnp.float32)
+                if index > 0:
+                    dq_part += dq[part]
+                elif not fresh:
+                    dq_part += refs[0][part]
+                dq[part] = dq_part
         for j in range(BUNDLE):
             dkv[index * BUNDLE + j, :, :width] = dk[j * toks : (j + 1) * toks]
             dkv[index * BUNDLE + j, :, width:] = dv[j * toks : (j + 1) * toks]
-        return carry
-
-    lax.fori_loop(0, count // BUNDLE, one_bundle, 0)
+
+    for index in range(count // BUNDLE):
+        one_bundle(index)
 
 
 def attention_grads(first, count, heads, toks, order, where, mine, theirs, dq):
@@ -132,7 +171,6 @@
     core = lax.axis_index("head")
     toks, heads, width = queries.shape[1:]
     half = toks // 2
-    rows = heads * toks
 
     def move(array, target):
         pairs = []
@@ -149,16 +187,7 @@
     def near(distance):
         return lambda z, c: (z ^ distance, c)
 
-    delta = jnp.transpose(
-        jnp.sum(out[0].astype(jnp.float32) * d_out[0].astype(jnp.float32), axis=-1)
-    )
-    payload = jnp.concatenate(
-        [
-            jnp.transpose(queries[0], (1, 0, 2)).reshape(rows, width),
-            jnp.transpose(d_out[0], (1, 0, 2)).reshape(rows, width),
-            *split_stats(jnp.concatenate([log_total[0] * LOG2E, delta])),
-        ]
-    )
+    payload = own_rows(queries[0], d_out[0], out[0], log_total[0])
     payloads = [payload] + [move(payload, near(i)) for i in range(1, NEAR)]
 
     kv = jnp.concatenate(

time: 152 us -> 149 us (0.980)
  waiting for transfers between devices: 19.8 us -> 16.1 us
  Pallas kernels: 9.15 us -> 11.8 us
    ppermute x10, waiting for transfers between devices: 19.8 us -> 16.1 us  [move(): return lax.ppermute(array, ('inner', 'head'), pairs)]
    pallas_call x0 -> x1, Pallas kernels: none -> 2.97 us  [own_rows(): pl.pallas_call(rows_kernel, out_shape=jax.ShapeDtypeStruct((2 * heads * t...]
    transpose x2 -> x0, local copies, waits for them, and re-layouts: 1.87 us -> none  [the longest x1 0.94 us: body(): jnp.transpose(queries[0], (1, 0, 2)).reshape(rows, width)]
  transfers between devices with their start and end apart: 10 -> 10, of which waited for: 6 -> 5; matrix products, arithmetic and copies ran while one was open for 1% -> 2% of each run, Pallas kernels for 5% -> 4%
where the time goes in v8:
time: 149 us; the launch traced here: 148 us
  blocking collectives  74.5 us (50%)
  starting transfers between devices  39.4 us (26%)
  waiting for transfers between devices  16.1 us (11%)
  Pallas kernels  11.8 us (8%)
  other arithmetic  2.99 us (2%)
  local copies, waits for them, and re-layouts  2.2 us (1%)
    all_gather x1, blocking collectives, body(): lax.all_gather(kv, ('inner', 'head'), axis_index_groups=groups, tiled=True)  74.5 us
    ppermute x10, starting transfers between devices, move(): return lax.ppermute(array, ('inner', 'head'), pairs)  39.4 us
    ppermute x10, waiting for transfers between devices, move(): return lax.ppermute(array, ('inner', 'head'), pairs)  16.1 us
    pallas_call x3, Pallas kernels, attention_grads(): pl.pallas_call(functools.partial(kernel, first, count, heads, toks), out_...  8.85 us
  transfers between devices with their start and end apart: 10, of which 5 were waited for; matrix products, arithmetic and copies ran while one was open for 2% of the time, Pallas kernels for 4%

profile of v8, /device:TPU:33, one launch (start us, length us, event | category | flops | bytes accessed | tf_op | source)
XLA Modules:
  0.0 148.0 jit_solution(6633699799728896382)
XLA Ops:
  0.6 3.0 %shard_map.94 = bf16[1072,128]{1,0:T(8,128)(2,1)} custom-call(bf16[128,4,128]{2,1,0:T(4,128)(2,1)} %bitcast.42, bf16[128,4,128]{2,1,0:T(4,128)(2,1)} %bitcast.43, bf16[128,4,128]{2,1,0:T(4,128)(2,1)} %bitcast.44, f32[4,128]{1,0:T(4,128)} %bitcast.45), custom_call_target="tpu_custom_call" | custom-call | flops 262144 | bytes 655360 | tf_op jit(solution)/shard_map/pallas_call | solution.py:49
  3.6 5.3 %collective-permute-start = (bf16[1072,128]{1,0:T(8,128)(2,1)}, bf16[1072,128]{1,0:T(8,128)(2,1)S(1)}, u32[]{:S(2)}, u32[]{:S(2)}) collective-permute-start(bf16[1072,128]{1,0:T(8,128)(2,1)} %shard_map.94), channel_id=1, source_target_pairs={{0,8},{1,9},{8,0},{9,1},{16,24},{17,25},{24,16},{25,17},{32,40},{3... | collective-permute-start | bytes 823304 | tf_op jit(solution)/shard_map/ppermute | solution.py:182
  8.9 0.7 dynamic-slice_bitcast_fusion
  9.6 74.5 %all_gather.3 = bf16[2048,128]{1,0:T(8,128)(2,1)S(1)} all-gather(bf16[128,128]{1,0:T(8,128)(2,1)S(1)} %pad_maximum_fusion.1), channel_id=1, replica_groups={{0,17,32,49,64,81,96,113,128,145,160,177,192,209,224,241},{1,16,33,48,6..., dimensions={0}, use_global_device_ids=true | all-gather | bytes 557056 | tf_op jit(solution)/shard_map/all_gather | solution.py:201
  84.2 0.0 copy-start.1
  84.2 0.0 collective-permute-done
  84.2 1.0 pad_maximum_fusion.mine
  85.2 2.0 %collective-permute-start.1 = (bf16[4192,128]{1,0:T(8,128)(2,1)S(1)}, bf16[4192,128]{1,0:T(8,128)(2,1)S(1)}, u32[]{:S(2)}, u32[]{:S(2)}) collective-permute-start(bf16[4192,128]{1,0:T(8,128)(2,1)S(1)} %pad_maximum_fusion.mine), channel_id=1, source_target_pairs={{0,1},{1,0},{8,9},{9,8},{16,17},{17,16},{24,25},{25,24},{32,33},{3... | collective-permute-start | bytes 3219464 | tf_op jit(solution)/shard_map/ppermute | solution.py:182
  87.3 0.1 pad_add_fusion.where
  87.3 2.5 %collective-permute-done.1.theirs = bf16[4192,128]{1,0:T(8,128)(2,1)S(1)} collective-permute-done((bf16[4192,128]{1,0:T(8,128)(2,1)S(1)}, bf16[4192,128]{1,0:T(8,128)(2,1)S(1)}, u32[]{:S(2)}, u32[]{:S(2)}) %collective-permute-start.1) | collective-permute-done | bytes 1073184 | tf_op jit(solution)/shard_map/ppermute | solution.py:182
  89.8 0.0 copy-done.1
  89.8 2.3 %shard_map.95 = (f32[4,512,128]{2,1,0:T(8,128)S(1)}, f32[2,128,256]{2,1,0:T(8,128)S(1)}) custom-call(s32[64]{0:T(128)S(1)} %bitcast.37, s32[2]{0:T(128)S(1)} %pad_add_fusion.where, bf16[4192,128]{1,0:T(8,128)(2,1)S(1)} %pad_maximum_fusion.mine, bf16[4192,128]{1,0:T(8,128)(2,1)S(1)} %collective-permute-done.1.theirs), custom_call_target="tpu_custom_call" | custom-call | flops 671088640 | bytes 2097152 | tf_op jit(solution)/shard_map/pallas_call | solution.py:150
  92.2 4.0 %collective-permute-start.4 = (bf16[2,128,256]{2,1,0:T(8,128)(2,1)S(1)}, bf16[2,128,256]{2,1,0:T(8,128)(2,1)S(1)}, u32[]{:S(2)}, u32[]{:S(2)}) collective-permute-start(bf16[2,128,256]{2,1,0:T(8,128)(2,1)S(1)} %convert_element_type.54), channel_id=1, source_target_pairs={{0,225},{1,32},{8,233},{9,40},{16,241},{17,48},{24,249},{25,56},{3... | collective-permute-start | bytes 393224 | tf_op jit(solution)/shard_map/ppermute | solution.py:182
  96.2 4.1 %shard_map.96 = (f32[4,512,128]{2,1,0:T(8,128)S(1)}, f32[4,128,256]{2,1,0:T(8,128)S(1)}) custom-call(s32[64]{0:T(128)S(1)} %bitcast.38, s32[2]{0:T(128)S(1)} %pad_add_fusion.where, bf16[4192,128]{1,0:T(8,128)(2,1)S(1)} %pad_maximum_fusion.mine, bf16[4192,128]{1,0:T(8,128)(2,1)S(1)} %collective-permute-done.1.theirs, ...), custom_call_target="tpu_custom_call", output_to_operand_aliasing={{0}: (4, {})} | custom-call | flops 1342177280 | bytes 2097152 | tf_op jit(solution)/shard_map/pallas_call | solution.py:150
  100.2 0.0 copy-start
  100.3 3.8 %collective-permute-done.4 = bf16[2,128,256]{2,1,0:T(8,128)(2,1)S(1)} collective-permute-done((bf16[2,128,256]{2,1,0:T(8,128)(2,1)S(1)}, bf16[2,128,256]{2,1,0:T(8,128)(2,1)S(1)}, u32[]{:S(2)}, u32[]{:S(2)}) %collective-permute-start.4) | collective-permute-done | bytes 131104 | tf_op jit(solution)/shard_map/ppermute | solution.py:182
  104.1 0.7 add_convert_fusion.1
  104.8 3.9 %collective-permute-start.5 = (bf16[2,128,256]{2,1,0:T(8,128)(2,1)}, bf16[2,128,256]{2,1,0:T(8,128)(2,1)}, u32[]{:S(2)}, u32[]{:S(2)}) collective-permute-start(bf16[2,128,256]{2,1,0:T(8,128)(2,1)} %add_convert_fusion.1), channel_id=1, source_target_pairs={{0,225},{1,32},{8,233},{9,40},{16,241},{17,48},{24,249},{25,56},{3... | collective-permute-start | bytes 393224 | tf_op jit(solution)/shard_map/ppermute | solution.py:182
  108.7 2.4 %shard_map.97 = (f32[4,512,128]{2,1,0:T(8,128)S(1)}, f32[2,128,256]{2,1,0:T(8,128)S(1)}) custom-call(s32[64]{0:T(128)S(1)} %bitcast.39, s32[2]{0:T(128)S(1)} %pad_add_fusion.where, bf16[4192,128]{1,0:T(8,128)(2,1)S(1)} %pad_maximum_fusion.mine, bf16[4192,128]{1,0:T(8,128)(2,1)S(1)} %collective-permute-done.1.theirs, ...), custom_call_target="tpu_custom_call", output_to_operand_aliasing={{0}: (4, {})} | custom-call | flops 671088640 | bytes 2097152 | tf_op jit(solution)/shard_map/pallas_call | solution.py:150
  111.1 0.0 copy-done
  111.2 5.1 %collective-permute-start.2 = (bf16[2,512,128]{2,1,0:T(8,128)(2,1)S(1)}, bf16[2,512,128]{2,1,0:T(8,128)(2,1)S(1)}, u32[]{:S(2)}, u32[]{:S(2)}) collective-permute-start(bf16[2,512,128]{2,1,0:T(8,128)(2,1)S(1)} %slice.71), channel_id=1, source_target_pairs={{0,1},{1,0},{8,9},{9,8},{16,17},{17,16},{24,25},{25,24},{32,33},{3... | collective-permute-start | bytes 786440 | tf_op jit(solution)/shard_map/ppermute | solution.py:182
  116.4 0.0 collective-permute-done.5
  116.4 1.0 add_convert_fusion
  117.4 4.4 %collective-permute-start.6 = (bf16[2,128,256]{2,1,0:T(8,128)(2,1)S(1)}, bf16[2,128,256]{2,1,0:T(8,128)(2,1)S(1)}, u32[]{:S(2)}, u32[]{:S(2)}) collective-permute-start(bf16[2,128,256]{2,1,0:T(8,128)(2,1)S(1)} %add_convert_fusion), channel_id=1, source_target_pairs={{0,225},{1,32},{8,233},{9,40},{16,241},{17,48},{24,249},{25,56},{3... | collective-permute-start | bytes 393224 | tf_op jit(solution)/shard_map/ppermute | solution.py:182
  121.8 0.0 collective-permute-done.2
  121.9 5.8 %collective-permute-done.6 = bf16[2,128,256]{2,1,0:T(8,128)(2,1)S(1)} collective-permute-done((bf16[2,128,256]{2,1,0:T(8,128)(2,1)S(1)}, bf16[2,128,256]{2,1,0:T(8,128)(2,1)S(1)}, u32[]{:S(2)}, u32[]{:S(2)}) %collective-permute-start.6) | collective-permute-done | bytes 131104 | tf_op jit(solution)/shard_map/ppermute | solution.py:182
  127.8 6.7 %collective-permute-start.7 = (bf16[128,256]{1,0:T(8,128)(2,1)S(1)}, bf16[128,256]{1,0:T(8,128)(2,1)S(1)}, u32[]{:S(2)}, u32[]{:S(2)}) collective-permute-start(bf16[128,256]{1,0:T(8,128)(2,1)S(1)} %fusion.5), channel_id=1, source_target_pairs={{0,241},{1,17},{8,249},{9,25},{16,0},{17,32},{24,8},{25,40},{32,48... | collective-permute-start | bytes 196616 | tf_op jit(solution)/shard_map/ppermute | solution.py:182
  134.5 2.0 %collective-permute-start.3 = (bf16[512,128]{1,0:T(8,128)(2,1)S(1)}, bf16[512,128]{1,0:T(8,128)(2,1)S(1)}, u32[]{:S(2)}, u32[]{:S(2)}) collective-permute-start(bf16[512,128]{1,0:T(8,128)(2,1)S(1)} %fusion.2), channel_id=1, source_target_pairs={{0,8},{1,9},{8,0},{9,1},{16,24},{17,25},{24,16},{25,17},{32,40},{3... | collective-permute-start | bytes 393224 | tf_op jit(solution)/shard_map/ppermute | solution.py:182
  136.5 0.5 collective-permute-done.7
  137.0 2.0 %collective-permute-start.8 = (bf16[128,256]{1,0:T(8,128)(2,1)S(1)}, bf16[128,256]{1,0:T(8,128)(2,1)S(1)}, u32[]{:S(2)}, u32[]{:S(2)}) collective-permute-start(bf16[128,256]{1,0:T(8,128)(2,1)S(1)} %fusion.4), channel_id=1, source_target_pairs={{0,1},{1,16},{8,9},{9,24},{16,17},{17,33},{24,25},{25,41},{32,49},... | collective-permute-start | bytes 196616 | tf_op jit(solution)/shard_map/ppermute | solution.py:182
  139.0 4.1 %collective-permute-start.9 = (bf16[128,256]{1,0:T(8,128)(2,1)S(1)}, bf16[128,256]{1,0:T(8,128)(2,1)S(1)}, u32[]{:S(2)}, u32[]{:S(2)}) collective-permute-start(bf16[128,256]{1,0:T(8,128)(2,1)S(1)} %fusion.4), channel_id=1, source_target_pairs={{1,17},{9,25},{17,32},{25,40},{32,48},{40,56},{48,65},{56,73},{65,... | collective-permute-start | bytes 196616 | tf_op jit(solution)/shard_map/ppermute | solution.py:182
  143.1 0.0 collective-permute-done.3
  143.1 0.8 copy.14
  143.9 0.0 collective-permute-done.8
  143.9 3.4 %collective-permute-done.9 = bf16[128,256]{1,0:T(8,128)(2,1)S(1)} collective-permute-done((bf16[128,256]{1,0:T(8,128)(2,1)S(1)}, bf16[128,256]{1,0:T(8,128)(2,1)S(1)}, u32[]{:S(2)}, u32[]{:S(2)}) %collective-permute-start.9) | collective-permute-done | bytes 65568 | tf_op jit(solution)/shard_map/ppermute | solution.py:182
  147.3 0.6 slice_bitcast_fusion.2
  (10 shorter events, 0.2 us)
Async XLA Ops:
  3.6 80.6 %collective-permute-start = (bf16[1072,128]{1,0:T(8,128)(2,1)}, bf16[1072,128]{1,0:T(8,128)(2,1)S(1)}, u32[]{:S(2)}, u32[]{:S(2)}) collective-permute-start(bf16[1072,128]{1,0:T(8,128)(2,1)} %shard_map.94), channel_id=1, source_target_pairs={{0,8},{1,9},{8,0},{9,1},{16,24},{17,25},{24,16},{25,17},{32,40},{3... | collective-permute-start | bytes 823304 | tf_op jit(solution)/shard_map/ppermute | solution.py:182
  84.2 5.7 %copy-start.1 = (s32[1,64]{1,0:T(1,128)S(1)}, s32[1,64]{1,0:T(1,128)}, u32[]{:S(2)}) copy-start(s32[1,64]{1,0:T(1,128)} %param.13) | copy-start | bytes 772
  85.2 4.6 %collective-permute-start.1 = (bf16[4192,128]{1,0:T(8,128)(2,1)S(1)}, bf16[4192,128]{1,0:T(8,128)(2,1)S(1)}, u32[]{:S(2)}, u32[]{:S(2)}) collective-permute-start(bf16[4192,128]{1,0:T(8,128)(2,1)S(1)} %pad_maximum_fusion.mine), channel_id=1, source_target_pairs={{0,1},{1,0},{8,9},{9,8},{16,17},{17,16},{24,25},{25,24},{32,33},{3... | collective-permute-start | bytes 3219464 | tf_op jit(solution)/shard_map/ppermute | solution.py:182
  92.2 11.9 %collective-permute-start.4 = (bf16[2,128,256]{2,1,0:T(8,128)(2,1)S(1)}, bf16[2,128,256]{2,1,0:T(8,128)(2,1)S(1)}, u32[]{:S(2)}, u32[]{:S(2)}) collective-permute-start(bf16[2,128,256]{2,1,0:T(8,128)(2,1)S(1)} %convert_element_type.54), channel_id=1, source_target_pairs={{0,225},{1,32},{8,233},{9,40},{16,241},{17,48},{24,249},{25,56},{3... | collective-permute-start | bytes 393224 | tf_op jit(solution)/shard_map/ppermute | solution.py:182
  100.2 10.9 %copy-start = (f32[4,128,256]{2,1,0:T(8,128)}, f32[4,128,256]{2,1,0:T(8,128)S(1)}, u32[]{:S(2)}) copy-start(f32[4,128,256]{2,1,0:T(8,128)S(1)} %get-tuple-element.13) | copy-start | bytes 1572868
  104.8 11.6 %collective-permute-start.5 = (bf16[2,128,256]{2,1,0:T(8,128)(2,1)}, bf16[2,128,256]{2,1,0:T(8,128)(2,1)}, u32[]{:S(2)}, u32[]{:S(2)}) collective-permute-start(bf16[2,128,256]{2,1,0:T(8,128)(2,1)} %add_convert_fusion.1), channel_id=1, source_target_pairs={{0,225},{1,32},{8,233},{9,40},{16,241},{17,48},{24,249},{25,56},{3... | collective-permute-start | bytes 393224 | tf_op jit(solution)/shard_map/ppermute | solution.py:182
  111.2 10.6 %collective-permute-start.2 = (bf16[2,512,128]{2,1,0:T(8,128)(2,1)S(1)}, bf16[2,512,128]{2,1,0:T(8,128)(2,1)S(1)}, u32[]{:S(2)}, u32[]{:S(2)}) collective-permute-start(bf16[2,512,128]{2,1,0:T(8,128)(2,1)S(1)} %slice.71), channel_id=1, source_target_pairs={{0,1},{1,0},{8,9},{9,8},{16,17},{17,16},{24,25},{25,24},{32,33},{3... | collective-permute-start | bytes 786440 | tf_op jit(solution)/shard_map/ppermute | solution.py:182
  117.4 10.3 %collective-permute-start.6 = (bf16[2,128,256]{2,1,0:T(8,128)(2,1)S(1)}, bf16[2,128,256]{2,1,0:T(8,128)(2,1)S(1)}, u32[]{:S(2)}, u32[]{:S(2)}) collective-permute-start(bf16[2,128,256]{2,1,0:T(8,128)(2,1)S(1)} %add_convert_fusion), channel_id=1, source_target_pairs={{0,225},{1,32},{8,233},{9,40},{16,241},{17,48},{24,249},{25,56},{3... | collective-permute-start | bytes 393224 | tf_op jit(solution)/shard_map/ppermute | solution.py:182
  127.8 9.2 %collective-permute-start.7 = (bf16[128,256]{1,0:T(8,128)(2,1)S(1)}, bf16[128,256]{1,0:T(8,128)(2,1)S(1)}, u32[]{:S(2)}, u32[]{:S(2)}) collective-permute-start(bf16[128,256]{1,0:T(8,128)(2,1)S(1)} %fusion.5), channel_id=1, source_target_pairs={{0,241},{1,17},{8,249},{9,25},{16,0},{17,32},{24,8},{25,40},{32,48... | collective-permute-start | bytes 196616 | tf_op jit(solution)/shard_map/ppermute | solution.py:182
  134.5 8.6 %collective-permute-start.3 = (bf16[512,128]{1,0:T(8,128)(2,1)S(1)}, bf16[512,128]{1,0:T(8,128)(2,1)S(1)}, u32[]{:S(2)}, u32[]{:S(2)}) collective-permute-start(bf16[512,128]{1,0:T(8,128)(2,1)S(1)} %fusion.2), channel_id=1, source_target_pairs={{0,8},{1,9},{8,0},{9,1},{16,24},{17,25},{24,16},{25,17},{32,40},{3... | collective-permute-start | bytes 393224 | tf_op jit(solution)/shard_map/ppermute | solution.py:182
  137.0 6.9 %collective-permute-start.8 = (bf16[128,256]{1,0:T(8,128)(2,1)S(1)}, bf16[128,256]{1,0:T(8,128)(2,1)S(1)}, u32[]{:S(2)}, u32[]{:S(2)}) collective-permute-start(bf16[128,256]{1,0:T(8,128)(2,1)S(1)} %fusion.4), channel_id=1, source_target_pairs={{0,1},{1,16},{8,9},{9,24},{16,17},{17,33},{24,25},{25,41},{32,49},... | collective-permute-start | bytes 196616 | tf_op jit(solution)/shard_map/ppermute | solution.py:182
  139.0 8.3 %collective-permute-start.9 = (bf16[128,256]{1,0:T(8,128)(2,1)S(1)}, bf16[128,256]{1,0:T(8,128)(2,1)S(1)}, u32[]{:S(2)}, u32[]{:S(2)}) collective-permute-start(bf16[128,256]{1,0:T(8,128)(2,1)S(1)} %fusion.4), channel_id=1, source_target_pairs={{1,17},{9,25},{17,32},{25,40},{32,48},{40,56},{48,65},{56,73},{65,... | collective-permute-start | bytes 196616 | tf_op jit(solution)/shard_map/ppermute | solution.py:182

commit v9 on v8

--- a/solution.py
+++ b/solution.py
@@ -16,8 +16,12 @@
 STAT_ROWS = 16
 
 
-def rows_kernel(*refs):
-    sources, payload, held, sems = refs[:4], refs[4], refs[5:9], refs[9]
+def rows_kernel(where, *refs):
+    sources, (payload, kv), held, sems = refs[:6], refs[6:8], refs[8:12], refs[12]
+    half = kv.shape[0] // 2
+    start = pl.multiple_of(where[1] * half, half)
+    sources = [*sources[:4], *[source.at[pl.ds(start, half)] for source in sources[4:]]]
+    held = [*held, kv.at[pl.ds(0, half)], kv.at[pl.ds(half, half)]]
     copies = [
         pltpu.make_async_copy(source, target, sems.at[i])
         for i, (source, target) in enumerate(zip(sources, held))
@@ -26,7 +30,7 @@
         copy.start()
     for copy in copies:
         copy.wait()
-    queries, d_out, out, log_total = held
+    queries, d_out, out, log_total = held[:4]
     toks, heads, width = queries.shape
     rows = heads * toks
     deltas = []
@@ -44,14 +48,18 @@
         rest = rest - term.astype(jnp.float32)
 
 
-def own_rows(*arrays):
+def own_rows(where, *arrays):
     toks, heads, width = arrays[0].shape
     return pl.pallas_call(
         rows_kernel,
-        out_shape=jax.ShapeDtypeStruct((2 * heads * toks + 3 * STAT_ROWS, width), jnp.bfloat16),
-        in_specs=[pl.BlockSpec(memory_space=pltpu.HBM)] * len(arrays),
-        out_specs=pl.BlockSpec(memory_space=pltpu.VMEM),
-        scratch_shapes=[pltpu.VMEM(a.shape, a.dtype) for a in arrays]
+        out_shape=(
+            jax.ShapeDtypeStruct((2 * heads * toks + 3 * STAT_ROWS, width), jnp.bfloat16),
+            jax.ShapeDtypeStruct((toks, width), jnp.bfloat16),
+        ),
+        in_specs=[pl.BlockSpec(memory_space=pltpu.SMEM)]
+        + [pl.BlockSpec(memory_space=pltpu.HBM)] * len(arrays),
+        out_specs=(pl.BlockSpec(memory_space=pltpu.VMEM),) * 2,
+        scratch_shapes=[pltpu.VMEM(a.shape, a.dtype) for a in arrays[:4]]
         + [pltpu.SemaphoreType.DMA((len(arrays),))],
         compiler_params=pltpu.CompilerParams(vmem_limit_bytes=63 * 1024 * 1024),
         cost_estimate=pl.CostEstimate(
@@ -59,7 +67,7 @@
             bytes_accessed=10 * heads * toks * width,
             transcendentals=0,
         ),
-    )(*arrays)
+    )(where, *arrays)
 
 
 def kernel(first, count, heads, toks, order, where, mine, theirs, *refs):
@@ -170,7 +178,6 @@
     place = lax.axis_index("inner")
     core = lax.axis_index("head")
     toks, heads, width = queries.shape[1:]
-    half = toks // 2
 
     def move(array, target):
         pairs = []
@@ -187,12 +194,12 @@
     def near(distance):
         return lambda z, c: (z ^ distance, c)
 
-    payload = own_rows(queries[0], d_out[0], out[0], log_total[0])
+    where = jnp.stack([place, core]).astype(jnp.int32)
+    payload, kv = own_rows(
+        where, queries[0], d_out[0], out[0], log_total[0], keys[0], values[0]
+    )
     payloads = [payload] + [move(payload, near(i)) for i in range(1, NEAR)]
 
-    kv = jnp.concatenate(
-        [lax.dynamic_slice_in_dim(a[0], core * half, half, 0) for a in (keys, values)]
-    )
     groups = [
         [2 * z + (z // NEAR + first) % 2 for z in range(chip, size, NEAR)]
         for chip in range(NEAR)
@@ -203,7 +210,6 @@
     theirs = move(mine, swap)
 
     order = span_order[0]
-    where = jnp.stack([place, core]).astype(jnp.int32)
     dq, parts, first = None, [], 0
     for count in CALLS:
         dq, part = attention_grads(first, count, heads, toks, order, where, mine, theirs, dq)

time: 149 us -> 148 us (level)
  other arithmetic: 2.99 us -> 0.88 us
    convert_element_type x2, other arithmetic: 1.7 us -> 0.06 us  [body(): total = sums.astype(jnp.bfloat16)]
  transfers between devices with their start and end apart: 10 -> 10, of which waited for: 5 -> 5; matrix products, arithmetic and copies ran while one was open for 2% -> 1% of each run, Pallas kernels for 4% -> 4%
where the time goes in v9:
time: 148 us; the launch traced here: 147 us
  blocking collectives  73.8 us (50%)
  starting transfers between devices  39.5 us (27%)
  waiting for transfers between devices  17 us (11%)
  Pallas kernels  12.5 us (8%)
  local copies, waits for them, and re-layouts  2.55 us (2%)
    all_gather x1, blocking collectives, body(): lax.all_gather(kv, ('inner', 'head'), axis_index_groups=groups, tiled=True)  73.8 us
    ppermute x10, starting transfers between devices, move(): return lax.ppermute(array, ('inner', 'head'), pairs)  39.5 us
    ppermute x10, waiting for transfers between devices, move(): return lax.ppermute(array, ('inner', 'head'), pairs)  17 us
    pallas_call x3, Pallas kernels, attention_grads(): pl.pallas_call(functools.partial(kernel, first, count, heads, toks), out_...  8.87 us
    pallas_call x1, Pallas kernels, own_rows(): pl.pallas_call(rows_kernel, out_shape=(jax.ShapeDtypeStruct((2 * heads *...  3.65 us
  transfers between devices with their start and end apart: 10, of which 5 were waited for; matrix products, arithmetic and copies ran while one was open for 1% of the time, Pallas kernels for 4%

profile of v9, /device:TPU:33, one launch (start us, length us, event | category | flops | bytes accessed | tf_op | source)
XLA Modules:
  0.0 147.2 jit_solution(10191906012301232987)
XLA Ops:
  0.6 0.7 pad_add_fusion.where
  1.3 3.7 %shard_map.94 = (bf16[1072,128]{1,0:T(8,128)(2,1)}, bf16[128,128]{1,0:T(8,128)(2,1)}) custom-call(s32[2]{0:T(128)} %pad_add_fusion.where, bf16[128,4,128]{2,1,0:T(4,128)(2,1)} %bitcast.40, bf16[128,4,128]{2,1,0:T(4,128)(2,1)} %bitcast.41, bf16[128,4,128]{2,1,0:T(4,128)(2,1)} %bitcast.42, f32[4,128]{1,0:T(4,128)} %bitcast.45, bf16[128,128]{1,0:T(8,128)(2,1)} %bitcast.43, ...), custom_call_target="tpu_custom_call" | custom-call | flops 262144 | bytes 655360 | tf_op jit(solution)/shard_map/pallas_call | solution.py:53
  4.9 5.3 %collective-permute-start = (bf16[1072,128]{1,0:T(8,128)(2,1)}, bf16[1072,128]{1,0:T(8,128)(2,1)S(1)}, u32[]{:S(2)}, u32[]{:S(2)}) collective-permute-start(bf16[1072,128]{1,0:T(8,128)(2,1)} %get-tuple-element.11), channel_id=1, source_target_pairs={{0,8},{1,9},{8,0},{9,1},{16,24},{17,25},{24,16},{25,17},{32,40},{3... | collective-permute-start | bytes 823304 | tf_op jit(solution)/shard_map/ppermute | solution.py:189
  10.2 1.0 constant_dynamic-update-slice_fusion.2
  11.2 0.0 copy-start
  11.2 0.0 copy-start.1
  11.2 73.8 %all_gather.3 = bf16[2048,128]{1,0:T(8,128)(2,1)S(1)} all-gather(bf16[128,128]{1,0:T(8,128)(2,1)} %get-tuple-element.12), channel_id=1, replica_groups={{0,17,32,49,64,81,96,113,128,145,160,177,192,209,224,241},{1,16,33,48,6..., dimensions={0}, use_global_device_ids=true | all-gather | bytes 557056 | tf_op jit(solution)/shard_map/all_gather | solution.py:208
  85.1 0.0 collective-permute-done
  85.1 0.1 constant_dynamic-update-slice_fusion.mine
  85.2 2.3 %collective-permute-start.1 = (bf16[4192,128]{1,0:T(8,128)(2,1)S(1)}, bf16[4192,128]{1,0:T(8,128)(2,1)S(1)}, u32[]{:S(2)}, u32[]{:S(2)}) collective-permute-start(bf16[4192,128]{1,0:T(8,128)(2,1)S(1)} %constant_dynamic-update-slice_fusion.mine), channel_id=1, source_target_pairs={{0,1},{1,0},{8,9},{9,8},{16,17},{17,16},{24,25},{25,24},{32,33},{3... | collective-permute-start | bytes 3219464 | tf_op jit(solution)/shard_map/ppermute | solution.py:189
  87.5 2.3 %collective-permute-done.1.theirs = bf16[4192,128]{1,0:T(8,128)(2,1)S(1)} collective-permute-done((bf16[4192,128]{1,0:T(8,128)(2,1)S(1)}, bf16[4192,128]{1,0:T(8,128)(2,1)S(1)}, u32[]{:S(2)}, u32[]{:S(2)}) %collective-permute-start.1) | collective-permute-done | bytes 1073184 | tf_op jit(solution)/shard_map/ppermute | solution.py:189
  89.8 0.0 copy-done
  89.8 0.0 copy-done.1
  89.8 2.4 %shard_map.95 = (f32[4,512,128]{2,1,0:T(8,128)S(1)}, f32[2,128,256]{2,1,0:T(8,128)S(1)}) custom-call(s32[64]{0:T(128)S(1)} %bitcast.35, s32[2]{0:T(128)S(1)} %copy-done, bf16[4192,128]{1,0:T(8,128)(2,1)S(1)} %constant_dynamic-update-slice_fusion.mine, bf16[4192,128]{1,0:T(8,128)(2,1)S(1)} %collective-permute-done.1.theirs), custom_call_target="tpu_custom_call" | custom-call | flops 671088640 | bytes 2097152 | tf_op jit(solution)/shard_map/pallas_call | solution.py:158
  92.2 4.1 %collective-permute-start.4 = (bf16[2,128,256]{2,1,0:T(8,128)(2,1)S(1)}, bf16[2,128,256]{2,1,0:T(8,128)(2,1)S(1)}, u32[]{:S(2)}, u32[]{:S(2)}) collective-permute-start(bf16[2,128,256]{2,1,0:T(8,128)(2,1)S(1)} %convert_element_type.54), channel_id=1, source_target_pairs={{0,225},{1,32},{8,233},{9,40},{16,241},{17,48},{24,249},{25,56},{3... | collective-permute-start | bytes 393224 | tf_op jit(solution)/shard_map/ppermute | solution.py:189
  96.3 4.1 %shard_map.96 = (f32[4,512,128]{2,1,0:T(8,128)S(1)}, f32[4,128,256]{2,1,0:T(8,128)S(1)}) custom-call(s32[64]{0:T(128)S(1)} %bitcast.36, s32[2]{0:T(128)S(1)} %copy-done, bf16[4192,128]{1,0:T(8,128)(2,1)S(1)} %constant_dynamic-update-slice_fusion.mine, bf16[4192,128]{1,0:T(8,128)(2,1)S(1)} %collective-permute-done.1.theirs, ...), custom_call_target="tpu_custom_call", output_to_operand_aliasing={{0}: (4, {})} | custom-call | flops 1342177280 | bytes 2097152 | tf_op jit(solution)/shard_map/pallas_call | solution.py:158
  100.4 3.1 %collective-permute-done.4 = bf16[2,128,256]{2,1,0:T(8,128)(2,1)S(1)} collective-permute-done((bf16[2,128,256]{2,1,0:T(8,128)(2,1)S(1)}, bf16[2,128,256]{2,1,0:T(8,128)(2,1)S(1)}, u32[]{:S(2)}, u32[]{:S(2)}) %collective-permute-start.4) | collective-permute-done | bytes 131104 | tf_op jit(solution)/shard_map/ppermute | solution.py:189
  103.6 4.6 %collective-permute-start.5 = (bf16[2,128,256]{2,1,0:T(8,128)(2,1)S(1)}, bf16[2,128,256]{2,1,0:T(8,128)(2,1)S(1)}, u32[]{:S(2)}, u32[]{:S(2)}) collective-permute-start(bf16[2,128,256]{2,1,0:T(8,128)(2,1)S(1)} %add_convert_fusion.1), channel_id=1, source_target_pairs={{0,225},{1,32},{8,233},{9,40},{16,241},{17,48},{24,249},{25,56},{3... | collective-permute-start | bytes 393224 | tf_op jit(solution)/shard_map/ppermute | solution.py:189
  108.2 2.5 %shard_map.97 = (f32[4,512,128]{2,1,0:T(8,128)S(1)}, f32[2,128,256]{2,1,0:T(8,128)S(1)}) custom-call(s32[64]{0:T(128)S(1)} %bitcast.37, s32[2]{0:T(128)S(1)} %copy-done, bf16[4192,128]{1,0:T(8,128)(2,1)S(1)} %constant_dynamic-update-slice_fusion.mine, bf16[4192,128]{1,0:T(8,128)(2,1)S(1)} %collective-permute-done.1.theirs, ...), custom_call_target="tpu_custom_call", output_to_operand_aliasing={{0}: (4, {})} | custom-call | flops 671088640 | bytes 2097152 | tf_op jit(solution)/shard_map/pallas_call | solution.py:158
  110.7 4.8 %collective-permute-start.2 = (bf16[2,512,128]{2,1,0:T(8,128)(2,1)S(1)}, bf16[2,512,128]{2,1,0:T(8,128)(2,1)S(1)}, u32[]{:S(2)}, u32[]{:S(2)}) collective-permute-start(bf16[2,512,128]{2,1,0:T(8,128)(2,1)S(1)} %slice.71), channel_id=1, source_target_pairs={{0,1},{1,0},{8,9},{9,8},{16,17},{17,16},{24,25},{25,24},{32,33},{3... | collective-permute-start | bytes 786440 | tf_op jit(solution)/shard_map/ppermute | solution.py:189
  115.6 0.0 collective-permute-done.5
  115.6 4.7 %collective-permute-start.6 = (bf16[2,128,256]{2,1,0:T(8,128)(2,1)S(1)}, bf16[2,128,256]{2,1,0:T(8,128)(2,1)S(1)}, u32[]{:S(2)}, u32[]{:S(2)}) collective-permute-start(bf16[2,128,256]{2,1,0:T(8,128)(2,1)S(1)} %add_convert_fusion), channel_id=1, source_target_pairs={{0,225},{1,32},{8,233},{9,40},{16,241},{17,48},{24,249},{25,56},{3... | collective-permute-start | bytes 393224 | tf_op jit(solution)/shard_map/ppermute | solution.py:189
  120.4 0.0 collective-permute-done.2
  120.4 5.8 %collective-permute-done.6 = bf16[2,128,256]{2,1,0:T(8,128)(2,1)S(1)} collective-permute-done((bf16[2,128,256]{2,1,0:T(8,128)(2,1)S(1)}, bf16[2,128,256]{2,1,0:T(8,128)(2,1)S(1)}, u32[]{:S(2)}, u32[]{:S(2)}) %collective-permute-start.6) | collective-permute-done | bytes 131104 | tf_op jit(solution)/shard_map/ppermute | solution.py:189
  126.2 6.2 %collective-permute-start.7 = (bf16[128,256]{1,0:T(8,128)(2,1)S(1)}, bf16[128,256]{1,0:T(8,128)(2,1)S(1)}, u32[]{:S(2)}, u32[]{:S(2)}) collective-permute-start(bf16[128,256]{1,0:T(8,128)(2,1)S(1)} %fusion.5), channel_id=1, source_target_pairs={{0,241},{1,17},{8,249},{9,25},{16,0},{17,32},{24,8},{25,40},{32,48... | collective-permute-start | bytes 196616 | tf_op jit(solution)/shard_map/ppermute | solution.py:189
  132.5 2.0 %collective-permute-start.3 = (bf16[512,128]{1,0:T(8,128)(2,1)S(1)}, bf16[512,128]{1,0:T(8,128)(2,1)S(1)}, u32[]{:S(2)}, u32[]{:S(2)}) collective-permute-start(bf16[512,128]{1,0:T(8,128)(2,1)S(1)} %fusion.2), channel_id=1, source_target_pairs={{0,8},{1,9},{8,0},{9,1},{16,24},{17,25},{24,16},{25,17},{32,40},{3... | collective-permute-start | bytes 393224 | tf_op jit(solution)/shard_map/ppermute | solution.py:189
  134.4 0.7 collective-permute-done.7
  135.1 3.0 %collective-permute-start.8 = (bf16[128,256]{1,0:T(8,128)(2,1)S(1)}, bf16[128,256]{1,0:T(8,128)(2,1)S(1)}, u32[]{:S(2)}, u32[]{:S(2)}) collective-permute-start(bf16[128,256]{1,0:T(8,128)(2,1)S(1)} %fusion.4), channel_id=1, source_target_pairs={{0,1},{1,16},{8,9},{9,24},{16,17},{17,33},{24,25},{25,41},{32,49},... | collective-permute-start | bytes 196616 | tf_op jit(solution)/shard_map/ppermute | solution.py:189
  138.1 2.6 %collective-permute-start.9 = (bf16[128,256]{1,0:T(8,128)(2,1)S(1)}, bf16[128,256]{1,0:T(8,128)(2,1)S(1)}, u32[]{:S(2)}, u32[]{:S(2)}) collective-permute-start(bf16[128,256]{1,0:T(8,128)(2,1)S(1)} %fusion.4), channel_id=1, source_target_pairs={{1,17},{9,25},{17,32},{25,40},{32,48},{40,56},{48,65},{56,73},{65,... | collective-permute-start | bytes 196616 | tf_op jit(solution)/shard_map/ppermute | solution.py:189
  140.7 0.0 collective-permute-done.3
  140.7 0.8 copy.14
  141.5 0.0 collective-permute-done.8
  141.5 5.0 %collective-permute-done.9 = bf16[128,256]{1,0:T(8,128)(2,1)S(1)} collective-permute-done((bf16[128,256]{1,0:T(8,128)(2,1)S(1)}, bf16[128,256]{1,0:T(8,128)(2,1)S(1)}, u32[]{:S(2)}, u32[]{:S(2)}) %collective-permute-start.9) | collective-permute-done | bytes 65568 | tf_op jit(solution)/shard_map/ppermute | solution.py:189
  146.6 0.6 slice_bitcast_fusion.2
  (12 shorter events, 0.3 us)
Async XLA Ops:
  4.9 80.1 %collective-permute-start = (bf16[1072,128]{1,0:T(8,128)(2,1)}, bf16[1072,128]{1,0:T(8,128)(2,1)S(1)}, u32[]{:S(2)}, u32[]{:S(2)}) collective-permute-start(bf16[1072,128]{1,0:T(8,128)(2,1)} %get-tuple-element.11), channel_id=1, source_target_pairs={{0,8},{1,9},{8,0},{9,1},{16,24},{17,25},{24,16},{25,17},{32,40},{3... | collective-permute-start | bytes 823304 | tf_op jit(solution)/shard_map/ppermute | solution.py:189
  11.2 78.6 %copy-start = (s32[2]{0:T(128)S(1)}, s32[2]{0:T(128)}, u32[]{:S(2)}) copy-start(s32[2]{0:T(128)} %pad_add_fusion.where) | copy-start | bytes 28
  11.2 78.6 %copy-start.1 = (s32[1,64]{1,0:T(1,128)S(1)}, s32[1,64]{1,0:T(1,128)}, u32[]{:S(2)}) copy-start(s32[1,64]{1,0:T(1,128)} %param.13) | copy-start | bytes 772
  85.2 4.6 %collective-permute-start.1 = (bf16[4192,128]{1,0:T(8,128)(2,1)S(1)}, bf16[4192,128]{1,0:T(8,128)(2,1)S(1)}, u32[]{:S(2)}, u32[]{:S(2)}) collective-permute-start(bf16[4192,128]{1,0:T(8,128)(2,1)S(1)} %constant_dynamic-update-slice_fusion.mine), channel_id=1, source_target_pairs={{0,1},{1,0},{8,9},{9,8},{16,17},{17,16},{24,25},{25,24},{32,33},{3... | collective-permute-start | bytes 3219464 | tf_op jit(solution)/shard_map/ppermute | solution.py:189
  92.2 11.3 %collective-permute-start.4 = (bf16[2,128,256]{2,1,0:T(8,128)(2,1)S(1)}, bf16[2,128,256]{2,1,0:T(8,128)(2,1)S(1)}, u32[]{:S(2)}, u32[]{:S(2)}) collective-permute-start(bf16[2,128,256]{2,1,0:T(8,128)(2,1)S(1)} %convert_element_type.54), channel_id=1, source_target_pairs={{0,225},{1,32},{8,233},{9,40},{16,241},{17,48},{24,249},{25,56},{3... | collective-permute-start | bytes 393224 | tf_op jit(solution)/shard_map/ppermute | solution.py:189
  103.6 12.0 %collective-permute-start.5 = (bf16[2,128,256]{2,1,0:T(8,128)(2,1)S(1)}, bf16[2,128,256]{2,1,0:T(8,128)(2,1)S(1)}, u32[]{:S(2)}, u32[]{:S(2)}) collective-permute-start(bf16[2,128,256]{2,1,0:T(8,128)(2,1)S(1)} %add_convert_fusion.1), channel_id=1, source_target_pairs={{0,225},{1,32},{8,233},{9,40},{16,241},{17,48},{24,249},{25,56},{3... | collective-permute-start | bytes 393224 | tf_op jit(solution)/shard_map/ppermute | solution.py:189
  110.7 9.7 %collective-permute-start.2 = (bf16[2,512,128]{2,1,0:T(8,128)(2,1)S(1)}, bf16[2,512,128]{2,1,0:T(8,128)(2,1)S(1)}, u32[]{:S(2)}, u32[]{:S(2)}) collective-permute-start(bf16[2,512,128]{2,1,0:T(8,128)(2,1)S(1)} %slice.71), channel_id=1, source_target_pairs={{0,1},{1,0},{8,9},{9,8},{16,17},{17,16},{24,25},{25,24},{32,33},{3... | collective-permute-start | bytes 786440 | tf_op jit(solution)/shard_map/ppermute | solution.py:189
  115.6 10.6 %collective-permute-start.6 = (bf16[2,128,256]{2,1,0:T(8,128)(2,1)S(1)}, bf16[2,128,256]{2,1,0:T(8,128)(2,1)S(1)}, u32[]{:S(2)}, u32[]{:S(2)}) collective-permute-start(bf16[2,128,256]{2,1,0:T(8,128)(2,1)S(1)} %add_convert_fusion), channel_id=1, source_target_pairs={{0,225},{1,32},{8,233},{9,40},{16,241},{17,48},{24,249},{25,56},{3... | collective-permute-start | bytes 393224 | tf_op jit(solution)/shard_map/ppermute | solution.py:189
  126.2 8.9 %collective-permute-start.7 = (bf16[128,256]{1,0:T(8,128)(2,1)S(1)}, bf16[128,256]{1,0:T(8,128)(2,1)S(1)}, u32[]{:S(2)}, u32[]{:S(2)}) collective-permute-start(bf16[128,256]{1,0:T(8,128)(2,1)S(1)} %fusion.5), channel_id=1, source_target_pairs={{0,241},{1,17},{8,249},{9,25},{16,0},{17,32},{24,8},{25,40},{32,48... | collective-permute-start | bytes 196616 | tf_op jit(solution)/shard_map/ppermute | solution.py:189
  132.5 8.2 %collective-permute-start.3 = (bf16[512,128]{1,0:T(8,128)(2,1)S(1)}, bf16[512,128]{1,0:T(8,128)(2,1)S(1)}, u32[]{:S(2)}, u32[]{:S(2)}) collective-permute-start(bf16[512,128]{1,0:T(8,128)(2,1)S(1)} %fusion.2), channel_id=1, source_target_pairs={{0,8},{1,9},{8,0},{9,1},{16,24},{17,25},{24,16},{25,17},{32,40},{3... | collective-permute-start | bytes 393224 | tf_op jit(solution)/shard_map/ppermute | solution.py:189
  135.1 6.3 %collective-permute-start.8 = (bf16[128,256]{1,0:T(8,128)(2,1)S(1)}, bf16[128,256]{1,0:T(8,128)(2,1)S(1)}, u32[]{:S(2)}, u32[]{:S(2)}) collective-permute-start(bf16[128,256]{1,0:T(8,128)(2,1)S(1)} %fusion.4), channel_id=1, source_target_pairs={{0,1},{1,16},{8,9},{9,24},{16,17},{17,33},{24,25},{25,41},{32,49},... | collective-permute-start | bytes 196616 | tf_op jit(solution)/shard_map/ppermute | solution.py:189
  138.1 8.4 %collective-permute-start.9 = (bf16[128,256]{1,0:T(8,128)(2,1)S(1)}, bf16[128,256]{1,0:T(8,128)(2,1)S(1)}, u32[]{:S(2)}, u32[]{:S(2)}) collective-permute-start(bf16[128,256]{1,0:T(8,128)(2,1)S(1)} %fusion.4), channel_id=1, source_target_pairs={{1,17},{9,25},{17,32},{25,40},{32,48},{40,56},{48,65},{56,73},{65,... | collective-permute-start | bytes 196616 | tf_op jit(solution)/shard_map/ppermute | solution.py:189
